TPU v7x, 32 devices: a whole 2x2x4 slice. The times are simulated.
32 devices in a mesh: seq: 16 (over z, y, x), rep: 2 (over core).
Axes of the slice: x: 2, y: 2, z: 4, core: 2. Of those that a mesh axis runs over, the one named last changes fastest.
Arguments:
- tokens: bfloat16 [4, 48, 180, 768], P('rep', 'seq'), may hold values from -6 to 6
- cotangent: bfloat16 [4, 48, 180, 768], P('rep', 'seq'), may hold values from -6 to 6
- in_weight: bfloat16 [2, 8, 96, 96], replicated, may hold values from -0.21875 to 0.21875
- in_bias: float32 [2, 768], replicated, may hold values from -0.6 to 0.6
- out_weight: bfloat16 [2, 8, 96, 96], replicated, may hold values from -0.21875 to 0.21875
- out_bias: float32 [2, 768], replicated, may hold values from -0.12 to 0.12
Outputs:
- mixed_out: bfloat16 [4, 48, 180, 768], P('rep', 'seq')
- tokens_grad: bfloat16 [4, 48, 180, 768], P('rep', 'seq')
- in_weight_grad: float32 [2, 8, 96, 96], replicated
- in_bias_grad: float32 [2, 768], replicated
- out_weight_grad: float32 [2, 8, 96, 96], replicated
- out_bias_grad: float32 [2, 768], replicated
All inputs are finite; a program needn't handle non-finite values.
Results may differ from a plain program's by a relative error of at most 0.0094.
Values may be sent and summed in bfloat16 or wider, within the bound.
No kernel may reach another device: no remote copies, remote signals or barrier semaphores. Data moves between devices by JAX's collectives and lax.ppermute only.
A program may use at most 64 MiB of HBM per device.

v0:
```python
import math

import jax
import jax.numpy as jnp
from jax import lax
from jax.sharding import PartitionSpec as P

BLOCKS = 8
BLOCK = 96
MODES = 64


def grid_tables(length, modes):
    position = jnp.arange(length, dtype=jnp.int32)
    frequency = jnp.arange(modes, dtype=jnp.int32)
    residue = position[:, None] * frequency[None, :] % length
    angles = residue.astype(jnp.float32) * (2.0 * math.pi / length)
    factor = 1.0 / math.sqrt(length)
    cosine_table = (jnp.cos(angles) * factor).astype(jnp.bfloat16)
    sine_table = (jnp.sin(angles) * factor).astype(jnp.bfloat16)
    return (cosine_table, sine_table)


def column_tables(grid_width, modes):
    cosine_table, sine_table = grid_tables(grid_width, modes)
    forward = jnp.stack([cosine_table, -sine_table], axis=2)
    doubling = jnp.where(jnp.arange(modes) == 0, 1.0, 2.0).astype(jnp.bfloat16)[:, None]
    inverse = jnp.stack([cosine_table.T * doubling, -(sine_table.T * doubling)], axis=1)
    return (forward, inverse)


def row_table(length):
    cosine_table, sine_table = grid_tables(length, length)
    upper_rows = jnp.stack([cosine_table, sine_table], axis=2)
    lower_rows = jnp.stack([-sine_table, cosine_table], axis=2)
    return jnp.stack([upper_rows, lower_rows], axis=1)


def block_weights(weight):
    real_part, imag_part = (weight[0], weight[1])
    upper_half = jnp.stack([real_part, imag_part], axis=2)
    lower_half = jnp.stack([-imag_part, real_part], axis=2)
    return jnp.stack([upper_half, lower_half], axis=1)


def fold_blocks(blockwise):
    real_part = blockwise[:, 0, :, 0, :] + blockwise[:, 1, :, 1, :]
    imag_part = blockwise[:, 0, :, 1, :] - blockwise[:, 1, :, 0, :]
    return jnp.stack([real_part, imag_part])


def mix_forward(spectrum, weights_in, weights_out, bias_in, bias_out):
    mode_count = spectrum.shape[0] * spectrum.shape[1] * spectrum.shape[2]
    flat_modes = spectrum.reshape(mode_count, 2, BLOCKS, BLOCK)
    hidden_pre = (
        jnp.einsum("mcbi,bciej->mebj", flat_modes, weights_in, preferred_element_type=jnp.float32)
        + bias_in
    )
    hidden = jax.nn.gelu(hidden_pre).astype(jnp.bfloat16)
    spectrum_out = (
        jnp.einsum("mcbi,bciej->mebj", hidden, weights_out, preferred_element_type=jnp.float32)
        + bias_out
    )
    return (
        flat_modes,
        hidden_pre,
        hidden,
        spectrum_out.astype(jnp.bfloat16).reshape(spectrum.shape),
    )


def mix_backward(flat_modes, hidden_pre, hidden, incoming, weights_in, weights_out):
    incoming_flat = incoming.reshape(flat_modes.shape)
    out_bias_part = jnp.sum(incoming_flat.astype(jnp.float32), axis=0).reshape(2, -1)
    out_weight_part = fold_blocks(
        jnp.einsum("mcbi,mebj->bciej", hidden, incoming_flat, preferred_element_type=jnp.float32)
    )
    hidden_grad = jnp.einsum(
        "mebj,bciej->mcbi", incoming_flat, weights_out, preferred_element_type=jnp.float32
    )
    pre_grad = jax.vjp(jax.nn.gelu, hidden_pre)[1](hidden_grad)[0].astype(jnp.bfloat16)
    in_bias_part = jnp.sum(pre_grad.astype(jnp.float32), axis=0).reshape(2, -1)
    in_weight_part = fold_blocks(
        jnp.einsum("mcbi,mebj->bciej", flat_modes, pre_grad, preferred_element_type=jnp.float32)
    )
    spectrum_grad = jnp.einsum(
        "mebj,bciej->mcbi", pre_grad, weights_in, preferred_element_type=jnp.float32
    )
    spectrum_grad = spectrum_grad.astype(jnp.bfloat16).reshape(incoming.shape)
    return (spectrum_grad, (in_weight_part, in_bias_part, out_weight_part, out_bias_part))


def shards(tokens, cotangent, in_weight, in_bias, out_weight, out_bias):
    samples, row_count, grid_width, channels = tokens.shape
    length = row_count * lax.axis_size("seq")
    column_forward, column_inverse = column_tables(grid_width, MODES)
    row_matrix = row_table(length)
    weights_in = block_weights(in_weight)
    weights_out = block_weights(out_weight)
    bias_in = in_bias.reshape(2, BLOCKS, BLOCK)
    bias_out = out_bias.reshape(2, BLOCKS, BLOCK)

    def along_rows(section):
        return jnp.einsum(
            "qehc,shkcd->sqked", row_matrix, section, preferred_element_type=jnp.float32
        ).astype(jnp.bfloat16)

    def back_rows(section):
        return jnp.einsum(
            "qehc,sqked->shkcd", row_matrix, section, preferred_element_type=jnp.float32
        ).astype(jnp.bfloat16)

    spec_rows = jnp.einsum(
        "shwd,wkc->shkcd", tokens, column_forward, preferred_element_type=jnp.float32
    ).astype(jnp.bfloat16)
    spectrum = along_rows(lax.all_to_all(spec_rows, "seq", split_axis=2, concat_axis=1, tiled=True))
    flat_modes, hidden_pre, hidden, spectrum_out = mix_forward(
        spectrum, weights_in, weights_out, bias_in, bias_out
    )
    mixed_grid = jnp.einsum(
        "shkcd,kcw->shwd",
        lax.all_to_all(back_rows(spectrum_out), "seq", split_axis=1, concat_axis=2, tiled=True),
        column_inverse,
        preferred_element_type=jnp.float32,
    )
    cot_rows = jnp.einsum(
        "shwd,kcw->shkcd", cotangent, column_inverse, preferred_element_type=jnp.float32
    ).astype(jnp.bfloat16)
    incoming = along_rows(lax.all_to_all(cot_rows, "seq", split_axis=2, concat_axis=1, tiled=True))
    spectrum_grad, partials = mix_backward(
        flat_modes, hidden_pre, hidden, incoming, weights_in, weights_out
    )
    adjoint_part = jnp.einsum(
        "shkcd,wkc->shwd",
        lax.all_to_all(back_rows(spectrum_grad), "seq", split_axis=1, concat_axis=2, tiled=True),
        column_forward,
        preferred_element_type=jnp.float32,
    )
    mixed_out = (tokens.astype(jnp.float32) + mixed_grid).astype(jnp.bfloat16)
    tokens_grad = (cotangent.astype(jnp.float32) + adjoint_part).astype(jnp.bfloat16)
    totals = lax.psum((partials[0], partials[1], partials[2], partials[3]), ("seq", "rep"))
    divisor = float(samples * lax.axis_size("rep"))
    return (
        mixed_out,
        tokens_grad,
        totals[0] / divisor,
        totals[1] / divisor,
        totals[2] / divisor,
        totals[3] / divisor,
    )


def solution(mesh):
    in_specs = (P("rep", "seq", None, None), P("rep", "seq", None, None), P(), P(), P(), P())
    out_specs = (P("rep", "seq", None, None), P("rep", "seq", None, None), P(), P(), P(), P())
    return jax.shard_map(shards, mesh=mesh, in_specs=in_specs, out_specs=out_specs, check_vma=False)
```

profile of v0, /device:TPU:0, one launch (start us, length us, event | category | flops | bytes accessed | tf_op | source)
XLA Modules:
  0.0 317.8 jit_solution(5726129648743128858)
XLA Ops:
  9.7 2.2 copy.183
  11.9 8.5 %all-to-all-start = ((bf16[2,3,64,2,768]{4,3,1,0,2:T(2,128)(2,1)}), bf16[2,3,64,2,768]{4,3,1,0,2:T(2,128)(2,1)S(1)}, u32[]{:S(2)}, u32[]{:S(2)}) async-start(bf16[2,3,64,2,768]{4,3,1,0,2:T(2,128)(2,1)} %copy.183), calls=%async_computation | async-start | bytes 2359296 | tf_op jit(solution)/shard_map/all_to_all | solution.py:116
  21.3 2.2 copy.198
  23.5 23.8 %all-to-all-done = bf16[2,3,64,2,768]{4,3,1,0,2:T(2,128)(2,1)S(1)} async-done(((bf16[2,3,64,2,768]{4,3,1,0,2:T(2,128)(2,1)}), bf16[2,3,64,2,768]{4,3,1,0,2:T(2,128)(2,1)S(1)}, u32[]{:S(2)}, u32[]{:S(2)}) %all-to-all-start) | async-done | bytes 1179680 | tf_op jit(solution)/shard_map/all_to_all | solution.py:116
  47.3 6.3 %all-to-all-start.2 = ((bf16[2,3,64,2,768]{4,3,1,0,2:T(2,128)(2,1)}), bf16[2,3,64,2,768]{4,3,1,0,2:T(2,128)(2,1)}, u32[]{:S(2)}, u32[]{:S(2)}) async-start(bf16[2,3,64,2,768]{4,3,1,0,2:T(2,128)(2,1)} %copy.198), calls=%async_computation.2 | async-start | bytes 2359296 | tf_op jit(solution)/shard_map/all_to_all | solution.py:129
  59.6 2.1 maximum_bitcast_fusion.2
  66.1 3.7 %reshape.381 = bf16[384,2,8,96]{3,2,1,0:T(8,128)(2,1)S(1)} reshape(bf16[2,48,4,2,768]{4,3,2,1,0:T(2,128)(2,1)} %copy.186) | data formatting | bytes 2359296 | tf_op jit(solution)/shard_map/reshape | solution.py:54
  69.7 9.7 %all-to-all-done.2 = bf16[2,3,64,2,768]{4,3,1,0,2:T(2,128)(2,1)} async-done(((bf16[2,3,64,2,768]{4,3,1,0,2:T(2,128)(2,1)}), bf16[2,3,64,2,768]{4,3,1,0,2:T(2,128)(2,1)}, u32[]{:S(2)}, u32[]{:S(2)}) %all-to-all-start.2) | async-done | bytes 1179680 | tf_op jit(solution)/shard_map/all_to_all | solution.py:129
  79.4 2.1 copy.199
  84.0 4.6 %reshape.383 = bf16[384,2,8,96]{3,2,1,0:T(8,128)(2,1)} reshape(bf16[2,48,4,2,768]{4,3,2,1,0:T(2,128)(2,1)} %copy.201) | data formatting | bytes 2359296 | tf_op jit(solution)/shard_map/reshape | solution.py:73
  88.6 2.0 fusion.23
  90.6 3.0 convert_reduce_fusion.1
  96.4 2.9 copy.205
  99.2 4.7 %reshape.384 = bf16[2,48,4,2,768]{4,3,2,1,0:T(2,128)(2,1)} reshape(bf16[384,2,8,96]{3,2,1,0:T(8,128)(2,1)} %copy.205) | data formatting | bytes 2359296 | tf_op jit(solution)/shard_map/reshape | solution.py:89
  105.7 2.0 copy.208
  107.7 6.6 %all-to-all-start.3 = ((bf16[2,48,4,2,768]{4,3,2,0,1:T(2,128)(2,1)}), bf16[2,48,4,2,768]{4,3,2,0,1:T(2,128)(2,1)}, u32[]{:S(2)}, u32[]{:S(2)}) async-start(bf16[2,48,4,2,768]{4,3,2,0,1:T(2,128)(2,1)} %copy.208), calls=%async_computation.3 | async-start | bytes 2359296 | tf_op jit(solution)/shard_map/all_to_all | solution.py:135
  114.3 4.5 %fusion.12 = bf16[384,2,8,96]{0,3,1,2:T(8,128)(2,1)} fusion(f32[2,8,96]{2,0,1:T(2,128)S(1)} %copy.189, bf16[8,1,96,2,96]{2,4,1,3,0:T(8,128)(2,1)} %get-tuple-element.49, bf16[8,1,96,2,96]{2,4,1,3,0:T(8,128)(2,1)} %get-tuple-element.48, f32[8,2,96,384,1]{3,2,4,1,0:T(8,128)} %copy-done.6, f32[2,8,96]{2,0,1:T(2,128)S(1)} %copy.188), kind=kOutput, calls=%fused_computation.20 | convolution fusion | flops 233865216 | bytes 4141056 | tf_op jit(solution)/shard_map/mcbi,bciej->mebj/dot_general | solution.py:61
  118.8 2.9 copy.190
  121.7 4.6 %reshape.382 = bf16[2,48,4,2,768]{4,3,2,1,0:T(2,128)(2,1)} reshape(bf16[384,2,8,96]{3,2,1,0:T(8,128)(2,1)} %copy.190) | data formatting | bytes 2359296 | tf_op jit(solution)/shard_map/reshape | solution.py:68
  128.1 2.0 copy.193
  132.0 9.0 %all-to-all-done.3 = bf16[2,48,4,2,768]{4,3,2,0,1:T(2,128)(2,1)} async-done(((bf16[2,48,4,2,768]{4,3,2,0,1:T(2,128)(2,1)}), bf16[2,48,4,2,768]{4,3,2,0,1:T(2,128)(2,1)}, u32[]{:S(2)}, u32[]{:S(2)}) %all-to-all-start.3) | async-done | bytes 1179680 | tf_op jit(solution)/shard_map/all_to_all | solution.py:135
  141.0 6.2 %all-to-all-start.1 = ((bf16[2,48,4,2,768]{4,3,2,0,1:T(2,128)(2,1)}), bf16[2,48,4,2,768]{4,3,2,0,1:T(2,128)(2,1)}, u32[]{:S(2)}, u32[]{:S(2)}) async-start(bf16[2,48,4,2,768]{4,3,2,0,1:T(2,128)(2,1)} %copy.193), calls=%async_computation.1 | async-start | bytes 2359296 | tf_op jit(solution)/shard_map/all_to_all | solution.py:122
  147.2 2.8 fusion.18
  151.2 49.3 %all-reduce = (f32[2,768]{1,0:T(2,128)S(1)}, f32[2,768]{1,0:T(2,128)S(1)}) all-reduce(f32[2,768]{1,0:T(2,128)S(1)} %reshape.385, f32[2,768]{1,0:T(2,128)S(1)} %get-tuple-element.56), channel_id=1, replica_groups=mesh['seq'=16,'rep'=2] {'seq','rep'}, use_global_device_ids=true, to_apply=%region_2.3 | all-reduce | flops 3072 | bytes 24576 | tf_op jit(solution)/shard_map/psum | solution.py:141
  201.7 89.5 %all-reduce.4.cloned.1.call-done = (f32[2,8,96,96]{3,2,1,0:T(8,128)}, f32[2,8,96,96]{3,2,1,0:T(8,128)}) async-done(((f32[2,8,96,96]{3,2,1,0:T(8,128)}, f32[2,8,96,96]{3,2,1,0:T(8,128)}), (f32[2,8,96,96]{3,2,1,0:T(8,128)}, f32[2,8,96,96]{3,2,1,0:T(8,128)})) %all-reduce.4.cloned.1.call-update) | async-done | bytes 1179664 | tf_op jit(solution)/shard_map/psum | solution.py:141
  291.2 2.2 broadcast_multiply_fusion
  294.3 2.8 copy.210
  297.1 2.4 all_to_all.67
  300.1 2.5 copy.221
  302.6 2.8 copy.195
  305.4 2.5 all_to_all.59
  308.5 2.5 copy.220
  (84 shorter events, 28.9 us)
Async XLA Ops:
  7.4 2.2 copy-start.13
  7.7 2.0 copy-start.15
  11.9 8.8 %copy-start = (bf16[2,3,180,768]{3,0,2,1:T(2,128)(2,1)S(1)}, bf16[2,3,180,768]{3,0,2,1:T(2,128)(2,1)}, u32[]{:S(2)}) copy-start(bf16[2,3,180,768]{3,0,2,1:T(2,128)(2,1)} %param.7) | copy-start | bytes 4976644
  11.9 35.4 %all-to-all-start = ((bf16[2,3,64,2,768]{4,3,1,0,2:T(2,128)(2,1)}), bf16[2,3,64,2,768]{4,3,1,0,2:T(2,128)(2,1)S(1)}, u32[]{:S(2)}, u32[]{:S(2)}) async-start(bf16[2,3,64,2,768]{4,3,1,0,2:T(2,128)(2,1)} %copy.183), calls=%async_computation | async-start | bytes 2359296 | tf_op jit(solution)/shard_map/all_to_all | solution.py:116
  47.3 32.1 %all-to-all-start.2 = ((bf16[2,3,64,2,768]{4,3,1,0,2:T(2,128)(2,1)}), bf16[2,3,64,2,768]{4,3,1,0,2:T(2,128)(2,1)}, u32[]{:S(2)}, u32[]{:S(2)}) async-start(bf16[2,3,64,2,768]{4,3,1,0,2:T(2,128)(2,1)} %copy.198), calls=%async_computation.2 | async-start | bytes 2359296 | tf_op jit(solution)/shard_map/all_to_all | solution.py:129
  53.6 5.6 %copy-start.17 = (f32[2,768]{1,0:T(2,128)S(1)}, f32[2,768]{1,0:T(2,128)}, u32[]{:S(2)}) copy-start(f32[2,768]{1,0:T(2,128)} %param.9) | copy-start | bytes 18436
  59.2 2.5 copy-start.10
  88.6 2.0 copy-start.7
  88.6 2.0 copy-start.11
  88.6 2.0 copy-start.12
  90.6 3.1 copy-start.6
  90.6 4.1 %copy-start.4 = (bf16[8,1,96,2,96]{2,4,1,3,0:T(8,128)(2,1)S(1)}, bf16[8,1,96,2,96]{2,4,1,3,0:T(8,128)(2,1)}, u32[]{:S(2)}) copy-start(bf16[8,1,96,2,96]{2,4,1,3,0:T(8,128)(2,1)} %get-tuple-element.46) | copy-start | bytes 884740
  90.6 4.1 %copy-start.5 = (bf16[8,1,96,2,96]{2,4,1,3,0:T(8,128)(2,1)S(1)}, bf16[8,1,96,2,96]{2,4,1,3,0:T(8,128)(2,1)}, u32[]{:S(2)}) copy-start(bf16[8,1,96,2,96]{2,4,1,3,0:T(8,128)(2,1)} %get-tuple-element.47) | copy-start | bytes 884740
  93.7 1.0 copy-start.2
  107.7 6.6 %copy-start.18 = (f32[2,768]{1,0:T(2,128)S(1)}, f32[2,768]{1,0:T(2,128)}, u32[]{:S(2)}) copy-start(f32[2,768]{1,0:T(2,128)} %param.11) | copy-start | bytes 18436
  107.7 33.3 %all-to-all-start.3 = ((bf16[2,48,4,2,768]{4,3,2,0,1:T(2,128)(2,1)}), bf16[2,48,4,2,768]{4,3,2,0,1:T(2,128)(2,1)}, u32[]{:S(2)}, u32[]{:S(2)}) async-start(bf16[2,48,4,2,768]{4,3,2,0,1:T(2,128)(2,1)} %copy.208), calls=%async_computation.3 | async-start | bytes 2359296 | tf_op jit(solution)/shard_map/all_to_all | solution.py:135
  128.1 2.0 copy-start.3
  131.0 16.2 %copy-start.8 = (bf16[384,2,8,96]{3,2,1,0:T(8,128)(2,1)S(1)}, bf16[384,2,8,96]{3,2,1,0:T(8,128)(2,1)}, u32[]{:S(2)}) copy-start(bf16[384,2,8,96]{3,2,1,0:T(8,128)(2,1)} %reshape.383) | copy-start | bytes 3538948
  141.0 161.6 %all-to-all-start.1 = ((bf16[2,48,4,2,768]{4,3,2,0,1:T(2,128)(2,1)}), bf16[2,48,4,2,768]{4,3,2,0,1:T(2,128)(2,1)}, u32[]{:S(2)}, u32[]{:S(2)}) async-start(bf16[2,48,4,2,768]{4,3,2,0,1:T(2,128)(2,1)} %copy.193), calls=%async_computation.1 | async-start | bytes 2359296 | tf_op jit(solution)/shard_map/all_to_all | solution.py:122
  147.2 144.0 %all-reduce.4.cloned.1.call-start = ((), (), s32[]{:S(2)}) async-start(), calls=%async_computation.4 | async-start | bytes 3145728 | tf_op jit(solution)/shard_map/psum | solution.py:141
  291.2 2.2 copy-start.9
  297.1 2.4 copy-start.14
  297.1 2.4 copy-start.16
  305.4 2.5 copy-start.1
Sparse Core Ops, SparseCore 0:
  154.0 137.0 all-reduce.3
where the time goes:
time: 319 us; the launch traced here: 318 us
  waiting for transfers between devices  132 us (41%)
  local copies, waits for them, and re-layouts  60.8 us (19%)
  blocking collectives  49.3 us (15%)
  starting transfers between devices  27.5 us (9%)
  matrix products  23.1 us (7%)
  between operations  14.5 us (5%)
  other arithmetic  10.6 us (3%)
    psum x1, waiting for transfers between devices, shards(): lax.psum((partials[0], partials[1], partials[2], partials[3]), ('seq', 'r...  89.5 us
    psum x1, blocking collectives, shards(): lax.psum((partials[0], partials[1], partials[2], partials[3]), ('seq', 'r...  49.3 us
    all_to_all x1, waiting for transfers between devices, shards(): lax.all_to_all(spec_rows, 'seq', split_axis=2, concat_axis=1, tiled=True)  23.8 us
    all_to_all x1, waiting for transfers between devices, shards(): lax.all_to_all(cot_rows, 'seq', split_axis=2, concat_axis=1, tiled=True)  9.66 us
    all_to_all x1, waiting for transfers between devices, shards(): lax.all_to_all(back_rows(spectrum_grad), 'seq', split_axis=1, concat_axis...  9.04 us
    unnamed x44, local copies, waits for them, and re-layouts  8.83 us
    all_to_all x1, starting transfers between devices, shards(): lax.all_to_all(spec_rows, 'seq', split_axis=2, concat_axis=1, tiled=True)  8.47 us
    all_to_all x1, starting transfers between devices, shards(): lax.all_to_all(back_rows(spectrum_grad), 'seq', split_axis=1, concat_axis...  6.58 us
  transfers between devices with their start and end apart: 5, of which 4 were waited for; matrix products, arithmetic and copies ran while one was open for 16% of the time, Pallas kernels for 0%

commit v1 on v0

v1 whole, which is shorter than its diff:
```python
import functools
import math

import jax
import jax.numpy as jnp
import numpy as np
from jax import lax
from jax.experimental import pallas as pl
from jax.experimental.pallas import tpu as pltpu
from jax.sharding import PartitionSpec as P

BLOCKS = 8
BLOCK = 96
MODES = 64
HALVES = 2
HALF = BLOCKS // HALVES * BLOCK
GROUPS = 8
GROUP = MODES // GROUPS
CK = 2 * GROUP
F32 = jnp.float32
BF16 = jnp.bfloat16


def grid_tables(length, modes):
    position = np.arange(length)
    frequency = np.arange(modes)
    residue = position[:, None] * frequency[None, :] % length
    angles = residue.astype(np.float32) * np.float32(2.0 * math.pi / length)
    factor = np.float32(1.0 / math.sqrt(length))
    cosine = (np.cos(angles) * factor).astype(np.float32).astype(BF16)
    sine = (np.sin(angles) * factor).astype(np.float32).astype(BF16)
    return cosine.astype(np.float32), sine.astype(np.float32)


def column_tables(width):
    cosine, sine = grid_tables(width, MODES)
    table = np.stack([cosine.T, -sine.T])
    doubling = np.where(np.arange(MODES) == 0, 1.0, 2.0).astype(np.float32)
    doubled = table * doubling[None, :, None]

    def order(t):
        t = t.reshape(2, GROUPS, GROUP, width).transpose(1, 0, 2, 3)
        return t.reshape(2 * MODES, width)

    return order(table), order(doubled)


def row_matrix(length):
    cosine, sine = grid_tables(length, length)
    small = np.stack(
        [np.stack([cosine.T, sine.T], axis=2), np.stack([-sine.T, cosine.T], axis=2)]
    )
    full = np.zeros((2, length, GROUP, length, 2, GROUP), np.float32)
    for k in range(GROUP):
        full[:, :, k, :, :, k] = small
    size = length * CK
    return full.reshape(size, size)


def dot(a, b):
    return lax.dot_general(a, b, (((1,), (0,)), ((), ())), preferred_element_type=F32)


def dot_t(a, b):
    return lax.dot_general(a, b, (((0,), (0,)), ((), ())), preferred_element_type=F32)


def far(*arrays):
    return [pltpu.with_memory_space_constraint(x, pltpu.HBM) for x in arrays]


def params(limit):
    return pltpu.CompilerParams(vmem_limit_bytes=limit * 1024 * 1024)


def cost(us):
    return pl.CostEstimate(flops=int(us * 2e8), bytes_accessed=int(us * 1e6), transcendentals=0)


def columns_kernel(x_ref, t_ref, o_ref):
    y = dot(t_ref[...], x_ref[0, 0]).astype(BF16)
    for half in range(HALVES):
        part = y[:, half * HALF : (half + 1) * HALF]
        o_ref[half, 0, :, 0] = part.reshape(GROUPS, CK, HALF)


def tile_spec(rows, local):
    return pl.BlockSpec(
        (HALVES, 1, GROUPS, 1, CK, HALF),
        lambda s, h: (0, s // local, 0, (s % local) * rows + h, 0, 0),
    )


def columns(x, table, dims):
    samples, rows, width, channels = x.shape
    split, local = dims
    return pl.pallas_call(
        columns_kernel,
        grid=(samples, rows),
        in_specs=[
            pl.BlockSpec((1, 1, width, channels), lambda s, h: (s, h, 0, 0)),
            pl.BlockSpec((2 * MODES, width), lambda s, h: (0, 0)),
        ],
        out_specs=tile_spec(rows, local),
        out_shape=pltpu.HBM((HALVES, split, GROUPS, local * rows, CK, HALF), BF16),
        compiler_params=params(6),
        cost_estimate=cost(3),
        name="columns",
    )(x, table)


def inverse_kernel(x_ref, t_ref, z_ref, o_ref):
    z = jnp.concatenate(
        [z_ref[half, 0, :, 0].reshape(2 * MODES, HALF) for half in range(HALVES)], axis=1
    )
    o_ref[0, 0] = (x_ref[0, 0].astype(F32) + dot(t_ref[...], z)).astype(BF16)


def inverse(x, table, z, dims):
    samples, rows, width, channels = x.shape
    whole = pl.BlockSpec((1, 1, width, channels), lambda s, h: (s, h, 0, 0))
    return pl.pallas_call(
        inverse_kernel,
        grid=(samples, rows),
        in_specs=[
            whole,
            pl.BlockSpec((width, 2 * MODES), lambda s, h: (0, 0)),
            tile_spec(rows, dims[1]),
        ],
        out_specs=whole,
        out_shape=jax.ShapeDtypeStruct(x.shape, BF16),
        compiler_params=params(8),
        cost_estimate=cost(4),
        name="inverse",
    )(x, table, z)


def prepare_kernel(half_ref, m_ref, wi_ref, wo_ref, n_ref, *outs):
    del half_ref
    n_ref[...] = m_ref[...].astype(F32).T.astype(BF16)
    row = lax.broadcasted_iota(jnp.int32, (BLOCK, HALF), 0)
    lane = lax.broadcasted_iota(jnp.int32, (BLOCK, HALF), 1)
    for w_ref, f_ref, t_ref in ((wi_ref, outs[0], outs[1]), (wo_ref, outs[2], outs[3])):
        diagonal = []
        for c in range(2):
            pieces = []
            for j in range(HALF // BLOCK):
                place = jnp.where(lane == row + j * BLOCK, 1.0, 0.0).astype(BF16)
                pieces.append(dot(w_ref[c, j], place))
            diagonal.append(jnp.concatenate(pieces, axis=0))
        real, imag = diagonal
        real_t, imag_t = real.T.astype(BF16), imag.T.astype(BF16)
        real, imag = real.astype(BF16), imag.astype(BF16)
        f_ref[:HALF, :HALF] = real
        f_ref[:HALF, HALF:] = imag
        f_ref[HALF:, :HALF] = -imag
        f_ref[HALF:, HALF:] = real
        t_ref[:HALF, :HALF] = real_t
        t_ref[:HALF, HALF:] = -imag_t
        t_ref[HALF:, :HALF] = imag_t
        t_ref[HALF:, HALF:] = real_t


def prepare(half, matrix, in_weight, out_weight):
    size = matrix.shape[0]
    weight = pl.BlockSpec((2, HALF // BLOCK, BLOCK, BLOCK), lambda i, half: (0, half[0], 0, 0))
    square = pl.BlockSpec((size, size), lambda i, half: (0, 0))
    wide = pl.BlockSpec((2 * HALF, 2 * HALF), lambda i, half: (0, 0))
    return pl.pallas_call(
        prepare_kernel,
        grid_spec=pltpu.PrefetchScalarGridSpec(
            num_scalar_prefetch=1,
            grid=(1,),
            in_specs=[square, weight, weight],
            out_specs=[square] + [wide] * 4,
        ),
        out_shape=[pltpu.HBM((size, size), BF16)] + [pltpu.HBM((2 * HALF, 2 * HALF), BF16)] * 4,
        compiler_params=params(24),
        cost_estimate=cost(4),
        name="prepare",
    )(half, matrix, in_weight, out_weight)


SLOPE = math.sqrt(2.0 / math.pi)


def side_by_side(x):
    rows = x.shape[0] // 2
    return jnp.concatenate([x[:rows], x[rows:]], axis=1)


def stacked(x):
    return jnp.concatenate([x[:, :HALF], x[:, HALF:]], axis=0)


def bias_row(ref):
    return jnp.concatenate([ref[0:1, :], ref[1:2, :]], axis=1)


def forward_kernel(
    half_ref, v_ref, m_ref, n_ref, wi_ref, wo_ref, bi_ref, bo_ref, o_ref, s_ref, h_ref, d_ref
):
    del half_ref
    size = m_ref.shape[0]
    spectrum = dot(m_ref[...], v_ref[...].reshape(size, HALF)).astype(BF16)
    s_ref[0] = spectrum
    pre = dot(side_by_side(spectrum), wi_ref[...]) + bias_row(bi_ref)
    square = pre * pre
    tanh = jnp.tanh(SLOPE * (pre + 0.044715 * (square * pre)))
    gate = 0.5 * (1.0 + tanh)
    hidden = (pre * gate).astype(BF16)
    d_ref[0] = gate + 0.5 * pre * (1.0 - tanh * tanh) * (SLOPE * (1.0 + 3 * 0.044715 * square))
    h_ref[0] = stacked(hidden)
    out = (dot(hidden, wo_ref[...]) + bias_row(bo_ref)).astype(BF16)
    back = dot(n_ref[...], stacked(out)).astype(BF16)
    o_ref[...] = back.reshape(o_ref.shape)


def forward(rows, local, half, v, m, n, wi, wo, in_bias, out_bias):
    shards = v.shape[0]
    size = m.shape[0]
    chunk = pl.BlockSpec((shards, rows, CK, HALF), lambda s, half: (0, s, 0, 0))
    square = pl.BlockSpec((size, size), lambda s, half: (0, 0))
    wide = pl.BlockSpec((2 * HALF, 2 * HALF), lambda s, half: (0, 0))
    bias = pl.BlockSpec((2, HALF), lambda s, half: (0, half[0]))
    tall = pl.BlockSpec((1, size, HALF), lambda s, half: (s, 0, 0))
    pair = pl.BlockSpec((1, size // 2, 2 * HALF), lambda s, half: (s, 0, 0))
    return pl.pallas_call(
        forward_kernel,
        grid_spec=pltpu.PrefetchScalarGridSpec(
            num_scalar_prefetch=1,
            grid=(local,),
            in_specs=[chunk, square, square, wide, wide, bias, bias],
            out_specs=[chunk, tall, tall, pair],
        ),
        out_shape=[
            pltpu.HBM(v.shape, BF16),
            pltpu.HBM((local, size, HALF), BF16),
            pltpu.HBM((local, size, HALF), BF16),
            pltpu.HBM((local, size // 2, 2 * HALF), F32),
        ],
        compiler_params=params(32),
        cost_estimate=cost(9),
        name="forward",
    )(half, *far(v, m, n, wi, wo), in_bias, out_bias)


PACK = 256


def outer_parts(p_ref, at, left, right):
    rows = right.shape[0] // 2
    turned = jnp.concatenate([right[rows:], -right[:rows]], axis=0)
    full = dot_t(left, jnp.concatenate([right, turned], axis=1))
    block = lax.broadcasted_iota(jnp.int32, (BLOCK, HALF), 1) // BLOCK
    for c in range(2):
        part = full[:, c * HALF : (c + 1) * HALF]
        packed = part[:BLOCK]
        for j in range(1, HALF // BLOCK):
            packed = jnp.where(block == j, part[j * BLOCK : (j + 1) * BLOCK], packed)
        p_ref[at, c * BLOCK : (c + 1) * BLOCK] += packed
    for c in range(2):
        total = jnp.sum(right[c * rows : (c + 1) * rows].astype(F32), axis=0, keepdims=True)
        p_ref[at, 2 * BLOCK + c : 2 * BLOCK + c + 1] += total


def backward_kernel(
    v_ref, m_ref, n_ref, wi_ref, wo_ref, s_ref, h_ref, d_ref, o_ref, p_ref
):
    size = m_ref.shape[0]

    @pl.when(pl.program_id(0) == 0)
    def _():
        p_ref[...] = jnp.zeros_like(p_ref)

    incoming = dot(m_ref[...], v_ref[...].reshape(size, HALF)).astype(BF16)
    hidden_grad = dot(side_by_side(incoming), wo_ref[...])
    pre_grad = (hidden_grad * d_ref[0]).astype(BF16)
    grad = dot(pre_grad, wi_ref[...]).astype(BF16)
    back = dot(n_ref[...], stacked(grad)).astype(BF16)
    o_ref[...] = back.reshape(o_ref.shape)
    outer_parts(p_ref, 0, s_ref[0], stacked(pre_grad))
    outer_parts(p_ref, 1, h_ref[0], incoming)


def backward(rows, local, v, m, n, wi, wo, spectrum, hidden, slope):
    shards = v.shape[0]
    size = m.shape[0]
    chunk = pl.BlockSpec((shards, rows, CK, HALF), lambda s: (0, s, 0, 0))
    square = pl.BlockSpec((size, size), lambda s: (0, 0))
    wide = pl.BlockSpec((2 * HALF, 2 * HALF), lambda s: (0, 0))
    tall = pl.BlockSpec((1, size, HALF), lambda s: (s, 0, 0))
    pair = pl.BlockSpec((1, size // 2, 2 * HALF), lambda s: (s, 0, 0))
    return pl.pallas_call(
        backward_kernel,
        grid=(local,),
        in_specs=[chunk, square, square, wide, wide, tall, tall, pair],
        out_specs=[chunk, pl.BlockSpec((2, PACK, HALF), lambda s: (0, 0, 0))],
        out_shape=[
            pltpu.HBM((shards, local * rows + 1, CK, HALF), BF16),
            jax.ShapeDtypeStruct((2, PACK, HALF), F32),
        ],
        compiler_params=params(32),
        cost_estimate=cost(9),
        name="backward",
    )(*far(v, m, n, wi, wo, spectrum, hidden, slope))


def unpack_kernel(scale, x_ref, iw_ref, ib_ref, ow_ref, ob_ref):
    per = HALF // BLOCK
    for mat, w_ref, b_ref in ((0, iw_ref, ib_ref), (1, ow_ref, ob_ref)):
        for half in range(HALVES):
            for c in range(2):
                part = x_ref[half, mat, c * BLOCK : (c + 1) * BLOCK].astype(F32) * scale
                for j in range(per):
                    moved = part if j == 0 else pltpu.roll(part, HALF - j * BLOCK, 1)
                    w_ref[c, half * per + j] = moved[:, :BLOCK]
            rows = x_ref[half, mat, 2 * BLOCK : 2 * BLOCK + 16].astype(F32) * scale
            b_ref[:, half * HALF : (half + 1) * HALF] = rows[:2]


def unpack(x, scale):
    weight = jax.ShapeDtypeStruct((2, BLOCKS, BLOCK, BLOCK), F32)
    bias = jax.ShapeDtypeStruct((2, HALVES * HALF), F32)
    return pl.pallas_call(
        functools.partial(unpack_kernel, scale),
        out_shape=[weight, bias, weight, bias],
        compiler_params=params(8),
        cost_estimate=cost(2),
        name="unpack",
    )(x)


def swap(x, axis, size, bit):
    return lax.ppermute(x, axis, [(i, i ^ bit) for i in range(size)])


def bits_below(size):
    return [1 << b for b in range((size - 1).bit_length())]


def shards(tokens, cotangent, in_weight, in_bias, out_weight, out_bias):
    samples, row_count, width, _ = tokens.shape
    seq, rep = lax.axis_size("seq"), lax.axis_size("rep")
    split = seq // (HALVES * GROUPS)
    dims = (split, samples // split)
    at, core = lax.axis_index("seq"), lax.axis_index("rep")
    half = (at // (seq // HALVES)).astype(jnp.int32).reshape(1)
    plain, doubled = column_tables(width)
    matrix = jnp.asarray(row_matrix(row_count * seq), BF16)

    def exchange(x):
        return lax.all_to_all(x.reshape((seq,) + x.shape[-3:]), "seq", 0, 0, tiled=True)

    def tiles(x):
        return x.reshape((HALVES, split, GROUPS) + x.shape[1:])

    received = exchange(columns(tokens, jnp.asarray(plain, BF16), dims))
    cot_rows = columns(cotangent, jnp.asarray(doubled, BF16), dims)
    prepared = prepare(half, matrix, in_weight, out_weight)
    cot_rows, prepared = lax.optimization_barrier((cot_rows, prepared))
    inv_matrix, in_fwd, in_bwd, out_fwd, out_bwd = prepared
    incoming = exchange(cot_rows)
    back, spectrum, hidden, slope = forward(
        row_count, dims[1], half, received, matrix, inv_matrix, in_fwd, out_fwd, in_bias, out_bias
    )
    back = exchange(back)
    grad, packet = backward(
        row_count, dims[1], incoming, matrix, inv_matrix, in_bwd, out_bwd, spectrum, hidden, slope
    )

    piece = packet.reshape(2 * PACK, HALF)
    steps = [(core, b) for b in reversed(bits_below(rep))]
    for index, bit in steps:
        count = piece.shape[0] // 2
        mine = (index // bit) % 2
        kept = lax.dynamic_slice_in_dim(piece, mine * count, count, 0)
        sent = lax.dynamic_slice_in_dim(piece, (1 - mine) * count, count, 0)
        piece = kept + swap(sent, "rep", rep, bit)
    part = piece.shape[0] // seq
    share = piece.astype(BF16).reshape(seq, part, HALF)
    if part < CK:
        share = jnp.pad(share, ((0, 0), (0, CK - part), (0, 0)))
    grad = lax.dynamic_update_slice(grad, share[:, None], (0, grad.shape[1] - 1, 0, 0))
    grad, back = lax.optimization_barrier((grad, back))
    grad = exchange(grad)
    total = grad[:, -1, :part].reshape(HALVES, seq // HALVES, part, HALF)
    total = jnp.sum(total.astype(F32), axis=1).astype(BF16)
    mixed_out = inverse(tokens, jnp.asarray(doubled.T, BF16), tiles(back), dims)
    total, mixed_out = lax.optimization_barrier((total, mixed_out))
    gathered = exchange(jnp.broadcast_to(total[None], (seq,) + total.shape))
    tokens_grad = inverse(cotangent, jnp.asarray(plain.T, BF16), tiles(grad), dims)
    gathered, tokens_grad = lax.optimization_barrier((gathered, tokens_grad))
    piece = gathered.transpose(1, 0, 2, 3).reshape(HALVES, seq * part, HALF)
    for index, bit in reversed(steps):
        other = swap(piece, "rep", rep, bit)
        first = ((index // bit) % 2) == 0
        piece = jnp.concatenate(
            [jnp.where(first, piece, other), jnp.where(first, other, piece)], axis=1
        )
    packets = piece.reshape(HALVES, 2, PACK, HALF)
    gradients = unpack(packets, 1.0 / (samples * rep))
    return (mixed_out, tokens_grad, *gradients)


def solution(mesh):
    in_specs = (P("rep", "seq", None, None), P("rep", "seq", None, None), P(), P(), P(), P())
    out_specs = (P("rep", "seq", None, None), P("rep", "seq", None, None), P(), P(), P(), P())
    return jax.shard_map(shards, mesh=mesh, in_specs=in_specs, out_specs=out_specs, check_vma=False)
```

time: 319 us -> 172 us (0.54)
  waiting for transfers between devices: 132 us -> 79.2 us
  blocking collectives: 49.3 us -> 0 us
  local copies, waits for them, and re-layouts: 60.8 us -> 16.1 us
  Pallas kernels: 0 us -> 39.3 us
  matrix products: 23.1 us -> 0 us
  between operations: 14.5 us -> 0.89 us
  other arithmetic: 10.6 us -> 1.38 us
  starting transfers between devices: 27.5 us -> 34.3 us
    psum x1 -> x0, waiting for transfers between devices: 89.5 us -> none  [shards(): lax.psum((partials[0], partials[1], partials[2], partials[3]), ('seq', 'r...]
    psum x1 -> x0, blocking collectives: 49.3 us -> none  [shards(): lax.psum((partials[0], partials[1], partials[2], partials[3]), ('seq', 'r...]
    pallas_call x0 -> x8, Pallas kernels: none -> 39.3 us  [the longest x1 10.9 us: backward(): pl.pallas_call(backward_kernel, grid=(local,), in_specs=[chunk, square, s...]
    all_to_all x4 -> x5, waiting for transfers between devices: 42.5 us -> 77.1 us  [exchange(): lax.all_to_all(x.reshape((seq,) + x.shape[-3:]), 'seq', 0, 0, tiled=True)]
    dot_general x14 -> x0, matrix products: 23.1 us -> none  [the longest x1 4.46 us: mix_forward(): jnp.einsum('mcbi,bciej->mebj', hidden, weights_out, preferred_element_typ...]
    convert_element_type x8 -> x0, local copies, waits for them, and re-layouts: 18 us -> none  [the longest x2 3.92 us: back_rows(): return jnp.einsum('qehc,sqked->shkcd', row_matrix, section, preferred_ele...]
    reshape x5 -> x0, local copies, waits for them, and re-layouts: 17.6 us -> none  [the longest x1 4.65 us: mix_backward(): spectrum_grad = spectrum_grad.astype(jnp.bfloat16).reshape(incoming.shape)]
    all_to_all x6 -> x0, local copies, waits for them, and re-layouts: 13.4 us -> none  [the longest x2 5.31 us: shards(): lax.all_to_all(back_rows(spectrum_out), 'seq', split_axis=1, concat_axis=...]
  transfers between devices with their start and end apart: 5 -> 7, of which waited for: 4 -> 6; matrix products, arithmetic and copies ran while one was open for 16% -> 6% of each run, Pallas kernels for 0% -> 20%
where the time goes in v1:
time: 172 us; the launch traced here: 171 us
  waiting for transfers between devices  79.2 us (46%)
  Pallas kernels  39.3 us (23%)
  starting transfers between devices  34.3 us (20%)
  local copies, waits for them, and re-layouts  16.1 us (9%)
    all_to_all x5, waiting for transfers between devices, exchange(): lax.all_to_all(x.reshape((seq,) + x.shape[-3:]), 'seq', 0, 0, tiled=True)  77.1 us
    all_to_all x5, starting transfers between devices, exchange(): lax.all_to_all(x.reshape((seq,) + x.shape[-3:]), 'seq', 0, 0, tiled=True)  34.3 us
    unnamed x26, local copies, waits for them, and re-layouts  11.9 us
    pallas_call x1, Pallas kernels, backward(): pl.pallas_call(backward_kernel, grid=(local,), in_specs=[chunk, square, s...  10.9 us
    pallas_call x1, Pallas kernels, forward(): pl.pallas_call(forward_kernel, grid_spec=pltpu.PrefetchScalarGridSpec(num...  9.9 us
    pallas_call x2, Pallas kernels, inverse(): pl.pallas_call(inverse_kernel, grid=(samples, rows), in_specs=[whole, pl....  7.71 us
    pallas_call x2, Pallas kernels, columns(): pl.pallas_call(columns_kernel, grid=(samples, rows), in_specs=[pl.BlockSp...  6.01 us
  transfers between devices with their start and end apart: 7, of which 6 were waited for; matrix products, arithmetic and copies ran while one was open for 6% of the time, Pallas kernels for 20%

profile of v1, /device:TPU:0, one launch (start us, length us, event | category | flops | bytes accessed | tf_op | source)
XLA Modules:
  0.0 171.2 jit_solution(3306321485928142240)
XLA Ops:
  0.6 1.7 copy.30.x_ref
  2.3 3.0 %columns.3 = bf16[2,1,8,6,16,384]{5,4,3,2,1,0:T(8,128)(2,1)} custom-call(bf16[2,3,180,768]{3,2,1,0:T(8,128)(2,1)S(1)} %copy.30.x_ref, bf16[128,180]{1,0:T(8,128)(2,1)S(1)} %copy-done.4), custom_call_target="tpu_custom_call" | custom-call | flops 600000000 | bytes 3000000 | tf_op jit(solution)/shard_map/columns/pallas_call | solution.py:97
  5.3 8.4 %all-to-all-start.1 = ((bf16[16,6,16,384]{3,2,1,0:T(8,128)(2,1)}), bf16[16,6,16,384]{3,2,1,0:T(8,128)(2,1)}, u32[]{:S(2)}, u32[]{:S(2)}) async-start(bf16[16,6,16,384]{3,2,1,0:T(8,128)(2,1)} %bitcast.19), calls=%async_computation.1 | async-start | bytes 2359296 | tf_op jit(solution)/shard_map/all_to_all | solution.py:353
  13.7 1.7 copy.29.x_ref
  15.5 3.0 %columns.2 = bf16[2,1,8,6,16,384]{5,4,3,2,1,0:T(8,128)(2,1)} custom-call(bf16[2,3,180,768]{3,2,1,0:T(8,128)(2,1)S(1)} %copy.29.x_ref, bf16[128,180]{1,0:T(8,128)(2,1)S(1)} %copy-done.3), custom_call_target="tpu_custom_call" | custom-call | flops 600000000 | bytes 3000000 | tf_op jit(solution)/shard_map/columns/pallas_call | solution.py:97
  18.5 3.3 %prepare.1 = (bf16[768,768]{1,0:T(8,128)(2,1)}, bf16[768,768]{1,0:T(8,128)(2,1)}, bf16[768,768]{1,0:T(8,128)(2,1)}, bf16[768,768]{1,0:T(8,128)(2,1)}, bf16[768,768]{1,0:T(8,128)(2,1)}) custom-call(s32[1]{0:T(128)} %bitcast.half_ref, bf16[768,768]{1,0:T(8,128)(2,1)S(1)} %copy-done.1, bf16[2,8,96,96]{3,2,1,0:T(8,128)(2,1)S(1)} %copy-done.7, ...), custom_call_target="tpu_custom_call" | custom-call | flops 800000000 | bytes 4000000 | tf_op jit(solution)/shard_map/prepare/pallas_call | solution.py:169
  21.8 18.9 %all-to-all-done.1.v_ref = bf16[16,6,16,384]{3,2,1,0:T(8,128)(2,1)} async-done(((bf16[16,6,16,384]{3,2,1,0:T(8,128)(2,1)}), bf16[16,6,16,384]{3,2,1,0:T(8,128)(2,1)}, u32[]{:S(2)}, u32[]{:S(2)}) %all-to-all-start.1) | async-done | bytes 1179680 | tf_op jit(solution)/shard_map/all_to_all | solution.py:353
  40.7 6.2 %all-to-all-start = ((bf16[16,6,16,384]{3,2,1,0:T(8,128)(2,1)}), bf16[16,6,16,384]{3,2,1,0:T(8,128)(2,1)}, u32[]{:S(2)}, u32[]{:S(2)}) async-start(bf16[16,6,16,384]{3,2,1,0:T(8,128)(2,1)} %bitcast.20), calls=%async_computation | async-start | bytes 2359296 | tf_op jit(solution)/shard_map/all_to_all | solution.py:353
  47.0 9.9 %forward.1 = (bf16[16,6,16,384]{3,2,1,0:T(8,128)(2,1)}, bf16[2,768,384]{2,1,0:T(8,128)(2,1)}, bf16[2,768,384]{2,1,0:T(8,128)(2,1)}, f32[2,384,768]{2,1,0:T(8,128)}) custom-call(s32[1]{0:T(128)} %bitcast.half_ref, bf16[16,6,16,384]{3,2,1,0:T(8,128)(2,1)} %all-to-all-done.1.v_ref, bf16[768,768]{1,0:T(8,128)(2,1)} %constant.68.clone.m_ref, ...), custom_call_target="tpu_custom_call" | custom-call | flops 1800000000 | bytes 9000000 | tf_op jit(solution)/shard_map/forward/pallas_call | solution.py:228
  56.9 15.9 %all-to-all-done.v_ref = bf16[16,6,16,384]{3,2,1,0:T(8,128)(2,1)} async-done(((bf16[16,6,16,384]{3,2,1,0:T(8,128)(2,1)}), bf16[16,6,16,384]{3,2,1,0:T(8,128)(2,1)}, u32[]{:S(2)}, u32[]{:S(2)}) %all-to-all-start) | async-done | bytes 1179680 | tf_op jit(solution)/shard_map/all_to_all | solution.py:353
  72.8 6.6 %all-to-all-start.2 = ((bf16[16,6,16,384]{3,2,1,0:T(8,128)(2,1)}), bf16[16,6,16,384]{3,2,1,0:T(8,128)(2,1)}, u32[]{:S(2)}, u32[]{:S(2)}) async-start(bf16[16,6,16,384]{3,2,1,0:T(8,128)(2,1)} %get-tuple-element.49), calls=%async_computation.2 | async-start | bytes 2359296 | tf_op jit(solution)/shard_map/all_to_all | solution.py:353
  79.4 10.9 %backward.1 = (bf16[16,7,16,384]{3,2,1,0:T(8,128)(2,1)}, f32[2,256,384]{2,1,0:T(8,128)S(1)}) custom-call(bf16[16,6,16,384]{3,2,1,0:T(8,128)(2,1)} %all-to-all-done.v_ref, bf16[768,768]{1,0:T(8,128)(2,1)} %constant.68.clone.m_ref, bf16[768,768]{1,0:T(8,128)(2,1)} %get-tuple-element.39.n_ref, bf16[768,768]{1,0:T(8,128)(2,1)} %get-tuple-element.40.wi_ref, ...), custom_call_target="tpu_custom_call" | custom-call | flops 1800000000 | bytes 9000000 | tf_op jit(solution)/shard_map/backward/pallas_call | solution.py:294
  90.3 0.9 copy-done.2
  91.2 0.8 constant_dynamic-slice_fusion
  92.0 2.1 %collective-permute-done = f32[256,384]{1,0:T(8,128)} collective-permute-done((f32[256,384]{1,0:T(8,128)}, f32[256,384]{1,0:T(8,128)}, u32[]{:S(2)}, u32[]{:S(2)}) %collective-permute-start) | collective-permute-done | bytes 393248 | tf_op jit(solution)/shard_map/ppermute | solution.py:335
  94.0 1.2 add_convert_fusion
  95.2 0.7 constant_dynamic-update-slice_fusion
  95.9 9.8 %all-to-all-done.2 = bf16[16,6,16,384]{3,2,1,0:T(8,128)(2,1)} async-done(((bf16[16,6,16,384]{3,2,1,0:T(8,128)(2,1)}), bf16[16,6,16,384]{3,2,1,0:T(8,128)(2,1)}, u32[]{:S(2)}, u32[]{:S(2)}) %all-to-all-start.2) | async-done | bytes 1179680 | tf_op jit(solution)/shard_map/all_to_all | solution.py:353
  105.7 6.2 %all-to-all-start.3 = ((bf16[16,7,16,384]{3,2,1,0:T(8,128)(2,1)}), bf16[16,7,16,384]{3,2,1,0:T(8,128)(2,1)}, u32[]{:S(2)}, u32[]{:S(2)}) async-start(bf16[16,7,16,384]{3,2,1,0:T(8,128)(2,1)} %constant_dynamic-update-slice_fusion), calls=%async_computation.3 | async-start | bytes 2752512 | tf_op jit(solution)/shard_map/all_to_all | solution.py:353
  112.0 3.9 %inverse.2 = bf16[2,3,180,768]{3,2,1,0:T(8,128)(2,1)S(1)} custom-call(bf16[2,3,180,768]{3,2,1,0:T(8,128)(2,1)S(1)} %copy.30.x_ref, bf16[180,128]{1,0:T(8,128)(2,1)S(1)} %copy-done.6, bf16[2,1,8,6,16,384]{5,4,3,2,1,0:T(8,128)(2,1)} %bitcast.6.z_ref), custom_call_target="tpu_custom_call" | custom-call | flops 800000000 | bytes 4000000 | tf_op jit(solution)/shard_map/inverse/pallas_call | solution.py:122
  115.8 1.2 copy-done
  117.0 24.7 %all-to-all-done.3 = bf16[16,7,16,384]{3,2,1,0:T(8,128)(2,1)} async-done(((bf16[16,7,16,384]{3,2,1,0:T(8,128)(2,1)}), bf16[16,7,16,384]{3,2,1,0:T(8,128)(2,1)}, u32[]{:S(2)}, u32[]{:S(2)}) %all-to-all-start.3) | async-done | bytes 1376288 | tf_op jit(solution)/shard_map/all_to_all | solution.py:353
  141.7 0.9 slice.4
  142.7 0.8 broadcast_in_dim.2
  143.5 6.8 %all-to-all-start.4 = ((bf16[16,2,16,384]{3,2,1,0:T(8,128)(2,1)}), bf16[16,2,16,384]{3,2,1,0:T(8,128)(2,1)}, u32[]{:S(2)}, u32[]{:S(2)}) async-start(bf16[16,2,16,384]{3,2,1,0:T(8,128)(2,1)} %broadcast_in_dim.2), calls=%async_computation.4 | async-start | bytes 786432 | tf_op jit(solution)/shard_map/all_to_all | solution.py:353
  150.3 3.9 %inverse.3 = bf16[2,3,180,768]{3,2,1,0:T(8,128)(2,1)S(1)} custom-call(bf16[2,3,180,768]{3,2,1,0:T(8,128)(2,1)S(1)} %copy.29.x_ref, bf16[180,128]{1,0:T(8,128)(2,1)S(1)} %copy-done.5, bf16[2,1,8,7,16,384]{5,4,3,2,1,0:T(8,128)(2,1)} %bitcast.7.z_ref), custom_call_target="tpu_custom_call" | custom-call | flops 800000000 | bytes 4000000 | tf_op jit(solution)/shard_map/inverse/pallas_call | solution.py:122
  154.2 7.8 %all-to-all-done.4 = bf16[16,2,16,384]{3,2,1,0:T(8,128)(2,1)} async-done(((bf16[16,2,16,384]{3,2,1,0:T(8,128)(2,1)}), bf16[16,2,16,384]{3,2,1,0:T(8,128)(2,1)}, u32[]{:S(2)}, u32[]{:S(2)}) %all-to-all-start.4) | async-done | bytes 393248 | tf_op jit(solution)/shard_map/all_to_all | solution.py:353
  162.0 1.0 copy.33
  163.1 3.9 %copy.34 = bf16[2,3,180,768]{3,0,2,1:T(2,128)(2,1)} copy(bf16[2,3,180,768]{3,2,1,0:T(8,128)(2,1)} %copy-done) | data formatting | bytes 3317760
  167.0 2.4 %copy.35 = bf16[2,3,180,768]{3,0,2,1:T(2,128)(2,1)} copy(bf16[2,3,180,768]{3,2,1,0:T(8,128)(2,1)S(1)} %inverse.3) | data formatting | bytes 3317760
  169.4 0.1 broadcast_select_fusion.1
  169.6 1.6 unpack.1
  (25 shorter events, 0.2 us)
Async XLA Ops:
  0.6 1.7 copy-start.4
  5.3 35.4 %all-to-all-start.1 = ((bf16[16,6,16,384]{3,2,1,0:T(8,128)(2,1)}), bf16[16,6,16,384]{3,2,1,0:T(8,128)(2,1)}, u32[]{:S(2)}, u32[]{:S(2)}) async-start(bf16[16,6,16,384]{3,2,1,0:T(8,128)(2,1)} %bitcast.19), calls=%async_computation.1 | async-start | bytes 2359296 | tf_op jit(solution)/shard_map/all_to_all | solution.py:353
  13.7 1.7 %copy-start.3 = (bf16[128,180]{1,0:T(8,128)(2,1)S(1)}, bf16[128,180]{1,0:T(8,128)(2,1)}, u32[]{:S(2)}) copy-start(bf16[128,180]{1,0:T(8,128)(2,1)} %constant.70.clone.t_ref) | copy-start | bytes 138244
  15.4 3.1 %copy-start.1 = (bf16[768,768]{1,0:T(8,128)(2,1)S(1)}, bf16[768,768]{1,0:T(8,128)(2,1)}, u32[]{:S(2)}) copy-start(bf16[768,768]{1,0:T(8,128)(2,1)} %constant.68.clone.m_ref) | copy-start | bytes 3538948
  15.5 3.1 %copy-start.7 = (bf16[2,8,96,96]{3,2,1,0:T(8,128)(2,1)S(1)}, bf16[2,8,96,96]{3,2,1,0:T(8,128)(2,1)}, u32[]{:S(2)}) copy-start(bf16[2,8,96,96]{3,2,1,0:T(8,128)(2,1)} %wi_ref.1) | copy-start | bytes 884740
  15.5 3.1 %copy-start.8 = (bf16[2,8,96,96]{3,2,1,0:T(8,128)(2,1)S(1)}, bf16[2,8,96,96]{3,2,1,0:T(8,128)(2,1)}, u32[]{:S(2)}) copy-start(bf16[2,8,96,96]{3,2,1,0:T(8,128)(2,1)} %wo_ref.1) | copy-start | bytes 884740
  21.8 25.1 %copy-start.9 = (f32[2,768]{1,0:T(2,128)S(1)}, f32[2,768]{1,0:T(2,128)}, u32[]{:S(2)}) copy-start(f32[2,768]{1,0:T(2,128)} %bi_ref.1) | copy-start | bytes 18436
  21.8 25.1 %copy-start.10 = (f32[2,768]{1,0:T(2,128)S(1)}, f32[2,768]{1,0:T(2,128)}, u32[]{:S(2)}) copy-start(f32[2,768]{1,0:T(2,128)} %bo_ref.1) | copy-start | bytes 18436
  40.7 32.1 %all-to-all-start = ((bf16[16,6,16,384]{3,2,1,0:T(8,128)(2,1)}), bf16[16,6,16,384]{3,2,1,0:T(8,128)(2,1)}, u32[]{:S(2)}, u32[]{:S(2)}) async-start(bf16[16,6,16,384]{3,2,1,0:T(8,128)(2,1)} %bitcast.20), calls=%async_computation | async-start | bytes 2359296 | tf_op jit(solution)/shard_map/all_to_all | solution.py:353
  72.8 33.0 %all-to-all-start.2 = ((bf16[16,6,16,384]{3,2,1,0:T(8,128)(2,1)}), bf16[16,6,16,384]{3,2,1,0:T(8,128)(2,1)}, u32[]{:S(2)}, u32[]{:S(2)}) async-start(bf16[16,6,16,384]{3,2,1,0:T(8,128)(2,1)} %get-tuple-element.49), calls=%async_computation.2 | async-start | bytes 2359296 | tf_op jit(solution)/shard_map/all_to_all | solution.py:353
  90.3 0.9 copy-start.2
  92.0 2.1 %collective-permute-start = (f32[256,384]{1,0:T(8,128)}, f32[256,384]{1,0:T(8,128)}, u32[]{:S(2)}, u32[]{:S(2)}) collective-permute-start(f32[256,384]{1,0:T(8,128)} %constant_dynamic-slice_fusion), channel_id=1, source_target_pairs={{0,1},{1,0},{2,3},{3,2},{4,5},{5,4},{6,7},{7,6},{8,9},{9,8},{10,11... | collective-permute-start | bytes 1179656 | tf_op jit(solution)/shard_map/ppermute | solution.py:335
  95.9 16.1 %copy-start.6 = (bf16[180,128]{1,0:T(8,128)(2,1)S(1)}, bf16[180,128]{1,0:T(8,128)(2,1)}, u32[]{:S(2)}) copy-start(bf16[180,128]{1,0:T(8,128)(2,1)} %constant.71.clone.t_ref) | copy-start | bytes 138244
  105.7 36.0 %all-to-all-start.3 = ((bf16[16,7,16,384]{3,2,1,0:T(8,128)(2,1)}), bf16[16,7,16,384]{3,2,1,0:T(8,128)(2,1)}, u32[]{:S(2)}, u32[]{:S(2)}) async-start(bf16[16,7,16,384]{3,2,1,0:T(8,128)(2,1)} %constant_dynamic-update-slice_fusion), calls=%async_computation.3 | async-start | bytes 2752512 | tf_op jit(solution)/shard_map/all_to_all | solution.py:353
  115.8 1.2 copy-start
  117.0 33.3 %copy-start.5 = (bf16[180,128]{1,0:T(8,128)(2,1)S(1)}, bf16[180,128]{1,0:T(8,128)(2,1)}, u32[]{:S(2)}) copy-start(bf16[180,128]{1,0:T(8,128)(2,1)} %constant.72.clone.t_ref) | copy-start | bytes 138244
  143.5 18.5 %all-to-all-start.4 = ((bf16[16,2,16,384]{3,2,1,0:T(8,128)(2,1)}), bf16[16,2,16,384]{3,2,1,0:T(8,128)(2,1)}, u32[]{:S(2)}, u32[]{:S(2)}) async-start(bf16[16,2,16,384]{3,2,1,0:T(8,128)(2,1)} %broadcast_in_dim.2), calls=%async_computation.4 | async-start | bytes 786432 | tf_op jit(solution)/shard_map/all_to_all | solution.py:353
  163.0 6.4 %collective-permute-start.1 = (bf16[2,256,384]{2,1,0:T(8,128)(2,1)S(1)}, bf16[2,256,384]{2,1,0:T(8,128)(2,1)S(1)}, u32[]{:S(2)}, u32[]{:S(2)}) collective-permute-start(bf16[2,256,384]{2,1,0:T(8,128)(2,1)S(1)} %bitcast.21), channel_id=1, source_target_pairs={{0,1},{1,0},{2,3},{3,2},{4,5},{5,4},{6,7},{7,6},{8,9},{9,8},{10,11... | collective-permute-start | bytes 1179656 | tf_op jit(solution)/shard_map/ppermute | solution.py:335

commit v2 on v1

v2 whole, which is shorter than its diff:
```python
import functools
import math

import jax
import jax.numpy as jnp
import numpy as np
from jax import lax
from jax.experimental import pallas as pl
from jax.experimental.pallas import tpu as pltpu
from jax.sharding import PartitionSpec as P

BLOCKS = 8
BLOCK = 96
MODES = 64
HALVES = 2
HALF = BLOCKS // HALVES * BLOCK
GROUPS = 8
GROUP = MODES // GROUPS
CK = 2 * GROUP
F32 = jnp.float32
BF16 = jnp.bfloat16


def grid_tables(length, modes):
    position = np.arange(length)
    frequency = np.arange(modes)
    residue = position[:, None] * frequency[None, :] % length
    angles = residue.astype(np.float32) * np.float32(2.0 * math.pi / length)
    factor = np.float32(1.0 / math.sqrt(length))
    cosine = (np.cos(angles) * factor).astype(np.float32).astype(BF16)
    sine = (np.sin(angles) * factor).astype(np.float32).astype(BF16)
    return cosine.astype(np.float32), sine.astype(np.float32)


def column_tables(width, samples):
    cosine, sine = grid_tables(width, MODES)
    table = np.stack([cosine.T, -sine.T])
    doubling = np.where(np.arange(MODES) == 0, 1.0, 2.0).astype(np.float32)
    doubled = table * doubling[None, :, None]

    def ordered(t):
        t = t.reshape(2, GROUPS, GROUP, width).transpose(1, 0, 2, 3).reshape(2 * MODES, width)
        full = np.zeros((samples, 2 * MODES, width, samples), np.float32)
        for s in range(samples):
            full[s, :, :, s] = t
        return full.reshape(samples * 2 * MODES, width * samples)

    return ordered(table), ordered(doubled)


def row_matrix(length):
    cosine, sine = grid_tables(length, length)
    small = np.stack(
        [np.stack([cosine.T, sine.T], axis=2), np.stack([-sine.T, cosine.T], axis=2)]
    )
    full = np.zeros((2, length, GROUP, length, 2, GROUP), np.float32)
    for k in range(GROUP):
        full[:, :, k, :, :, k] = small
    size = length * CK
    return full.reshape(size, size).T


def dot(a, b):
    return lax.dot_general(a, b, (((1,), (0,)), ((), ())), preferred_element_type=F32)


def dot_t(a, b):
    return lax.dot_general(a, b, (((0,), (0,)), ((), ())), preferred_element_type=F32)


def far(*arrays):
    return [pltpu.with_memory_space_constraint(x, pltpu.HBM) for x in arrays]


def params(limit):
    return pltpu.CompilerParams(vmem_limit_bytes=limit * 1024 * 1024)


def cost(us):
    return pl.CostEstimate(flops=int(us * 2e8), bytes_accessed=int(us * 1e6), transcendentals=0)


def half_lanes(half):
    return pl.ds(pl.multiple_of(half * HALF, HALF), HALF)


def column_modes(x_ref, t_ref):
    _, width, samples, channels = x_ref.shape
    return dot(t_ref[...], x_ref[0].reshape(width * samples, channels)).astype(BF16)


def columns_kernel(x_ref, t_ref, o_ref):
    y = column_modes(x_ref, t_ref)
    _, split, _, local = o_ref.shape[:4]
    for s in range(split * local):
        for half in range(HALVES):
            part = y[s * 2 * MODES : (s + 1) * 2 * MODES, half * HALF : (half + 1) * HALF]
            o_ref[half, s // local, :, s % local, 0] = part.reshape(GROUPS, CK, HALF)


def tile_spec(dims):
    split, local = dims
    return pl.BlockSpec(
        (HALVES, split, GROUPS, local, 1, CK, HALF), lambda h: (0, 0, 0, 0, h, 0, 0)
    )


def columns(x, table, dims):
    rows, width, samples, channels = x.shape
    split, local = dims
    return pl.pallas_call(
        columns_kernel,
        grid=(rows,),
        in_specs=[
            pl.BlockSpec((1, width, samples, channels), lambda h: (h, 0, 0, 0)),
            pl.BlockSpec(table.shape, lambda h: (0, 0)),
        ],
        out_specs=tile_spec(dims),
        out_shape=pltpu.HBM((HALVES, split, GROUPS, local, rows, CK, HALF), BF16),
        compiler_params=params(16),
        cost_estimate=cost(3),
        name="columns",
    )(*far(x), table)


def columns_apart_kernel(at_ref, x_ref, t_ref, *refs):
    *outs, y_ref = refs
    y_ref[...] = column_modes(x_ref, t_ref).reshape(y_ref.shape)
    split, local = outs[0].shape[:2]
    for s in range(split * local):
        for a in range(HALVES):
            lanes = half_lanes(a ^ at_ref[1])
            for b in range(GROUPS):
                tile = y_ref[s * GROUPS + (b ^ at_ref[3]), :, lanes]
                outs[GROUPS * a + b][(s // local) ^ at_ref[2], s % local, 0] = tile


def columns_apart(at, x, table, dims):
    rows, width, samples, channels = x.shape
    split, local = dims
    out = pl.BlockSpec((split, local, 1, CK, HALF), lambda h, at: (0, 0, h, 0, 0))
    return pl.pallas_call(
        columns_apart_kernel,
        grid_spec=pltpu.PrefetchScalarGridSpec(
            num_scalar_prefetch=1,
            grid=(rows,),
            in_specs=[
                pl.BlockSpec((1, width, samples, channels), lambda h, at: (h, 0, 0, 0)),
                pl.BlockSpec(table.shape, lambda h, at: (0, 0)),
            ],
            out_specs=[out] * (HALVES * GROUPS),
            scratch_shapes=[pltpu.VMEM((samples * GROUPS, CK, channels), BF16)],
        ),
        out_shape=[pltpu.HBM((split, local, rows, CK, HALF), BF16)] * (HALVES * GROUPS),
        compiler_params=params(16),
        cost_estimate=cost(3),
        name="columns_apart",
    )(at, *far(x), table)


def add_modes(o_ref, x_ref, t_ref, z):
    _, width, samples, channels = x_ref.shape
    x = x_ref[0].reshape(width * samples, channels).astype(F32)
    o_ref[0] = (x + dot(t_ref[...], z)).astype(BF16).reshape(width, samples, channels)


def inverse_kernel(x_ref, t_ref, z_ref, o_ref):
    _, split, _, local = z_ref.shape[:4]
    z = jnp.concatenate(
        [
            jnp.concatenate(
                [
                    z_ref[half, s // local, :, s % local, 0].reshape(2 * MODES, HALF)
                    for half in range(HALVES)
                ],
                axis=1,
            )
            for s in range(split * local)
        ],
        axis=0,
    )
    add_modes(o_ref, x_ref, t_ref, z)


def inverse(x, table, z, dims):
    rows, width, samples, channels = x.shape
    whole = pl.BlockSpec((1, width, samples, channels), lambda h: (h, 0, 0, 0))
    return pl.pallas_call(
        inverse_kernel,
        grid=(rows,),
        in_specs=[whole, pl.BlockSpec(table.shape, lambda h: (0, 0)), tile_spec(dims)],
        out_specs=whole,
        out_shape=pltpu.HBM(x.shape, BF16),
        compiler_params=params(16),
        cost_estimate=cost(4),
        name="inverse",
    )(*far(x), table, *far(z))


def inverse_apart_kernel(at_ref, x_ref, t_ref, *refs):
    *slabs, o_ref, z_ref = refs
    split, local = slabs[0].shape[0], len(slabs) // (HALVES * GROUPS)
    for s in range(split * local):
        for a in range(HALVES):
            lanes = half_lanes(a ^ at_ref[1])
            for b in range(GROUPS):
                slab = slabs[(GROUPS * a + b) * local + s % local]
                tile = slab[(s // local) ^ at_ref[2], 0]
                z_ref[s * GROUPS + (b ^ at_ref[3]), :, lanes] = tile
    add_modes(o_ref, x_ref, t_ref, z_ref[...].reshape(t_ref.shape[1], x_ref.shape[3]))


def inverse_apart(at, x, table, slabs, dims):
    rows, width, samples, channels = x.shape
    split, local = dims
    whole = pl.BlockSpec((1, width, samples, channels), lambda h, at: (h, 0, 0, 0))
    slab = [
        pl.BlockSpec((split, 1, CK, HALF), lambda h, at, l=l: (0, l * rows + h, 0, 0))
        for l in range(local)
    ]
    return pl.pallas_call(
        inverse_apart_kernel,
        grid_spec=pltpu.PrefetchScalarGridSpec(
            num_scalar_prefetch=1,
            grid=(rows,),
            in_specs=[whole, pl.BlockSpec(table.shape, lambda h, at: (0, 0))]
            + slab * len(slabs),
            out_specs=whole,
            scratch_shapes=[pltpu.VMEM((samples * GROUPS, CK, channels), BF16)],
        ),
        out_shape=pltpu.HBM(x.shape, BF16),
        compiler_params=params(16),
        cost_estimate=cost(4),
        name="inverse_apart",
    )(at, *far(x), table, *[y for y in far(*slabs) for _ in range(local)])


def transposed(out_ref, blocks):
    for j in range(0, len(blocks), 8):
        rows = jnp.concatenate([x.astype(F32) for x in blocks[j : j + 8]], axis=0)
        width = rows.shape[0]
        out_ref[:, (j // 8) * width : (j // 8 + 1) * width] = rows.T.astype(BF16)


def prepare_kernel(at_ref, base_ref, wi_ref, wo_ref, m_ref, mx_ref, nx_ref, *outs):
    shards = base_ref.shape[0]
    transposed(m_ref, [base_ref[r] for r in range(shards)])
    for r in range(shards):
        nx_ref[r] = base_ref[r ^ at_ref[0]]
    transposed(mx_ref, [nx_ref[r] for r in range(shards)])
    row = lax.broadcasted_iota(jnp.int32, (BLOCK, HALF), 0)
    lane = lax.broadcasted_iota(jnp.int32, (BLOCK, HALF), 1)
    for w_ref, f_ref, t_ref in ((wi_ref, outs[0], outs[1]), (wo_ref, outs[2], outs[3])):
        diagonal = []
        for c in range(2):
            pieces = []
            for j in range(HALF // BLOCK):
                place = jnp.where(lane == row + j * BLOCK, 1.0, 0.0).astype(BF16)
                pieces.append(dot(w_ref[c, j], place))
            diagonal.append(jnp.concatenate(pieces, axis=0))
        real, imag = diagonal
        real_t, imag_t = real.T.astype(BF16), imag.T.astype(BF16)
        real, imag = real.astype(BF16), imag.astype(BF16)
        f_ref[:HALF, :HALF] = real
        f_ref[:HALF, HALF:] = imag
        f_ref[HALF:, :HALF] = -imag
        f_ref[HALF:, HALF:] = real
        t_ref[:HALF, :HALF] = real_t
        t_ref[:HALF, HALF:] = -imag_t
        t_ref[HALF:, :HALF] = imag_t
        t_ref[HALF:, HALF:] = real_t


def prepare(at, base, in_weight, out_weight):
    blocks, rows, size = base.shape
    weight = pl.BlockSpec((2, HALF // BLOCK, BLOCK, BLOCK), lambda i, at: (0, at[1], 0, 0))
    square = pl.BlockSpec((size, size), lambda i, at: (0, 0))
    stack = pl.BlockSpec((blocks, rows, size), lambda i, at: (0, 0, 0))
    wide = pl.BlockSpec((2 * HALF, 2 * HALF), lambda i, at: (0, 0))
    return pl.pallas_call(
        prepare_kernel,
        grid_spec=pltpu.PrefetchScalarGridSpec(
            num_scalar_prefetch=1,
            grid=(1,),
            in_specs=[stack, weight, weight],
            out_specs=[square, square, stack] + [wide] * 4,
        ),
        out_shape=[pltpu.HBM((size, size), BF16)] * 2
        + [pltpu.HBM((blocks, rows, size), BF16)]
        + [pltpu.HBM((2 * HALF, 2 * HALF), BF16)] * 4,
        compiler_params=params(40),
        cost_estimate=cost(4),
        name="prepare",
    )(at, base, in_weight, out_weight)


SLOPE = math.sqrt(2.0 / math.pi)


def side_by_side(x):
    rows = x.shape[0] // 2
    return jnp.concatenate([x[:rows], x[rows:]], axis=1)


def stacked(x):
    return jnp.concatenate([x[:, :HALF], x[:, HALF:]], axis=0)


def bias_row(ref):
    return jnp.concatenate([ref[0:1, :], ref[1:2, :]], axis=1)


def forward_kernel(
    at_ref, v_ref, m_ref, n_ref, wi_ref, wo_ref, bi_ref, bo_ref, o_ref, s_ref, h_ref, d_ref
):
    del at_ref
    size = m_ref.shape[0]
    spectrum = dot(m_ref[...], v_ref[...].reshape(size, HALF)).astype(BF16)
    s_ref[0] = spectrum
    pre = dot(side_by_side(spectrum), wi_ref[...]) + bias_row(bi_ref)
    square = pre * pre
    tanh = jnp.tanh(SLOPE * (pre + 0.044715 * (square * pre)))
    gate = 0.5 * (1.0 + tanh)
    hidden = (pre * gate).astype(BF16)
    d_ref[0] = gate + 0.5 * pre * (1.0 - tanh * tanh) * (SLOPE * (1.0 + 3 * 0.044715 * square))
    h_ref[0] = stacked(hidden)
    out = (dot(hidden, wo_ref[...]) + bias_row(bo_ref)).astype(BF16)
    back = dot(n_ref[...].reshape(size, size), stacked(out)).astype(BF16)
    o_ref[...] = back.reshape(o_ref.shape)


def forward(rows, local, at, v, m, n, wi, wo, in_bias, out_bias):
    shards = v.shape[0]
    size = m.shape[0]
    chunk = pl.BlockSpec((shards, rows, CK, HALF), lambda s, at: (0, s, 0, 0))
    square = pl.BlockSpec((size, size), lambda s, at: (0, 0))
    stack = pl.BlockSpec(n.shape, lambda s, at: (0, 0, 0))
    wide = pl.BlockSpec((2 * HALF, 2 * HALF), lambda s, at: (0, 0))
    bias = pl.BlockSpec((2, HALF), lambda s, at: (0, at[1]))
    tall = pl.BlockSpec((1, size, HALF), lambda s, at: (s, 0, 0))
    pair = pl.BlockSpec((1, size // 2, 2 * HALF), lambda s, at: (s, 0, 0))
    return pl.pallas_call(
        forward_kernel,
        grid_spec=pltpu.PrefetchScalarGridSpec(
            num_scalar_prefetch=1,
            grid=(local,),
            in_specs=[chunk, square, stack, wide, wide, bias, bias],
            out_specs=[chunk, tall, tall, pair],
        ),
        out_shape=[
            pltpu.HBM(v.shape, BF16),
            pltpu.HBM((local, size, HALF), BF16),
            pltpu.HBM((local, size, HALF), BF16),
            pltpu.HBM((local, size // 2, 2 * HALF), F32),
        ],
        compiler_params=params(40),
        cost_estimate=cost(9),
        name="forward",
    )(at, *far(v, m, n, wi, wo), in_bias, out_bias)


PACK = 256


def outer_parts(p_ref, at, left, right):
    rows = right.shape[0] // 2
    turned = jnp.concatenate([right[rows:], -right[:rows]], axis=0)
    full = dot_t(left, jnp.concatenate([right, turned], axis=1))
    block = lax.broadcasted_iota(jnp.int32, (BLOCK, HALF), 1) // BLOCK
    for c in range(2):
        part = full[:, c * HALF : (c + 1) * HALF]
        packed = part[:BLOCK]
        for j in range(1, HALF // BLOCK):
            packed = jnp.where(block == j, part[j * BLOCK : (j + 1) * BLOCK], packed)
        p_ref[at, c * BLOCK : (c + 1) * BLOCK] += packed
    for c in range(2):
        total = jnp.sum(right[c * rows : (c + 1) * rows].astype(F32), axis=0, keepdims=True)
        p_ref[at, 2 * BLOCK + c : 2 * BLOCK + c + 1] += total


def backward_kernel(at_ref, m_ref, wi_ref, wo_ref, s_ref, h_ref, d_ref, *refs):
    *slabs, g_ref, kept_ref, sent_ref, p_ref = refs

    @pl.when(pl.program_id(0) == 0)
    def _():
        p_ref[...] = jnp.zeros_like(p_ref)

    rows = slabs[0].shape[0] * CK
    v = jnp.concatenate([x[...].reshape(rows, HALF) for x in slabs], axis=0)
    incoming = dot(m_ref[...], v).astype(BF16)
    hidden_grad = dot(side_by_side(incoming), wo_ref[...])
    pre_grad = (hidden_grad * d_ref[0]).astype(BF16)
    outer_parts(p_ref, 0, s_ref[0], stacked(pre_grad))
    outer_parts(p_ref, 1, h_ref[0], incoming)
    g_ref[0] = stacked(dot(pre_grad, wi_ref[...]).astype(BF16))

    @pl.when(pl.program_id(0) == pl.num_programs(0) - 1)
    def _():
        kept_ref[...] = p_ref[at_ref[4]]
        sent_ref[...] = p_ref[1 - at_ref[4]]


def backward(rows, local, at, slabs, m, wi, wo, spectrum, hidden, slope):
    size = m.shape[0]
    slab = pl.BlockSpec((rows, CK, HALF), lambda s, at: (s, 0, 0))
    square = pl.BlockSpec((size, size), lambda s, at: (0, 0))
    wide = pl.BlockSpec((2 * HALF, 2 * HALF), lambda s, at: (0, 0))
    tall = pl.BlockSpec((1, size, HALF), lambda s, at: (s, 0, 0))
    pair = pl.BlockSpec((1, size // 2, 2 * HALF), lambda s, at: (s, 0, 0))
    packet = pl.BlockSpec((PACK, HALF), lambda s, at: (0, 0))
    return pl.pallas_call(
        backward_kernel,
        grid_spec=pltpu.PrefetchScalarGridSpec(
            num_scalar_prefetch=1,
            grid=(local,),
            in_specs=[square, wide, wide, tall, tall, pair] + [slab] * len(slabs),
            out_specs=[tall, packet, packet],
            scratch_shapes=[pltpu.VMEM((2, PACK, HALF), F32)],
        ),
        out_shape=[pltpu.HBM((local, size, HALF), BF16)] + [pltpu.HBM((PACK, HALF), F32)] * 2,
        compiler_params=params(40),
        cost_estimate=cost(9),
        name="backward",
    )(at, *far(m, wi, wo, spectrum, hidden, slope, *slabs))


def rows_back_kernel(at_ref, n_ref, g_ref, kept_ref, other_ref, *outs):
    blocks, rows, size = n_ref.shape
    local = g_ref.shape[0]
    for s in range(local):
        back = dot(n_ref[...].reshape(blocks * rows, size), g_ref[s]).astype(BF16)
        back = back.reshape(blocks, rows // CK, CK, HALF)
        for r in range(blocks):
            outs[r][s * rows // CK : (s + 1) * rows // CK] = back[r]
    for r in range(blocks):
        to = r ^ at_ref[0]
        outs[r][local * rows // CK] = (kept_ref[to] + other_ref[to]).astype(BF16)


def rows_back(at, n, grad, kept, other):
    blocks, rows, _ = n.shape
    local = grad.shape[0]
    return pl.pallas_call(
        rows_back_kernel,
        in_specs=[pl.BlockSpec(memory_space=pltpu.SMEM)] + [pl.BlockSpec()] * 4,
        out_shape=[pltpu.HBM((local * rows // CK + 1, CK, HALF), BF16)] * blocks,
        compiler_params=params(24),
        cost_estimate=cost(4),
        name="rows_back",
    )(at, *far(n, grad, kept, other))


def totals_kernel(at_ref, *refs):
    *shares, o_ref = refs
    count = len(shares) // HALVES
    for a in range(HALVES):
        total = shares[a * count][0].astype(F32)
        for x in shares[a * count + 1 : (a + 1) * count]:
            total = total + x[0].astype(F32)
        total = total.astype(BF16)
        for t in range(len(shares)):
            o_ref[t, a ^ at_ref[1]] = total


def totals(at, slabs):
    last = slabs[0].shape[0] - 1
    share = pl.BlockSpec((1, CK, HALF), lambda i, at: (last, 0, 0))
    shape = (len(slabs), HALVES, CK, HALF)
    return pl.pallas_call(
        totals_kernel,
        grid_spec=pltpu.PrefetchScalarGridSpec(
            num_scalar_prefetch=1,
            grid=(1,),
            in_specs=[share] * len(slabs),
            out_specs=pl.BlockSpec(shape, lambda i, at: (0, 0, 0, 0)),
        ),
        out_shape=pltpu.HBM(shape, BF16),
        compiler_params=params(8),
        cost_estimate=cost(2),
        name="totals",
    )(at, *far(*slabs))


def unpack_kernel(scale, at_ref, x_ref, y_ref, iw_ref, ib_ref, ow_ref, ob_ref, pack_ref):
    per = HALF // BLOCK
    for i, ref in enumerate((x_ref, y_ref)):
        for place in range(ref.shape[0]):
            for half in range(HALVES):
                pack_ref[i ^ at_ref[4], half, place] = ref[place, half].astype(F32) * scale
    for mat, w_ref, b_ref in ((0, iw_ref, ib_ref), (1, ow_ref, ob_ref)):
        for half in range(HALVES):
            part = pack_ref[mat, half].reshape(PACK, HALF)
            for j in range(per):
                moved = part if j == 0 else pltpu.roll(part, HALF - j * BLOCK, 1)
                for c in range(2):
                    w_ref[c, half * per + j] = moved[c * BLOCK : (c + 1) * BLOCK, :BLOCK]
            b_ref[:, half * HALF : (half + 1) * HALF] = part[2 * BLOCK : 2 * BLOCK + 2]


def unpack(at, x, y, scale):
    weight = jax.ShapeDtypeStruct((2, BLOCKS, BLOCK, BLOCK), F32)
    bias = jax.ShapeDtypeStruct((2, HALVES * HALF), F32)
    return pl.pallas_call(
        functools.partial(unpack_kernel, scale),
        in_specs=[pl.BlockSpec(memory_space=pltpu.SMEM)]
        + [pl.BlockSpec(memory_space=pltpu.VMEM)] * 2,
        out_shape=[weight, bias, weight, bias],
        scratch_shapes=[pltpu.VMEM((2, HALVES, x.shape[0], CK, HALF), F32)],
        compiler_params=params(16),
        cost_estimate=cost(2),
        name="unpack",
    )(at, x, y)


def unpack_joined(scale, packets):
    per = HALF // BLOCK
    out = []
    for mat in range(2):
        both = packets[mat].astype(F32) * scale
        weight = both[:, : 2 * BLOCK].reshape(HALVES, 2, BLOCK, per, BLOCK)
        out.append(weight.transpose(1, 0, 3, 2, 4).reshape(2, BLOCKS, BLOCK, BLOCK))
        out.append(both[:, 2 * BLOCK : 2 * BLOCK + 2].transpose(1, 0, 2).reshape(2, -1))
    return out


def swap(x, axis, size, bit):
    return lax.ppermute(x, axis, [(i, i ^ bit) for i in range(size)])


def far_first(seq):
    quarter = max(seq // 4, 1)
    classes = [2, 3, 1, 0] if seq >= 4 else [1, 0]
    spread = [[c * quarter + i for i in range(quarter)] for c in classes]
    far = [r for pair in zip(spread[0], spread[1]) for r in pair]
    return [r for r in far + spread[2] + spread[3] if r]


def bits_below(size):
    return [1 << b for b in range((size - 1).bit_length())]


def program(tokens, cotangent, in_weight, in_bias, out_weight, out_bias):
    samples, rows, width, _ = tokens.shape
    seq, rep = lax.axis_size("seq"), lax.axis_size("rep")
    split = seq // (HALVES * GROUPS)
    dims = (split, samples // split)
    local = dims[1]
    place, core = lax.axis_index("seq"), lax.axis_index("rep")
    at = jnp.stack(
        [
            place,
            place // (seq // HALVES),
            place // GROUPS % split,
            place % GROUPS,
            core // max(rep // 2, 1),
        ]
    ).astype(jnp.int32)
    plain, doubled = column_tables(width, samples)
    tokens, cotangent = (x.transpose(1, 2, 0, 3) for x in (tokens, cotangent))
    base = jnp.asarray(row_matrix(rows * seq).reshape(seq, rows * CK, -1), BF16)

    def table(t):
        return jnp.asarray(t, BF16)

    def exchange(x):
        return lax.all_to_all(x.reshape((seq, -1) + x.shape[-2:]), "seq", 0, 0, tiled=True)

    def apart(slabs):
        out = {0: slabs[0]}
        for r in far_first(seq):
            out[r] = swap(slabs[r], "seq", seq, r)
        return [out[r] for r in range(seq)]

    received = exchange(columns(tokens, table(plain), dims))
    cot = columns_apart(at, cotangent, table(doubled), dims)
    cot = [
        cot[GROUPS * a + b][c].reshape(local * rows, CK, HALF)
        for a in range(2)
        for c in range(split)
        for b in range(GROUPS)
    ]
    incoming = apart(cot)
    matrix, matrix_x, base_x, in_fwd, in_bwd, out_fwd, out_bwd = prepare(
        at, base, in_weight, out_weight
    )
    back, spectrum, hidden, slope = forward(
        rows, local, at, received, matrix, base, in_fwd, out_fwd, in_bias, out_bias
    )
    back = exchange(back)
    grad, kept, sent = backward(
        rows, local, at, incoming, matrix_x, in_bwd, out_bwd, spectrum, hidden, slope
    )

    bits = bits_below(rep)[::-1]
    other = swap(sent, "rep", rep, bits[0]) if bits else jnp.zeros_like(sent)
    for bit in bits[1:]:
        piece = kept + other
        count = piece.shape[0] // 2
        mine = (core // bit) % 2
        kept = lax.dynamic_slice_in_dim(piece, mine * count, count, 0)
        sent = lax.dynamic_slice_in_dim(piece, (1 - mine) * count, count, 0)
        other = swap(sent, "rep", rep, bit)
    part = kept.shape[0] // seq

    def by_place(x):
        x = x.reshape(seq, part, HALF)
        return jnp.pad(x, ((0, 0), (0, CK - part), (0, 0))) if part < CK else x

    grad = apart(rows_back(at, base_x, grad, by_place(kept), by_place(other)))
    mixed_out = inverse(
        tokens,
        table(doubled.T),
        back.reshape(HALVES, split, GROUPS, local, rows, CK, HALF),
        dims,
    )
    total = totals(at, grad)
    gathered = exchange(total)
    slabs = [
        jnp.stack([grad[(a * split + c) * GROUPS + b] for c in range(split)])
        for a in range(2)
        for b in range(GROUPS)
    ]
    tokens_grad = inverse_apart(at, cotangent, table(plain.T), slabs, dims)
    gathered, tokens_grad = lax.optimization_barrier((gathered, tokens_grad))
    scale = 1.0 / (samples * rep)
    if rep == 2 and part == CK:
        gradients = unpack(at, gathered, swap(gathered, "rep", rep, 1), scale)
    else:
        piece = gathered[:, :, :part].transpose(1, 0, 2, 3).reshape(HALVES, seq * part, HALF)
        for bit in bits[::-1]:
            other = swap(piece, "rep", rep, bit)
            first = ((core // bit) % 2) == 0
            piece = jnp.concatenate(
                [jnp.where(first, piece, other), jnp.where(first, other, piece)], axis=1
            )
        packets = piece.reshape(HALVES, 2, PACK, HALF).transpose(1, 0, 2, 3)
        gradients = unpack_joined(scale, packets)
    mixed_out, tokens_grad = (x.transpose(2, 0, 1, 3) for x in (mixed_out, tokens_grad))
    return (mixed_out, tokens_grad, *gradients)


def solution(mesh):
    in_specs = (P("rep", "seq", None, None), P("rep", "seq", None, None), P(), P(), P(), P())
    out_specs = (P("rep", "seq", None, None), P("rep", "seq", None, None), P(), P(), P(), P())
    return jax.shard_map(program, mesh=mesh, in_specs=in_specs, out_specs=out_specs, check_vma=False)
```

time: 172 us -> 199 us (1.16)
  starting transfers between devices: 34.3 us -> 65.7 us
  waiting for transfers between devices: 79.2 us -> 53.4 us
  blocking collectives: 0 us -> 18.6 us
  Pallas kernels: 39.3 us -> 52.3 us
  local copies, waits for them, and re-layouts: 16.1 us -> 6.31 us
    all_to_all x5 -> x2, waiting for transfers between devices: 77.1 us -> 16.2 us  [exchange(): lax.all_to_all(x.reshape((seq, -1) + x.shape[-2:]), 'seq', 0, 0, tiled=True)]
    ppermute x2 -> x32, starting transfers between devices: 0.07 us -> 53.4 us  [swap(): return lax.ppermute(x, axis, [(i, i ^ bit) for i in range(size)])]
    ppermute x2 -> x32, waiting for transfers between devices: 2.06 us -> 37.2 us  [swap(): return lax.ppermute(x, axis, [(i, i ^ bit) for i in range(size)])]
    all_to_all x5 -> x2, starting transfers between devices: 34.3 us -> 12.3 us  [exchange(): lax.all_to_all(x.reshape((seq, -1) + x.shape[-2:]), 'seq', 0, 0, tiled=True)]
    all_to_all x0 -> x1, blocking collectives: none -> 18.6 us  [exchange(): lax.all_to_all(x.reshape((seq, -1) + x.shape[-2:]), 'seq', 0, 0, tiled=True)]
    pallas_call x6 -> x8, Pallas kernels: 26.2 us -> 37.4 us  [the longest x1 10.5 us: backward(): pl.pallas_call(backward_kernel, grid_spec=pltpu.PrefetchScalarGridSpec(nu...]
    unnamed x26 -> x84, local copies, waits for them, and re-layouts: 11.9 us -> 6.22 us
  transfers between devices with their start and end apart: 7 -> 34, of which waited for: 6 -> 7; matrix products, arithmetic and copies ran while one was open for 6% -> 0% of each run, Pallas kernels for 20% -> 14%
where the time goes in v2:
time: 199 us; the launch traced here: 197 us
  starting transfers between devices  65.7 us (33%)
  waiting for transfers between devices  53.4 us (27%)
  Pallas kernels  52.3 us (26%)
  blocking collectives  18.6 us (9%)
  local copies, waits for them, and re-layouts  6.31 us (3%)
    ppermute x32, starting transfers between devices, swap(): return lax.ppermute(x, axis, [(i, i ^ bit) for i in range(size)])  53.4 us
    ppermute x32, waiting for transfers between devices, swap(): return lax.ppermute(x, axis, [(i, i ^ bit) for i in range(size)])  37.2 us
    all_to_all x1, blocking collectives, exchange(): lax.all_to_all(x.reshape((seq, -1) + x.shape[-2:]), 'seq', 0, 0, tiled=True)  18.6 us
    all_to_all x2, waiting for transfers between devices, exchange(): lax.all_to_all(x.reshape((seq, -1) + x.shape[-2:]), 'seq', 0, 0, tiled=True)  16.2 us
    all_to_all x2, starting transfers between devices, exchange(): lax.all_to_all(x.reshape((seq, -1) + x.shape[-2:]), 'seq', 0, 0, tiled=True)  12.3 us
    pallas_call x1, Pallas kernels, backward(): pl.pallas_call(backward_kernel, grid_spec=pltpu.PrefetchScalarGridSpec(nu...  10.5 us
    pallas_call x1, Pallas kernels, forward(): pl.pallas_call(forward_kernel, grid_spec=pltpu.PrefetchScalarGridSpec(num...  10.4 us
    unnamed x84, local copies, waits for them, and re-layouts  6.22 us
  transfers between devices with their start and end apart: 34, of which 7 were waited for; matrix products, arithmetic and copies ran while one was open for 0% of the time, Pallas kernels for 14%

profile of v2, /device:TPU:0, one launch (start us, length us, event | category | flops | bytes accessed | tf_op | source)
XLA Modules:
  0.0 197.4 jit_solution(3992088342392384587)
XLA Ops:
  1.6 3.8 %columns.1 = bf16[2,1,8,2,3,16,384]{6,5,4,3,2,1,0:T(8,128)(2,1)} custom-call(bf16[3,180,2,768]{3,2,1,0:T(2,128)(2,1)} %bitcast.44, bf16[256,360]{1,0:T(8,128)(2,1)S(1)} %copy-done), custom_call_target="tpu_custom_call" | custom-call | flops 600000000 | bytes 3000000 | tf_op jit(solution)/shard_map/columns/pallas_call | solution.py:111
  5.3 8.5 %all-to-all-start = ((bf16[16,6,16,384]{3,2,1,0:T(8,128)(2,1)}), bf16[16,6,16,384]{3,2,1,0:T(8,128)(2,1)S(1)}, u32[]{:S(2)}, u32[]{:S(2)}) async-start(bf16[16,6,16,384]{3,2,1,0:T(8,128)(2,1)} %bitcast.46), calls=%async_computation | async-start | bytes 2359296 | tf_op jit(solution)/shard_map/all_to_all | solution.py:566
  14.0 4.4 %columns_apart.1 = (bf16[1,2,3,16,384]{4,3,2,1,0:T(8,128)(2,1)}, bf16[1,2,3,16,384]{4,3,2,1,0:T(8,128)(2,1)}, bf16[1,2,3,16,384]{4,3,2,1,0:T(8,128)(2,1)}, bf16[...) custom-call(s32[5]{0:T(128)S(1)} %stack.68.at_ref, ...), custom_call_target="tpu_custom_call" | custom-call | flops 600000000 | bytes 3000000 | tf_op jit(solution)/shard_map/columns_apart/pallas_call | solution.py:142
  18.4 2.0 %collective-permute-start = (bf16[6,16,384]{2,1,0:T(8,128)(2,1)}, bf16[6,16,384]{2,1,0:T(8,128)(2,1)S(1)}, u32[]{:S(2)}, u32[]{:S(2)}) collective-permute-start(bf16[6,16,384]{2,1,0:T(8,128)(2,1)} %bitcast.96), channel_id=1, source_target_pairs={{0,2},{2,0},{4,6},{6,4},{8,10},{10,8},{12,14},{14,12},{16,18},{18,... | collective-permute-start | bytes 221192 | tf_op jit(solution)/shard_map/ppermute | solution.py:527
  21.8 2.4 %collective-permute-start.10 = (bf16[6,16,384]{2,1,0:T(8,128)(2,1)}, bf16[6,16,384]{2,1,0:T(8,128)(2,1)S(1)}, u32[]{:S(2)}, u32[]{:S(2)}) collective-permute-start(bf16[6,16,384]{2,1,0:T(8,128)(2,1)} %bitcast.94), channel_id=1, source_target_pairs={{0,22},{2,20},{4,18},{6,16},{8,30},{10,28},{12,26},{14,24},{16,6},... | collective-permute-start | bytes 221192 | tf_op jit(solution)/shard_map/ppermute | solution.py:527
  25.7 3.3 %collective-permute-start.12 = (bf16[6,16,384]{2,1,0:T(8,128)(2,1)}, bf16[6,16,384]{2,1,0:T(8,128)(2,1)S(1)}, u32[]{:S(2)}, u32[]{:S(2)}) collective-permute-start(bf16[6,16,384]{2,1,0:T(8,128)(2,1)} %bitcast.92), channel_id=1, source_target_pairs={{0,26},{2,24},{4,30},{6,28},{8,18},{10,16},{12,22},{14,20},{16,10}... | collective-permute-start | bytes 221192 | tf_op jit(solution)/shard_map/ppermute | solution.py:527
  28.9 2.4 %collective-permute-start.13 = (bf16[6,16,384]{2,1,0:T(8,128)(2,1)}, bf16[6,16,384]{2,1,0:T(8,128)(2,1)S(1)}, u32[]{:S(2)}, u32[]{:S(2)}) collective-permute-start(bf16[6,16,384]{2,1,0:T(8,128)(2,1)} %bitcast.91), channel_id=1, source_target_pairs={{0,28},{2,30},{4,24},{6,26},{8,20},{10,22},{12,16},{14,18},{16,12}... | collective-permute-start | bytes 221192 | tf_op jit(solution)/shard_map/ppermute | solution.py:527
  31.3 2.4 %collective-permute-start.14 = (bf16[6,16,384]{2,1,0:T(8,128)(2,1)}, bf16[6,16,384]{2,1,0:T(8,128)(2,1)S(1)}, u32[]{:S(2)}, u32[]{:S(2)}) collective-permute-start(bf16[6,16,384]{2,1,0:T(8,128)(2,1)} %bitcast.90), channel_id=1, source_target_pairs={{0,30},{2,28},{4,26},{6,24},{8,22},{10,20},{12,18},{14,16},{16,14}... | collective-permute-start | bytes 221192 | tf_op jit(solution)/shard_map/ppermute | solution.py:527
  33.7 21.3 %collective-permute-done.10.refs_11_ = bf16[6,16,384]{2,1,0:T(8,128)(2,1)S(1)} collective-permute-done((bf16[6,16,384]{2,1,0:T(8,128)(2,1)}, bf16[6,16,384]{2,1,0:T(8,128)(2,1)S(1)}, u32[]{:S(2)}, u32[]{:S(2)}) %collective-permute-start.10) | collective-permute-done | bytes 73760 | tf_op jit(solution)/shard_map/ppermute | solution.py:527
  55.8 2.9 %collective-permute-start.4 = (bf16[6,16,384]{2,1,0:T(8,128)(2,1)}, bf16[6,16,384]{2,1,0:T(8,128)(2,1)S(1)}, u32[]{:S(2)}, u32[]{:S(2)}) collective-permute-start(bf16[6,16,384]{2,1,0:T(8,128)(2,1)} %bitcast.87), channel_id=1, source_target_pairs={{0,10},{2,8},{4,14},{6,12},{8,2},{10,0},{12,6},{14,4},{16,26},{18,... | collective-permute-start | bytes 221192 | tf_op jit(solution)/shard_map/ppermute | solution.py:527
  58.7 4.5 %prepare.1 = (bf16[768,768]{1,0:T(8,128)(2,1)}, bf16[768,768]{1,0:T(8,128)(2,1)}, bf16[16,48,768]{2,1,0:T(8,128)(2,1)}, bf16[768,768]{1,0:T(8,128)(2,1)}, bf16[7...) custom-call(s32[5]{0:T(128)S(1)} %stack.68.at_ref, bf16[16,48,768]{2,1,0:T(8,128)(2,1)S(1)} %copy-done.7, ...), custom_call_target="tpu_custom_call" | custom-call | flops 800000000 | bytes 4000000 | tf_op jit(solution)/shard_map/prepare/pallas_call | solution.py:280
  66.7 3.4 %collective-permute-start.8 = (bf16[6,16,384]{2,1,0:T(8,128)(2,1)}, bf16[6,16,384]{2,1,0:T(8,128)(2,1)S(1)}, u32[]{:S(2)}, u32[]{:S(2)}) collective-permute-start(bf16[6,16,384]{2,1,0:T(8,128)(2,1)} %bitcast.18), channel_id=1, source_target_pairs={{0,18},{2,16},{4,22},{6,20},{8,26},{10,24},{12,30},{14,28},{16,2},... | collective-permute-start | bytes 221192 | tf_op jit(solution)/shard_map/ppermute | solution.py:527
  73.1 10.4 %forward.1 = (bf16[16,6,16,384]{3,2,1,0:T(8,128)(2,1)}, bf16[2,768,384]{2,1,0:T(8,128)(2,1)}, bf16[2,768,384]{2,1,0:T(8,128)(2,1)}, f32[2,384,768]{2,1,0:T(8,128)}) custom-call(s32[5]{0:T(128)S(1)} %stack.68.at_ref, bf16[16,6,16,384]{3,2,1,0:T(8,128)(2,1)} %copy-done.10, bf16[768,768]{1,0:T(8,128)(2,1)} %get-tuple-element.58.m_ref, ...), custom_call_target="tpu_custom_call" | custom-call | flops 1800000000 | bytes 9000000 | tf_op jit(solution)/shard_map/forward/pallas_call | solution.py:342
  84.3 10.5 %backward.1 = (bf16[2,768,384]{2,1,0:T(8,128)(2,1)}, f32[256,384]{1,0:T(8,128)}, f32[256,384]{1,0:T(8,128)}) custom-call(s32[5]{0:T(128)S(1)} %stack.68.at_ref, bf16[768,768]{1,0:T(8,128)(2,1)} %get-tuple-element.63.m_ref, bf16[768,768]{1,0:T(8,128)(2,1)} %get-tuple-element.64.wi_ref, bf16[768,768]{1,0:T(8,128)(2,1)} %get-tuple-element.65.wo_ref, ...), custom_call_target="tpu_custom_call" | custom-call | flops 1800000000 | bytes 9000000 | tf_op jit(solution)/shard_map/backward/pallas_call | solution.py:411
  97.5 4.2 %rows_back.1 = (bf16[7,16,384]{2,1,0:T(8,128)(2,1)}, bf16[7,16,384]{2,1,0:T(8,128)(2,1)}, bf16[7,16,384]{2,1,0:T(8,128)(2,1)}, bf16[7,16,384]{2,1,0:T(8,128)(2,1...) custom-call(s32[5]{0:T(128)S(1)} %stack.68.at_ref, ...), custom_call_target="tpu_custom_call" | custom-call | flops 800000000 | bytes 4000000 | tf_op jit(solution)/shard_map/rows_back/pallas_call | solution.py:443
  103.0 2.2 %collective-permute-start.18 = (bf16[7,16,384]{2,1,0:T(8,128)(2,1)}, bf16[7,16,384]{2,1,0:T(8,128)(2,1)S(1)}, u32[]{:S(2)}, u32[]{:S(2)}) collective-permute-start(bf16[7,16,384]{2,1,0:T(8,128)(2,1)} %get-tuple-element.91), channel_id=1, source_target_pairs={{0,6},{2,4},{4,2},{6,0},{8,14},{10,12},{12,10},{14,8},{16,22},{18,... | collective-permute-start | bytes 258056 | tf_op jit(solution)/shard_map/ppermute | solution.py:527
  109.4 2.0 %collective-permute-start.22 = (bf16[7,16,384]{2,1,0:T(8,128)(2,1)}, bf16[7,16,384]{2,1,0:T(8,128)(2,1)S(1)}, u32[]{:S(2)}, u32[]{:S(2)}) collective-permute-start(bf16[7,16,384]{2,1,0:T(8,128)(2,1)} %get-tuple-element.95), channel_id=1, source_target_pairs={{0,14},{2,12},{4,10},{6,8},{8,6},{10,4},{12,2},{14,0},{16,30},{18,... | collective-permute-start | bytes 258056 | tf_op jit(solution)/shard_map/ppermute | solution.py:527
  111.5 2.5 %collective-permute-start.23 = (bf16[7,16,384]{2,1,0:T(8,128)(2,1)}, bf16[7,16,384]{2,1,0:T(8,128)(2,1)S(1)}, u32[]{:S(2)}, u32[]{:S(2)}) collective-permute-start(bf16[7,16,384]{2,1,0:T(8,128)(2,1)} %get-tuple-element.96), channel_id=1, source_target_pairs={{0,16},{2,18},{4,20},{6,22},{8,24},{10,26},{12,28},{14,30},{16,0},... | collective-permute-start | bytes 258056 | tf_op jit(solution)/shard_map/ppermute | solution.py:527
  114.2 2.7 %collective-permute-start.25 = (bf16[7,16,384]{2,1,0:T(8,128)(2,1)}, bf16[7,16,384]{2,1,0:T(8,128)(2,1)S(1)}, u32[]{:S(2)}, u32[]{:S(2)}) collective-permute-start(bf16[7,16,384]{2,1,0:T(8,128)(2,1)} %get-tuple-element.98), channel_id=1, source_target_pairs={{0,20},{2,22},{4,16},{6,18},{8,28},{10,30},{12,24},{14,26},{16,4},... | collective-permute-start | bytes 258056 | tf_op jit(solution)/shard_map/ppermute | solution.py:527
  117.0 2.2 %collective-permute-start.26 = (bf16[7,16,384]{2,1,0:T(8,128)(2,1)}, bf16[7,16,384]{2,1,0:T(8,128)(2,1)S(1)}, u32[]{:S(2)}, u32[]{:S(2)}) collective-permute-start(bf16[7,16,384]{2,1,0:T(8,128)(2,1)} %get-tuple-element.99), channel_id=1, source_target_pairs={{0,22},{2,20},{4,18},{6,16},{8,30},{10,28},{12,26},{14,24},{16,6},... | collective-permute-start | bytes 258056 | tf_op jit(solution)/shard_map/ppermute | solution.py:527
  121.0 6.7 %collective-permute-done.23.refs_8_ = bf16[7,16,384]{2,1,0:T(8,128)(2,1)S(1)} collective-permute-done((bf16[7,16,384]{2,1,0:T(8,128)(2,1)}, bf16[7,16,384]{2,1,0:T(8,128)(2,1)S(1)}, u32[]{:S(2)}, u32[]{:S(2)}) %collective-permute-start.23) | collective-permute-done | bytes 86048 | tf_op jit(solution)/shard_map/ppermute | solution.py:527
  129.7 2.7 %collective-permute-start.29 = (bf16[7,16,384]{2,1,0:T(8,128)(2,1)}, bf16[7,16,384]{2,1,0:T(8,128)(2,1)S(1)}, u32[]{:S(2)}, u32[]{:S(2)}) collective-permute-start(bf16[7,16,384]{2,1,0:T(8,128)(2,1)} %get-tuple-element.102), channel_id=1, source_target_pairs={{0,28},{2,30},{4,24},{6,26},{8,20},{10,22},{12,16},{14,18},{16,12}... | collective-permute-start | bytes 258056 | tf_op jit(solution)/shard_map/ppermute | solution.py:527
  132.3 2.8 %collective-permute-start.30 = (bf16[7,16,384]{2,1,0:T(8,128)(2,1)}, bf16[7,16,384]{2,1,0:T(8,128)(2,1)S(1)}, u32[]{:S(2)}, u32[]{:S(2)}) collective-permute-start(bf16[7,16,384]{2,1,0:T(8,128)(2,1)} %get-tuple-element.103), channel_id=1, source_target_pairs={{0,30},{2,28},{4,26},{6,24},{8,22},{10,20},{12,18},{14,16},{16,14}... | collective-permute-start | bytes 258056 | tf_op jit(solution)/shard_map/ppermute | solution.py:527
  135.2 2.2 %collective-permute-done.29.refs_14_ = bf16[7,16,384]{2,1,0:T(8,128)(2,1)S(1)} collective-permute-done((bf16[7,16,384]{2,1,0:T(8,128)(2,1)}, bf16[7,16,384]{2,1,0:T(8,128)(2,1)S(1)}, u32[]{:S(2)}, u32[]{:S(2)}) %collective-permute-start.29) | collective-permute-done | bytes 86048 | tf_op jit(solution)/shard_map/ppermute | solution.py:527
  137.4 3.3 %collective-permute-done.30.refs_15_ = bf16[7,16,384]{2,1,0:T(8,128)(2,1)S(1)} collective-permute-done((bf16[7,16,384]{2,1,0:T(8,128)(2,1)}, bf16[7,16,384]{2,1,0:T(8,128)(2,1)S(1)}, u32[]{:S(2)}, u32[]{:S(2)}) %collective-permute-start.30) | collective-permute-done | bytes 86048 | tf_op jit(solution)/shard_map/ppermute | solution.py:527
  141.4 2.2 %totals.1 = bf16[16,2,16,384]{3,2,1,0:T(8,128)(2,1)} custom-call(s32[5]{0:T(128)S(1)} %stack.68.at_ref, bf16[7,16,384]{2,1,0:T(8,128)(2,1)} %get-tuple-element.88.refs_0_, bf16[7,16,384]{2,1,0:T(8,128)(2,1)} %copy-done.11, bf16[7,16,384]{2,1,0:T(8,128)(2,1)} %copy-done.12, bf16[7,16,384]{2,1,0:T(8,128)(2,1)} %copy-done.13, bf16[7,16,384]{2,1,0:T(8,128)(2,1)} %copy-done.14, ...), custom_call_target="tpu_custom_call" | custom-call | flops 400000000 | bytes 2000000 | tf_op jit(solution)/shard_map/totals/pallas_call | solution.py:469
  143.6 18.6 %all_to_all.15.x_ref = bf16[16,2,16,384]{3,2,1,0:T(8,128)(2,1)S(1)} all-to-all(bf16[16,2,16,384]{3,2,1,0:T(8,128)(2,1)} %totals.1), channel_id=1, replica_groups=mesh['seq'=16,'rep'=2] {'seq'}, dimensions={0} | all-to-all | bytes 786432 | tf_op jit(solution)/shard_map/all_to_all | solution.py:566
  162.2 3.8 %all-to-all-start.1 = ((bf16[16,6,16,384]{3,2,1,0:T(8,128)(2,1)}), bf16[16,6,16,384]{3,2,1,0:T(8,128)(2,1)S(1)}, u32[]{:S(2)}, u32[]{:S(2)}) async-start(bf16[16,6,16,384]{3,2,1,0:T(8,128)(2,1)} %get-tuple-element.61), calls=%async_computation.1 | async-start | bytes 2359296 | tf_op jit(solution)/shard_map/all_to_all | solution.py:566
  166.0 5.5 %inverse_apart.1 = bf16[3,180,2,768]{3,2,1,0:T(2,128)(2,1)} custom-call(s32[5]{0:T(128)S(1)} %stack.68.at_ref, bf16[3,180,2,768]{3,2,1,0:T(2,128)(2,1)} %bitcast.49, bf16[360,256]{1,0:T(8,128)(2,1)S(1)} %copy-done.2, bf16[1,7,16,384]{3,2,1,0:T(8,128)(2,1)} %bitcast.52, bf16[1,7,16,384]{3,2,1,0:T(8,128)(2,1)} %bitcast.53, bf16[1,7,16,384]{3,2,1,0:T(8,128)(2,1)} %bitcast.54, ...), custom_call_target="tpu_custom_call" | custom-call | flops 800000000 | bytes 4000000 | tf_op jit(solution)/shard_map/inverse_apart/pallas_call | solution.py:221
  173.4 2.2 %unpack.1 = (f32[2,8,96,96]{3,2,1,0:T(8,128)}, f32[2,768]{1,0:T(2,128)}, f32[2,8,96,96]{3,2,1,0:T(8,128)}, f32[2,768]{1,0:T(2,128)}) custom-call(s32[5]{0:T(128)S(1)} %stack.68.at_ref, bf16[16,2,16,384]{3,2,1,0:T(8,128)(2,1)S(1)} %all_to_all.15.x_ref, bf16[16,2,16,384]{3,2,1,0:T(8,128)(2,1)S(1)} %collective-permute-done.31.y_ref), custom_call_target="tpu_custom_call" | custom-call | flops 400000000 | bytes 2000000 | tf_op jit(solution)/shard_map/unpack/pallas_call | solution.py:503
  175.6 16.2 %all-to-all-done.1 = bf16[16,6,16,384]{3,2,1,0:T(8,128)(2,1)S(1)} async-done(((bf16[16,6,16,384]{3,2,1,0:T(8,128)(2,1)}), bf16[16,6,16,384]{3,2,1,0:T(8,128)(2,1)S(1)}, u32[]{:S(2)}, u32[]{:S(2)}) %all-to-all-start.1) | async-done | bytes 1179680 | tf_op jit(solution)/shard_map/all_to_all | solution.py:566
  192.8 4.6 %inverse.1 = bf16[3,180,2,768]{3,2,1,0:T(2,128)(2,1)} custom-call(bf16[3,180,2,768]{3,2,1,0:T(2,128)(2,1)} %bitcast.45, bf16[360,256]{1,0:T(8,128)(2,1)S(1)} %copy-done.1, bf16[2,1,8,2,3,16,384]{6,5,4,3,2,1,0:T(8,128)(2,1)} %bitcast.47), custom_call_target="tpu_custom_call" | custom-call | flops 800000000 | bytes 4000000 | tf_op jit(solution)/shard_map/inverse/pallas_call | solution.py:188
  (132 shorter events, 27.7 us)
Async XLA Ops:
  5.3 66.8 %all-to-all-start = ((bf16[16,6,16,384]{3,2,1,0:T(8,128)(2,1)}), bf16[16,6,16,384]{3,2,1,0:T(8,128)(2,1)S(1)}, u32[]{:S(2)}, u32[]{:S(2)}) async-start(bf16[16,6,16,384]{3,2,1,0:T(8,128)(2,1)} %bitcast.46), calls=%async_computation | async-start | bytes 2359296 | tf_op jit(solution)/shard_map/all_to_all | solution.py:566
  18.4 10.5 %collective-permute-start = (bf16[6,16,384]{2,1,0:T(8,128)(2,1)}, bf16[6,16,384]{2,1,0:T(8,128)(2,1)S(1)}, u32[]{:S(2)}, u32[]{:S(2)}) collective-permute-start(bf16[6,16,384]{2,1,0:T(8,128)(2,1)} %bitcast.96), channel_id=1, source_target_pairs={{0,2},{2,0},{4,6},{6,4},{8,10},{10,8},{12,14},{14,12},{16,18},{18,... | collective-permute-start | bytes 221192 | tf_op jit(solution)/shard_map/ppermute | solution.py:527
  20.4 10.9 %collective-permute-start.1 = (bf16[6,16,384]{2,1,0:T(8,128)(2,1)}, bf16[6,16,384]{2,1,0:T(8,128)(2,1)S(1)}, u32[]{:S(2)}, u32[]{:S(2)}) collective-permute-start(bf16[6,16,384]{2,1,0:T(8,128)(2,1)} %bitcast.95), channel_id=1, source_target_pairs={{0,4},{2,6},{4,0},{6,2},{8,12},{10,14},{12,8},{14,10},{16,20},{18,... | collective-permute-start | bytes 221192 | tf_op jit(solution)/shard_map/ppermute | solution.py:527
  21.8 33.1 %collective-permute-start.10 = (bf16[6,16,384]{2,1,0:T(8,128)(2,1)}, bf16[6,16,384]{2,1,0:T(8,128)(2,1)S(1)}, u32[]{:S(2)}, u32[]{:S(2)}) collective-permute-start(bf16[6,16,384]{2,1,0:T(8,128)(2,1)} %bitcast.94), channel_id=1, source_target_pairs={{0,22},{2,20},{4,18},{6,16},{8,30},{10,28},{12,26},{14,24},{16,6},... | collective-permute-start | bytes 221192 | tf_op jit(solution)/shard_map/ppermute | solution.py:527
  24.2 31.0 %collective-permute-start.11 = (bf16[6,16,384]{2,1,0:T(8,128)(2,1)}, bf16[6,16,384]{2,1,0:T(8,128)(2,1)S(1)}, u32[]{:S(2)}, u32[]{:S(2)}) collective-permute-start(bf16[6,16,384]{2,1,0:T(8,128)(2,1)} %bitcast.93), channel_id=1, source_target_pairs={{0,24},{2,26},{4,28},{6,30},{8,16},{10,18},{12,20},{14,22},{16,8},... | collective-permute-start | bytes 221192 | tf_op jit(solution)/shard_map/ppermute | solution.py:527
  25.7 29.5 %collective-permute-start.12 = (bf16[6,16,384]{2,1,0:T(8,128)(2,1)}, bf16[6,16,384]{2,1,0:T(8,128)(2,1)S(1)}, u32[]{:S(2)}, u32[]{:S(2)}) collective-permute-start(bf16[6,16,384]{2,1,0:T(8,128)(2,1)} %bitcast.92), channel_id=1, source_target_pairs={{0,26},{2,24},{4,30},{6,28},{8,18},{10,16},{12,22},{14,20},{16,10}... | collective-permute-start | bytes 221192 | tf_op jit(solution)/shard_map/ppermute | solution.py:527
  28.9 34.3 %collective-permute-start.13 = (bf16[6,16,384]{2,1,0:T(8,128)(2,1)}, bf16[6,16,384]{2,1,0:T(8,128)(2,1)S(1)}, u32[]{:S(2)}, u32[]{:S(2)}) collective-permute-start(bf16[6,16,384]{2,1,0:T(8,128)(2,1)} %bitcast.91), channel_id=1, source_target_pairs={{0,28},{2,30},{4,24},{6,26},{8,20},{10,22},{12,16},{14,18},{16,12}... | collective-permute-start | bytes 221192 | tf_op jit(solution)/shard_map/ppermute | solution.py:527
  31.3 33.3 %collective-permute-start.14 = (bf16[6,16,384]{2,1,0:T(8,128)(2,1)}, bf16[6,16,384]{2,1,0:T(8,128)(2,1)S(1)}, u32[]{:S(2)}, u32[]{:S(2)}) collective-permute-start(bf16[6,16,384]{2,1,0:T(8,128)(2,1)} %bitcast.90), channel_id=1, source_target_pairs={{0,30},{2,28},{4,26},{6,24},{8,22},{10,20},{12,18},{14,16},{16,14}... | collective-permute-start | bytes 221192 | tf_op jit(solution)/shard_map/ppermute | solution.py:527
  55.0 11.6 %collective-permute-start.2 = (bf16[6,16,384]{2,1,0:T(8,128)(2,1)}, bf16[6,16,384]{2,1,0:T(8,128)(2,1)S(1)}, u32[]{:S(2)}, u32[]{:S(2)}) collective-permute-start(bf16[6,16,384]{2,1,0:T(8,128)(2,1)} %bitcast.89), channel_id=1, source_target_pairs={{0,6},{2,4},{4,2},{6,0},{8,14},{10,12},{12,10},{14,8},{16,22},{18,... | collective-permute-start | bytes 221192 | tf_op jit(solution)/shard_map/ppermute | solution.py:527
  55.2 11.5 %collective-permute-start.3 = (bf16[6,16,384]{2,1,0:T(8,128)(2,1)}, bf16[6,16,384]{2,1,0:T(8,128)(2,1)S(1)}, u32[]{:S(2)}, u32[]{:S(2)}) collective-permute-start(bf16[6,16,384]{2,1,0:T(8,128)(2,1)} %bitcast.88), channel_id=1, source_target_pairs={{0,8},{2,10},{4,12},{6,14},{8,0},{10,2},{12,4},{14,6},{16,24},{18,... | collective-permute-start | bytes 221192 | tf_op jit(solution)/shard_map/ppermute | solution.py:527
  55.8 14.3 %collective-permute-start.4 = (bf16[6,16,384]{2,1,0:T(8,128)(2,1)}, bf16[6,16,384]{2,1,0:T(8,128)(2,1)S(1)}, u32[]{:S(2)}, u32[]{:S(2)}) collective-permute-start(bf16[6,16,384]{2,1,0:T(8,128)(2,1)} %bitcast.87), channel_id=1, source_target_pairs={{0,10},{2,8},{4,14},{6,12},{8,2},{10,0},{12,6},{14,4},{16,26},{18,... | collective-permute-start | bytes 221192 | tf_op jit(solution)/shard_map/ppermute | solution.py:527
  63.3 20.3 %collective-permute-start.5 = (bf16[6,16,384]{2,1,0:T(8,128)(2,1)}, bf16[6,16,384]{2,1,0:T(8,128)(2,1)S(1)}, u32[]{:S(2)}, u32[]{:S(2)}) collective-permute-start(bf16[6,16,384]{2,1,0:T(8,128)(2,1)} %bitcast.15), channel_id=1, source_target_pairs={{0,12},{2,14},{4,8},{6,10},{8,4},{10,6},{12,0},{14,2},{16,28},{18,... | collective-permute-start | bytes 221192 | tf_op jit(solution)/shard_map/ppermute | solution.py:527
  64.6 18.9 %collective-permute-start.6 = (bf16[6,16,384]{2,1,0:T(8,128)(2,1)}, bf16[6,16,384]{2,1,0:T(8,128)(2,1)S(1)}, u32[]{:S(2)}, u32[]{:S(2)}) collective-permute-start(bf16[6,16,384]{2,1,0:T(8,128)(2,1)} %bitcast.16), channel_id=1, source_target_pairs={{0,14},{2,12},{4,10},{6,8},{8,6},{10,4},{12,2},{14,0},{16,30},{18,... | collective-permute-start | bytes 221192 | tf_op jit(solution)/shard_map/ppermute | solution.py:527
  66.6 17.0 %collective-permute-start.7 = (bf16[6,16,384]{2,1,0:T(8,128)(2,1)}, bf16[6,16,384]{2,1,0:T(8,128)(2,1)S(1)}, u32[]{:S(2)}, u32[]{:S(2)}) collective-permute-start(bf16[6,16,384]{2,1,0:T(8,128)(2,1)} %bitcast.17), channel_id=1, source_target_pairs={{0,16},{2,18},{4,20},{6,22},{8,24},{10,26},{12,28},{14,30},{16,0},... | collective-permute-start | bytes 221192 | tf_op jit(solution)/shard_map/ppermute | solution.py:527
  66.7 16.9 %collective-permute-start.8 = (bf16[6,16,384]{2,1,0:T(8,128)(2,1)}, bf16[6,16,384]{2,1,0:T(8,128)(2,1)S(1)}, u32[]{:S(2)}, u32[]{:S(2)}) collective-permute-start(bf16[6,16,384]{2,1,0:T(8,128)(2,1)} %bitcast.18), channel_id=1, source_target_pairs={{0,18},{2,16},{4,22},{6,20},{8,26},{10,24},{12,30},{14,28},{16,2},... | collective-permute-start | bytes 221192 | tf_op jit(solution)/shard_map/ppermute | solution.py:527
  70.7 12.9 %collective-permute-start.9 = (bf16[6,16,384]{2,1,0:T(8,128)(2,1)}, bf16[6,16,384]{2,1,0:T(8,128)(2,1)S(1)}, u32[]{:S(2)}, u32[]{:S(2)}) collective-permute-start(bf16[6,16,384]{2,1,0:T(8,128)(2,1)} %bitcast.19), channel_id=1, source_target_pairs={{0,20},{2,22},{4,16},{6,18},{8,28},{10,30},{12,24},{14,26},{16,4},... | collective-permute-start | bytes 221192 | tf_op jit(solution)/shard_map/ppermute | solution.py:527
  101.7 5.8 %collective-permute-start.16 = (bf16[7,16,384]{2,1,0:T(8,128)(2,1)}, bf16[7,16,384]{2,1,0:T(8,128)(2,1)S(1)}, u32[]{:S(2)}, u32[]{:S(2)}) collective-permute-start(bf16[7,16,384]{2,1,0:T(8,128)(2,1)} %get-tuple-element.89), channel_id=1, source_target_pairs={{0,2},{2,0},{4,6},{6,4},{8,10},{10,8},{12,14},{14,12},{16,18},{18,... | collective-permute-start | bytes 258056 | tf_op jit(solution)/shard_map/ppermute | solution.py:527
  102.5 6.9 %collective-permute-start.17 = (bf16[7,16,384]{2,1,0:T(8,128)(2,1)}, bf16[7,16,384]{2,1,0:T(8,128)(2,1)S(1)}, u32[]{:S(2)}, u32[]{:S(2)}) collective-permute-start(bf16[7,16,384]{2,1,0:T(8,128)(2,1)} %get-tuple-element.90), channel_id=1, source_target_pairs={{0,4},{2,6},{4,0},{6,2},{8,12},{10,14},{12,8},{14,10},{16,20},{18,... | collective-permute-start | bytes 258056 | tf_op jit(solution)/shard_map/ppermute | solution.py:527
  103.0 8.4 %collective-permute-start.18 = (bf16[7,16,384]{2,1,0:T(8,128)(2,1)}, bf16[7,16,384]{2,1,0:T(8,128)(2,1)S(1)}, u32[]{:S(2)}, u32[]{:S(2)}) collective-permute-start(bf16[7,16,384]{2,1,0:T(8,128)(2,1)} %get-tuple-element.91), channel_id=1, source_target_pairs={{0,6},{2,4},{4,2},{6,0},{8,14},{10,12},{12,10},{14,8},{16,22},{18,... | collective-permute-start | bytes 258056 | tf_op jit(solution)/shard_map/ppermute | solution.py:527
  105.2 8.7 %collective-permute-start.19 = (bf16[7,16,384]{2,1,0:T(8,128)(2,1)}, bf16[7,16,384]{2,1,0:T(8,128)(2,1)S(1)}, u32[]{:S(2)}, u32[]{:S(2)}) collective-permute-start(bf16[7,16,384]{2,1,0:T(8,128)(2,1)} %get-tuple-element.92), channel_id=1, source_target_pairs={{0,8},{2,10},{4,12},{6,14},{8,0},{10,2},{12,4},{14,6},{16,24},{18,... | collective-permute-start | bytes 258056 | tf_op jit(solution)/shard_map/ppermute | solution.py:527
  106.6 7.6 %collective-permute-start.20 = (bf16[7,16,384]{2,1,0:T(8,128)(2,1)}, bf16[7,16,384]{2,1,0:T(8,128)(2,1)S(1)}, u32[]{:S(2)}, u32[]{:S(2)}) collective-permute-start(bf16[7,16,384]{2,1,0:T(8,128)(2,1)} %get-tuple-element.93), channel_id=1, source_target_pairs={{0,10},{2,8},{4,14},{6,12},{8,2},{10,0},{12,6},{14,4},{16,26},{18,... | collective-permute-start | bytes 258056 | tf_op jit(solution)/shard_map/ppermute | solution.py:527
  107.5 9.5 %collective-permute-start.21 = (bf16[7,16,384]{2,1,0:T(8,128)(2,1)}, bf16[7,16,384]{2,1,0:T(8,128)(2,1)S(1)}, u32[]{:S(2)}, u32[]{:S(2)}) collective-permute-start(bf16[7,16,384]{2,1,0:T(8,128)(2,1)} %get-tuple-element.94), channel_id=1, source_target_pairs={{0,12},{2,14},{4,8},{6,10},{8,4},{10,6},{12,0},{14,2},{16,28},{18,... | collective-permute-start | bytes 258056 | tf_op jit(solution)/shard_map/ppermute | solution.py:527
  109.4 9.7 %collective-permute-start.22 = (bf16[7,16,384]{2,1,0:T(8,128)(2,1)}, bf16[7,16,384]{2,1,0:T(8,128)(2,1)S(1)}, u32[]{:S(2)}, u32[]{:S(2)}) collective-permute-start(bf16[7,16,384]{2,1,0:T(8,128)(2,1)} %get-tuple-element.95), channel_id=1, source_target_pairs={{0,14},{2,12},{4,10},{6,8},{8,6},{10,4},{12,2},{14,0},{16,30},{18,... | collective-permute-start | bytes 258056 | tf_op jit(solution)/shard_map/ppermute | solution.py:527
  111.5 16.2 %collective-permute-start.23 = (bf16[7,16,384]{2,1,0:T(8,128)(2,1)}, bf16[7,16,384]{2,1,0:T(8,128)(2,1)S(1)}, u32[]{:S(2)}, u32[]{:S(2)}) collective-permute-start(bf16[7,16,384]{2,1,0:T(8,128)(2,1)} %get-tuple-element.96), channel_id=1, source_target_pairs={{0,16},{2,18},{4,20},{6,22},{8,24},{10,26},{12,28},{14,30},{16,0},... | collective-permute-start | bytes 258056 | tf_op jit(solution)/shard_map/ppermute | solution.py:527
  113.9 15.7 %collective-permute-start.24 = (bf16[7,16,384]{2,1,0:T(8,128)(2,1)}, bf16[7,16,384]{2,1,0:T(8,128)(2,1)S(1)}, u32[]{:S(2)}, u32[]{:S(2)}) collective-permute-start(bf16[7,16,384]{2,1,0:T(8,128)(2,1)} %get-tuple-element.97), channel_id=1, source_target_pairs={{0,18},{2,16},{4,22},{6,20},{8,26},{10,24},{12,30},{14,28},{16,2},... | collective-permute-start | bytes 258056 | tf_op jit(solution)/shard_map/ppermute | solution.py:527
  114.2 18.1 %collective-permute-start.25 = (bf16[7,16,384]{2,1,0:T(8,128)(2,1)}, bf16[7,16,384]{2,1,0:T(8,128)(2,1)S(1)}, u32[]{:S(2)}, u32[]{:S(2)}) collective-permute-start(bf16[7,16,384]{2,1,0:T(8,128)(2,1)} %get-tuple-element.98), channel_id=1, source_target_pairs={{0,20},{2,22},{4,16},{6,18},{8,28},{10,30},{12,24},{14,26},{16,4},... | collective-permute-start | bytes 258056 | tf_op jit(solution)/shard_map/ppermute | solution.py:527
  117.0 18.2 %collective-permute-start.26 = (bf16[7,16,384]{2,1,0:T(8,128)(2,1)}, bf16[7,16,384]{2,1,0:T(8,128)(2,1)S(1)}, u32[]{:S(2)}, u32[]{:S(2)}) collective-permute-start(bf16[7,16,384]{2,1,0:T(8,128)(2,1)} %get-tuple-element.99), channel_id=1, source_target_pairs={{0,22},{2,20},{4,18},{6,16},{8,30},{10,28},{12,26},{14,24},{16,6},... | collective-permute-start | bytes 258056 | tf_op jit(solution)/shard_map/ppermute | solution.py:527
  119.1 16.0 %collective-permute-start.27 = (bf16[7,16,384]{2,1,0:T(8,128)(2,1)}, bf16[7,16,384]{2,1,0:T(8,128)(2,1)S(1)}, u32[]{:S(2)}, u32[]{:S(2)}) collective-permute-start(bf16[7,16,384]{2,1,0:T(8,128)(2,1)} %get-tuple-element.100), channel_id=1, source_target_pairs={{0,24},{2,26},{4,28},{6,30},{8,16},{10,18},{12,20},{14,22},{16,8},... | collective-permute-start | bytes 258056 | tf_op jit(solution)/shard_map/ppermute | solution.py:527
  127.7 7.5 %collective-permute-start.28 = (bf16[7,16,384]{2,1,0:T(8,128)(2,1)}, bf16[7,16,384]{2,1,0:T(8,128)(2,1)S(1)}, u32[]{:S(2)}, u32[]{:S(2)}) collective-permute-start(bf16[7,16,384]{2,1,0:T(8,128)(2,1)} %get-tuple-element.101), channel_id=1, source_target_pairs={{0,26},{2,24},{4,30},{6,28},{8,18},{10,16},{12,22},{14,20},{16,10}... | collective-permute-start | bytes 258056 | tf_op jit(solution)/shard_map/ppermute | solution.py:527
  129.7 7.7 %collective-permute-start.29 = (bf16[7,16,384]{2,1,0:T(8,128)(2,1)}, bf16[7,16,384]{2,1,0:T(8,128)(2,1)S(1)}, u32[]{:S(2)}, u32[]{:S(2)}) collective-permute-start(bf16[7,16,384]{2,1,0:T(8,128)(2,1)} %get-tuple-element.102), channel_id=1, source_target_pairs={{0,28},{2,30},{4,24},{6,26},{8,20},{10,22},{12,16},{14,18},{16,12}... | collective-permute-start | bytes 258056 | tf_op jit(solution)/shard_map/ppermute | solution.py:527
  132.3 8.4 %collective-permute-start.30 = (bf16[7,16,384]{2,1,0:T(8,128)(2,1)}, bf16[7,16,384]{2,1,0:T(8,128)(2,1)S(1)}, u32[]{:S(2)}, u32[]{:S(2)}) collective-permute-start(bf16[7,16,384]{2,1,0:T(8,128)(2,1)} %get-tuple-element.103), channel_id=1, source_target_pairs={{0,30},{2,28},{4,26},{6,24},{8,22},{10,20},{12,18},{14,16},{16,14}... | collective-permute-start | bytes 258056 | tf_op jit(solution)/shard_map/ppermute | solution.py:527
  162.2 29.6 %all-to-all-start.1 = ((bf16[16,6,16,384]{3,2,1,0:T(8,128)(2,1)}), bf16[16,6,16,384]{3,2,1,0:T(8,128)(2,1)S(1)}, u32[]{:S(2)}, u32[]{:S(2)}) async-start(bf16[16,6,16,384]{3,2,1,0:T(8,128)(2,1)} %get-tuple-element.61), calls=%async_computation.1 | async-start | bytes 2359296 | tf_op jit(solution)/shard_map/all_to_all | solution.py:566
  (44 other events, 563.3 us)

commit v3 on v2

--- a/solution.py
+++ b/solution.py
@@ -120,7 +120,7 @@
         compiler_params=params(16),
         cost_estimate=cost(3),
         name="columns",
-    )(*far(x), table)
+    )(*far(x, table))
 
 
 def columns_apart_kernel(at_ref, x_ref, t_ref, *refs):
@@ -155,7 +155,7 @@
         compiler_params=params(16),
         cost_estimate=cost(3),
         name="columns_apart",
-    )(at, *far(x), table)
+    )(at, *far(x, table))
 
 
 def add_modes(o_ref, x_ref, t_ref, z):
@@ -194,7 +194,7 @@
         compiler_params=params(16),
         cost_estimate=cost(4),
         name="inverse",
-    )(*far(x), table, *far(z))
+    )(*far(x, table, z))
 
 
 def inverse_apart_kernel(at_ref, x_ref, t_ref, *refs):
@@ -232,7 +232,7 @@
         compiler_params=params(16),
         cost_estimate=cost(4),
         name="inverse_apart",
-    )(at, *far(x), table, *[y for y in far(*slabs) for _ in range(local)])
+    )(at, *far(x, table), *[y for y in far(*slabs) for _ in range(local)])
 
 
 def transposed(out_ref, blocks):
@@ -356,7 +356,7 @@
         compiler_params=params(40),
         cost_estimate=cost(9),
         name="forward",
-    )(at, *far(v, m, n, wi, wo), in_bias, out_bias)
+    )(at, *far(v, m, n, wi, wo, in_bias, out_bias))
 
 
 PACK = 256
@@ -432,61 +432,70 @@
         back = back.reshape(blocks, rows // CK, CK, HALF)
         for r in range(blocks):
             outs[r][s * rows // CK : (s + 1) * rows // CK] = back[r]
-    for r in range(blocks):
-        to = r ^ at_ref[0]
-        outs[r][local * rows // CK] = (kept_ref[to] + other_ref[to]).astype(BF16)
+    tiles = local * rows // CK
+    for r in range(blocks // HALVES):
+        to = (r ^ at_ref[0]) % (blocks // HALVES)
+        outs[r][tiles:] = (kept_ref[to] + other_ref[to]).astype(BF16)
 
 
 def rows_back(at, n, grad, kept, other):
     blocks, rows, _ = n.shape
-    local = grad.shape[0]
+    tiles = grad.shape[0] * rows // CK
+    counts = [tiles + kept.shape[1]] * (blocks // HALVES) + [tiles] * (blocks // HALVES)
     return pl.pallas_call(
         rows_back_kernel,
         in_specs=[pl.BlockSpec(memory_space=pltpu.SMEM)] + [pl.BlockSpec()] * 4,
-        out_shape=[pltpu.HBM((local * rows // CK + 1, CK, HALF), BF16)] * blocks,
+        out_shape=[pltpu.HBM((count, CK, HALF), BF16) for count in counts],
         compiler_params=params(24),
         cost_estimate=cost(4),
         name="rows_back",
     )(at, *far(n, grad, kept, other))
 
 
-def totals_kernel(at_ref, *refs):
+def totals_kernel(*refs):
     *shares, o_ref = refs
-    count = len(shares) // HALVES
-    for a in range(HALVES):
-        total = shares[a * count][0].astype(F32)
-        for x in shares[a * count + 1 : (a + 1) * count]:
-            total = total + x[0].astype(F32)
-        total = total.astype(BF16)
-        for t in range(len(shares)):
-            o_ref[t, a ^ at_ref[1]] = total
-
-
-def totals(at, slabs):
-    last = slabs[0].shape[0] - 1
-    share = pl.BlockSpec((1, CK, HALF), lambda i, at: (last, 0, 0))
-    shape = (len(slabs), HALVES, CK, HALF)
-    return pl.pallas_call(
-        totals_kernel,
-        grid_spec=pltpu.PrefetchScalarGridSpec(
-            num_scalar_prefetch=1,
-            grid=(1,),
-            in_specs=[share] * len(slabs),
-            out_specs=pl.BlockSpec(shape, lambda i, at: (0, 0, 0, 0)),
-        ),
-        out_shape=pltpu.HBM(shape, BF16),
+    total = shares[0][...].astype(F32)
+    for x in shares[1:]:
+        total = total + x[...].astype(F32)
+    total = total.astype(BF16)
+    for t in range(o_ref.shape[0]):
+        o_ref[t] = total
+
+
+def totals(slabs, tiles):
+    extra = slabs[0].shape[0] - tiles
+    count = sum(x.shape[0] > tiles for x in slabs)
+    shares = [
+        pl.BlockSpec((1, CK, HALF), lambda i, t=t: (tiles + t, 0, 0)) for t in range(extra)
+    ]
+    body = totals_kernel
+    if extra > 1:
+
+        def body(*refs):
+            *pieces, o_ref = refs
+            for t in range(extra):
+                totals_kernel(*pieces[t::extra], o_ref.at[:, t : t + 1])
+
+    return pl.pallas_call(
+        body,
+        grid=(1,),
+        in_specs=shares * count,
+        out_specs=pl.BlockSpec((len(slabs), extra, CK, HALF), lambda i: (0, 0, 0, 0)),
+        out_shape=pltpu.HBM((len(slabs), extra, CK, HALF), BF16),
         compiler_params=params(8),
         cost_estimate=cost(2),
         name="totals",
-    )(at, *far(*slabs))
+    )(*[y for y in far(*slabs[:count]) for _ in range(extra)])
 
 
 def unpack_kernel(scale, at_ref, x_ref, y_ref, iw_ref, ib_ref, ow_ref, ob_ref, pack_ref):
     per = HALF // BLOCK
     for i, ref in enumerate((x_ref, y_ref)):
-        for place in range(ref.shape[0]):
-            for half in range(HALVES):
-                pack_ref[i ^ at_ref[4], half, place] = ref[place, half].astype(F32) * scale
+        count = ref.shape[0] // HALVES
+        for half in range(HALVES):
+            for place in range(count):
+                block = ref[half * count + place].astype(F32) * scale
+                pack_ref[i ^ at_ref[4], half, place] = block
     for mat, w_ref, b_ref in ((0, iw_ref, ib_ref), (1, ow_ref, ob_ref)):
         for half in range(HALVES):
             part = pack_ref[mat, half].reshape(PACK, HALF)
@@ -505,7 +514,7 @@
         in_specs=[pl.BlockSpec(memory_space=pltpu.SMEM)]
         + [pl.BlockSpec(memory_space=pltpu.VMEM)] * 2,
         out_shape=[weight, bias, weight, bias],
-        scratch_shapes=[pltpu.VMEM((2, HALVES, x.shape[0], CK, HALF), F32)],
+        scratch_shapes=[pltpu.VMEM((2, HALVES, x.shape[0] // HALVES, *x.shape[1:]), F32)],
         compiler_params=params(16),
         cost_estimate=cost(2),
         name="unpack",
@@ -525,14 +534,6 @@
 
 def swap(x, axis, size, bit):
     return lax.ppermute(x, axis, [(i, i ^ bit) for i in range(size)])
-
-
-def far_first(seq):
-    quarter = max(seq // 4, 1)
-    classes = [2, 3, 1, 0] if seq >= 4 else [1, 0]
-    spread = [[c * quarter + i for i in range(quarter)] for c in classes]
-    far = [r for pair in zip(spread[0], spread[1]) for r in pair]
-    return [r for r in far + spread[2] + spread[3] if r]
 
 
 def bits_below(size):
@@ -567,7 +568,7 @@
 
     def apart(slabs):
         out = {0: slabs[0]}
-        for r in far_first(seq):
+        for r in range(1, seq):
             out[r] = swap(slabs[r], "seq", seq, r)
         return [out[r] for r in range(seq)]
 
@@ -600,20 +601,24 @@
         kept = lax.dynamic_slice_in_dim(piece, mine * count, count, 0)
         sent = lax.dynamic_slice_in_dim(piece, (1 - mine) * count, count, 0)
         other = swap(sent, "rep", rep, bit)
-    part = kept.shape[0] // seq
+    part = kept.shape[0] * HALVES // seq
+    whole_tiles = part % CK == 0
 
     def by_place(x):
-        x = x.reshape(seq, part, HALF)
-        return jnp.pad(x, ((0, 0), (0, CK - part), (0, 0))) if part < CK else x
+        x = x.reshape(seq // HALVES, part, HALF)
+        x = jnp.pad(x, ((0, 0), (0, -part % CK), (0, 0)))
+        return x.reshape(seq // HALVES, -1, CK, HALF)
 
     grad = apart(rows_back(at, base_x, grad, by_place(kept), by_place(other)))
+    near, back = lax.optimization_barrier((grad[: seq // HALVES], back))
+    grad = near + grad[seq // HALVES :]
+    total = totals(grad, local * rows)
     mixed_out = inverse(
         tokens,
         table(doubled.T),
         back.reshape(HALVES, split, GROUPS, local, rows, CK, HALF),
         dims,
     )
-    total = totals(at, grad)
     gathered = exchange(total)
     slabs = [
         jnp.stack([grad[(a * split + c) * GROUPS + b] for c in range(split)])
@@ -623,10 +628,10 @@
     tokens_grad = inverse_apart(at, cotangent, table(plain.T), slabs, dims)
     gathered, tokens_grad = lax.optimization_barrier((gathered, tokens_grad))
     scale = 1.0 / (samples * rep)
-    if rep == 2 and part == CK:
+    if rep == 2 and whole_tiles:
         gradients = unpack(at, gathered, swap(gathered, "rep", rep, 1), scale)
     else:
-        piece = gathered[:, :, :part].transpose(1, 0, 2, 3).reshape(HALVES, seq * part, HALF)
+        piece = gathered.reshape(seq, -1, HALF)[:, :part].reshape(HALVES, -1, HALF)
         for bit in bits[::-1]:
             other = swap(piece, "rep", rep, bit)
             first = ((core // bit) % 2) == 0

time: 199 us -> 200 us (level)
  blocking collectives: 18.6 us -> 0 us
  starting transfers between devices: 65.7 us -> 79.1 us
  waiting for transfers between devices: 53.4 us -> 62.8 us
  local copies, waits for them, and re-layouts: 6.31 us -> 3.65 us
    all_to_all x1 -> x0, blocking collectives: 18.6 us -> none  [exchange(): lax.all_to_all(x.reshape((seq, -1) + x.shape[-2:]), 'seq', 0, 0, tiled=True)]
    all_to_all x2 -> x3, starting transfers between devices: 12.3 us -> 19.5 us  [exchange(): lax.all_to_all(x.reshape((seq, -1) + x.shape[-2:]), 'seq', 0, 0, tiled=True)]
    all_to_all x2 -> x3, waiting for transfers between devices: 16.2 us -> 22.3 us  [exchange(): lax.all_to_all(x.reshape((seq, -1) + x.shape[-2:]), 'seq', 0, 0, tiled=True)]
    ppermute x32, starting transfers between devices: 53.4 us -> 59.5 us  [swap(): return lax.ppermute(x, axis, [(i, i ^ bit) for i in range(size)])]
    ppermute x32, waiting for transfers between devices: 37.2 us -> 40.5 us  [swap(): return lax.ppermute(x, axis, [(i, i ^ bit) for i in range(size)])]
    unnamed x84 -> x88, local copies, waits for them, and re-layouts: 6.22 us -> 3.56 us
  transfers between devices with their start and end apart: 34 -> 35, of which waited for: 7 -> 15; matrix products, arithmetic and copies ran while one was open for 0% -> 0% of each run, Pallas kernels for 14% -> 17%
where the time goes in v3:
time: 200 us; the launch traced here: 199 us
  starting transfers between devices  79.1 us (40%)
  waiting for transfers between devices  62.8 us (31%)
  Pallas kernels  52 us (26%)
  local copies, waits for them, and re-layouts  3.65 us (2%)
    ppermute x32, starting transfers between devices, swap(): return lax.ppermute(x, axis, [(i, i ^ bit) for i in range(size)])  59.5 us
    ppermute x32, waiting for transfers between devices, swap(): return lax.ppermute(x, axis, [(i, i ^ bit) for i in range(size)])  40.5 us
    all_to_all x3, waiting for transfers between devices, exchange(): lax.all_to_all(x.reshape((seq, -1) + x.shape[-2:]), 'seq', 0, 0, tiled=True)  22.3 us
    all_to_all x3, starting transfers between devices, exchange(): lax.all_to_all(x.reshape((seq, -1) + x.shape[-2:]), 'seq', 0, 0, tiled=True)  19.5 us
    pallas_call x1, Pallas kernels, backward(): pl.pallas_call(backward_kernel, grid_spec=pltpu.PrefetchScalarGridSpec(nu...  10.5 us
    pallas_call x1, Pallas kernels, forward(): pl.pallas_call(forward_kernel, grid_spec=pltpu.PrefetchScalarGridSpec(num...  10.4 us
    pallas_call x1, Pallas kernels, inverse_apart(): pl.pallas_call(inverse_apart_kernel, grid_spec=pltpu.PrefetchScalarGridSp...  5.59 us
    pallas_call x1, Pallas kernels, inverse(): pl.pallas_call(inverse_kernel, grid=(rows,), in_specs=[whole, pl.BlockSpe...  4.65 us
  transfers between devices with their start and end apart: 35, of which 15 were waited for; matrix products, arithmetic and copies ran while one was open for 0% of the time, Pallas kernels for 17%

profile of v3, /device:TPU:0, one launch (start us, length us, event | category | flops | bytes accessed | tf_op | source)
XLA Modules:
  0.0 198.6 jit_solution(384891187008624667)
XLA Ops:
  0.6 3.8 %columns.1 = bf16[2,1,8,2,3,16,384]{6,5,4,3,2,1,0:T(8,128)(2,1)} custom-call(bf16[3,180,2,768]{3,2,1,0:T(2,128)(2,1)} %bitcast.44, bf16[256,360]{1,0:T(8,128)(2,1)} %constant.67.clone.t_ref), custom_call_target="tpu_custom_call" | custom-call | flops 600000000 | bytes 3000000 | tf_op jit(solution)/shard_map/columns/pallas_call | solution.py:111
  4.5 8.5 %all-to-all-start = ((bf16[16,6,16,384]{3,2,1,0:T(8,128)(2,1)}), bf16[16,6,16,384]{3,2,1,0:T(8,128)(2,1)S(1)}, u32[]{:S(2)}, u32[]{:S(2)}) async-start(bf16[16,6,16,384]{3,2,1,0:T(8,128)(2,1)} %bitcast.46), calls=%async_computation | async-start | bytes 2359296 | tf_op jit(solution)/shard_map/all_to_all | solution.py:567
  13.1 4.5 %prepare.1 = (bf16[768,768]{1,0:T(8,128)(2,1)}, bf16[768,768]{1,0:T(8,128)(2,1)}, bf16[16,48,768]{2,1,0:T(8,128)(2,1)}, bf16[768,768]{1,0:T(8,128)(2,1)}, bf16[7...) custom-call(s32[5]{0:T(128)S(1)} %stack.68.at_ref, bf16[16,48,768]{2,1,0:T(8,128)(2,1)S(1)} %copy-done.2, ...), custom_call_target="tpu_custom_call" | custom-call | flops 800000000 | bytes 4000000 | tf_op jit(solution)/shard_map/prepare/pallas_call | solution.py:280
  17.6 22.3 %all-to-all-done.v_ref = bf16[16,6,16,384]{3,2,1,0:T(8,128)(2,1)S(1)} async-done(((bf16[16,6,16,384]{3,2,1,0:T(8,128)(2,1)}), bf16[16,6,16,384]{3,2,1,0:T(8,128)(2,1)S(1)}, u32[]{:S(2)}, u32[]{:S(2)}) %all-to-all-start) | async-done | bytes 1179680 | tf_op jit(solution)/shard_map/all_to_all | solution.py:567
  40.9 10.4 %forward.1 = (bf16[16,6,16,384]{3,2,1,0:T(8,128)(2,1)}, bf16[2,768,384]{2,1,0:T(8,128)(2,1)}, bf16[2,768,384]{2,1,0:T(8,128)(2,1)}, f32[2,384,768]{2,1,0:T(8,128)}) custom-call(s32[5]{0:T(128)S(1)} %stack.68.at_ref, bf16[16,6,16,384]{3,2,1,0:T(8,128)(2,1)} %copy-done.11, bf16[768,768]{1,0:T(8,128)(2,1)} %get-tuple-element.71.m_ref, ...), custom_call_target="tpu_custom_call" | custom-call | flops 1800000000 | bytes 9000000 | tf_op jit(solution)/shard_map/forward/pallas_call | solution.py:342
  51.3 6.2 %all-to-all-start.1 = ((bf16[16,6,16,384]{3,2,1,0:T(8,128)(2,1)}), bf16[16,6,16,384]{3,2,1,0:T(8,128)(2,1)S(1)}, u32[]{:S(2)}, u32[]{:S(2)}) async-start(bf16[16,6,16,384]{3,2,1,0:T(8,128)(2,1)} %get-tuple-element.104), calls=%async_computation.1 | async-start | bytes 2359296 | tf_op jit(solution)/shard_map/all_to_all | solution.py:567
  57.5 4.5 %columns_apart.1 = (bf16[1,2,3,16,384]{4,3,2,1,0:T(8,128)(2,1)}, bf16[1,2,3,16,384]{4,3,2,1,0:T(8,128)(2,1)}, bf16[1,2,3,16,384]{4,3,2,1,0:T(8,128)(2,1)}, bf16[...) custom-call(s32[5]{0:T(128)S(1)} %stack.68.at_ref, ...), custom_call_target="tpu_custom_call" | custom-call | flops 600000000 | bytes 3000000 | tf_op jit(solution)/shard_map/columns_apart/pallas_call | solution.py:142
  68.9 2.4 %collective-permute-start.5 = (bf16[6,16,384]{2,1,0:T(8,128)(2,1)}, bf16[6,16,384]{2,1,0:T(8,128)(2,1)S(1)}, u32[]{:S(2)}, u32[]{:S(2)}) collective-permute-start(bf16[6,16,384]{2,1,0:T(8,128)(2,1)} %bitcast.96), channel_id=1, source_target_pairs={{0,12},{2,14},{4,8},{6,10},{8,4},{10,6},{12,0},{14,2},{16,28},{18,... | collective-permute-start | bytes 221192 | tf_op jit(solution)/shard_map/ppermute | solution.py:536
  72.9 3.0 %collective-permute-start.7 = (bf16[6,16,384]{2,1,0:T(8,128)(2,1)}, bf16[6,16,384]{2,1,0:T(8,128)(2,1)S(1)}, u32[]{:S(2)}, u32[]{:S(2)}) collective-permute-start(bf16[6,16,384]{2,1,0:T(8,128)(2,1)} %bitcast.94), channel_id=1, source_target_pairs={{0,16},{2,18},{4,20},{6,22},{8,24},{10,26},{12,28},{14,30},{16,0},... | collective-permute-start | bytes 221192 | tf_op jit(solution)/shard_map/ppermute | solution.py:536
  76.0 3.4 %collective-permute-done.3.refs_4_ = bf16[6,16,384]{2,1,0:T(8,128)(2,1)S(1)} collective-permute-done((bf16[6,16,384]{2,1,0:T(8,128)(2,1)}, bf16[6,16,384]{2,1,0:T(8,128)(2,1)S(1)}, u32[]{:S(2)}, u32[]{:S(2)}) %collective-permute-start.3) | collective-permute-done | bytes 73760 | tf_op jit(solution)/shard_map/ppermute | solution.py:536
  79.4 5.6 %collective-permute-start.8 = (bf16[6,16,384]{2,1,0:T(8,128)(2,1)}, bf16[6,16,384]{2,1,0:T(8,128)(2,1)S(1)}, u32[]{:S(2)}, u32[]{:S(2)}) collective-permute-start(bf16[6,16,384]{2,1,0:T(8,128)(2,1)} %bitcast.93), channel_id=1, source_target_pairs={{0,18},{2,16},{4,22},{6,20},{8,26},{10,24},{12,30},{14,28},{16,2},... | collective-permute-start | bytes 221192 | tf_op jit(solution)/shard_map/ppermute | solution.py:536
  85.0 2.5 %collective-permute-start.9 = (bf16[6,16,384]{2,1,0:T(8,128)(2,1)}, bf16[6,16,384]{2,1,0:T(8,128)(2,1)S(1)}, u32[]{:S(2)}, u32[]{:S(2)}) collective-permute-start(bf16[6,16,384]{2,1,0:T(8,128)(2,1)} %bitcast.92), channel_id=1, source_target_pairs={{0,20},{2,22},{4,16},{6,18},{8,28},{10,30},{12,24},{14,26},{16,4},... | collective-permute-start | bytes 221192 | tf_op jit(solution)/shard_map/ppermute | solution.py:536
  89.7 6.5 %collective-permute-done.7.refs_8_ = bf16[6,16,384]{2,1,0:T(8,128)(2,1)S(1)} collective-permute-done((bf16[6,16,384]{2,1,0:T(8,128)(2,1)}, bf16[6,16,384]{2,1,0:T(8,128)(2,1)S(1)}, u32[]{:S(2)}, u32[]{:S(2)}) %collective-permute-start.7) | collective-permute-done | bytes 73760 | tf_op jit(solution)/shard_map/ppermute | solution.py:536
  96.2 3.0 %collective-permute-start.12 = (bf16[6,16,384]{2,1,0:T(8,128)(2,1)}, bf16[6,16,384]{2,1,0:T(8,128)(2,1)S(1)}, u32[]{:S(2)}, u32[]{:S(2)}) collective-permute-start(bf16[6,16,384]{2,1,0:T(8,128)(2,1)} %bitcast.89), channel_id=1, source_target_pairs={{0,26},{2,24},{4,30},{6,28},{8,18},{10,16},{12,22},{14,20},{16,10}... | collective-permute-start | bytes 221192 | tf_op jit(solution)/shard_map/ppermute | solution.py:536
  99.2 2.9 %collective-permute-start.13 = (bf16[6,16,384]{2,1,0:T(8,128)(2,1)}, bf16[6,16,384]{2,1,0:T(8,128)(2,1)S(1)}, u32[]{:S(2)}, u32[]{:S(2)}) collective-permute-start(bf16[6,16,384]{2,1,0:T(8,128)(2,1)} %bitcast.88), channel_id=1, source_target_pairs={{0,28},{2,30},{4,24},{6,26},{8,20},{10,22},{12,16},{14,18},{16,12}... | collective-permute-start | bytes 221192 | tf_op jit(solution)/shard_map/ppermute | solution.py:536
  104.3 2.4 %collective-permute-done.13.refs_14_ = bf16[6,16,384]{2,1,0:T(8,128)(2,1)S(1)} collective-permute-done((bf16[6,16,384]{2,1,0:T(8,128)(2,1)}, bf16[6,16,384]{2,1,0:T(8,128)(2,1)S(1)}, u32[]{:S(2)}, u32[]{:S(2)}) %collective-permute-start.13) | collective-permute-done | bytes 73760 | tf_op jit(solution)/shard_map/ppermute | solution.py:536
  106.8 3.6 %collective-permute-done.14.refs_15_ = bf16[6,16,384]{2,1,0:T(8,128)(2,1)S(1)} collective-permute-done((bf16[6,16,384]{2,1,0:T(8,128)(2,1)}, bf16[6,16,384]{2,1,0:T(8,128)(2,1)S(1)}, u32[]{:S(2)}, u32[]{:S(2)}) %collective-permute-start.14) | collective-permute-done | bytes 73760 | tf_op jit(solution)/shard_map/ppermute | solution.py:536
  111.0 10.5 %backward.1 = (bf16[2,768,384]{2,1,0:T(8,128)(2,1)}, f32[256,384]{1,0:T(8,128)}, f32[256,384]{1,0:T(8,128)}) custom-call(s32[5]{0:T(128)S(1)} %stack.68.at_ref, bf16[768,768]{1,0:T(8,128)(2,1)} %get-tuple-element.68.m_ref, bf16[768,768]{1,0:T(8,128)(2,1)} %get-tuple-element.69.wi_ref, bf16[768,768]{1,0:T(8,128)(2,1)} %get-tuple-element.70.wo_ref, ...), custom_call_target="tpu_custom_call" | custom-call | flops 1800000000 | bytes 9000000 | tf_op jit(solution)/shard_map/backward/pallas_call | solution.py:411
  124.2 4.2 %rows_back.1 = (bf16[8,16,384]{2,1,0:T(8,128)(2,1)}, bf16[8,16,384]{2,1,0:T(8,128)(2,1)}, bf16[8,16,384]{2,1,0:T(8,128)(2,1)}, bf16[8,16,384]{2,1,0:T(8,128)(2,1...) custom-call(s32[5]{0:T(128)S(1)} %stack.68.at_ref, ...), custom_call_target="tpu_custom_call" | custom-call | flops 800000000 | bytes 4000000 | tf_op jit(solution)/shard_map/rows_back/pallas_call | solution.py:445
  129.3 2.7 %collective-permute-start.18 = (bf16[8,16,384]{2,1,0:T(8,128)(2,1)}, bf16[8,16,384]{2,1,0:T(8,128)(2,1)S(1)}, u32[]{:S(2)}, u32[]{:S(2)}) collective-permute-start(bf16[8,16,384]{2,1,0:T(8,128)(2,1)} %get-tuple-element.99), channel_id=1, source_target_pairs={{0,6},{2,4},{4,2},{6,0},{8,14},{10,12},{12,10},{14,8},{16,22},{18,... | collective-permute-start | bytes 294920 | tf_op jit(solution)/shard_map/ppermute | solution.py:536
  132.0 2.5 %collective-permute-start.19 = (bf16[8,16,384]{2,1,0:T(8,128)(2,1)}, bf16[8,16,384]{2,1,0:T(8,128)(2,1)S(1)}, u32[]{:S(2)}, u32[]{:S(2)}) collective-permute-start(bf16[8,16,384]{2,1,0:T(8,128)(2,1)} %get-tuple-element.100), channel_id=1, source_target_pairs={{0,8},{2,10},{4,12},{6,14},{8,0},{10,2},{12,4},{14,6},{16,24},{18,... | collective-permute-start | bytes 294920 | tf_op jit(solution)/shard_map/ppermute | solution.py:536
  138.4 2.8 %collective-permute-done.20.refs_10_.refs_11_ = bf16[8,16,384]{2,1,0:T(8,128)(2,1)S(1)} collective-permute-done((bf16[8,16,384]{2,1,0:T(8,128)(2,1)}, bf16[8,16,384]{2,1,0:T(8,128)(2,1)S(1)}, u32[]{:S(2)}, u32[]{:S(2)}) %collective-permute-start.20) | collective-permute-done | bytes 98336 | tf_op jit(solution)/shard_map/ppermute | solution.py:536
  145.7 4.8 %all-to-all-start.2 = ((bf16[16,2,16,384]{3,2,1,0:T(8,128)(2,1)}), bf16[16,2,16,384]{3,2,1,0:T(8,128)(2,1)S(1)}, u32[]{:S(2)}, u32[]{:S(2)}) async-start(bf16[16,2,16,384]{3,2,1,0:T(8,128)(2,1)} %totals.1), calls=%async_computation.2 | async-start | bytes 786432 | tf_op jit(solution)/shard_map/all_to_all | solution.py:567
  150.6 2.9 %collective-permute-start.23 = (bf16[6,16,384]{2,1,0:T(8,128)(2,1)S(1)}, bf16[6,16,384]{2,1,0:T(8,128)(2,1)S(1)}, u32[]{:S(2)}, u32[]{:S(2)}) collective-permute-start(bf16[6,16,384]{2,1,0:T(8,128)(2,1)S(1)} %copy-done.43), channel_id=1, source_target_pairs={{0,16},{2,18},{4,20},{6,22},{8,24},{10,26},{12,28},{14,30},{16,0},... | collective-permute-start | bytes 221192 | tf_op jit(solution)/shard_map/ppermute | solution.py:536
  154.9 3.3 %collective-permute-start.25 = (bf16[6,16,384]{2,1,0:T(8,128)(2,1)S(1)}, bf16[6,16,384]{2,1,0:T(8,128)(2,1)S(1)}, u32[]{:S(2)}, u32[]{:S(2)}) collective-permute-start(bf16[6,16,384]{2,1,0:T(8,128)(2,1)S(1)} %copy-done.41), channel_id=1, source_target_pairs={{0,20},{2,22},{4,16},{6,18},{8,28},{10,30},{12,24},{14,26},{16,4},... | collective-permute-start | bytes 221192 | tf_op jit(solution)/shard_map/ppermute | solution.py:536
  158.3 3.7 %collective-permute-start.27 = (bf16[6,16,384]{2,1,0:T(8,128)(2,1)S(1)}, bf16[6,16,384]{2,1,0:T(8,128)(2,1)S(1)}, u32[]{:S(2)}, u32[]{:S(2)}) collective-permute-start(bf16[6,16,384]{2,1,0:T(8,128)(2,1)S(1)} %copy-done.39), channel_id=1, source_target_pairs={{0,24},{2,26},{4,28},{6,30},{8,16},{10,18},{12,20},{14,22},{16,8},... | collective-permute-start | bytes 221192 | tf_op jit(solution)/shard_map/ppermute | solution.py:536
  162.0 9.8 %collective-permute-done.23 = bf16[6,16,384]{2,1,0:T(8,128)(2,1)S(1)} collective-permute-done((bf16[6,16,384]{2,1,0:T(8,128)(2,1)S(1)}, bf16[6,16,384]{2,1,0:T(8,128)(2,1)S(1)}, u32[]{:S(2)}, u32[]{:S(2)}) %collective-permute-start.23) | collective-permute-done | bytes 73760 | tf_op jit(solution)/shard_map/ppermute | solution.py:536
  175.1 2.2 %collective-permute-start.29 = (bf16[6,16,384]{2,1,0:T(8,128)(2,1)S(1)}, bf16[6,16,384]{2,1,0:T(8,128)(2,1)S(1)}, u32[]{:S(2)}, u32[]{:S(2)}) collective-permute-start(bf16[6,16,384]{2,1,0:T(8,128)(2,1)S(1)} %copy-done.37), channel_id=1, source_target_pairs={{0,28},{2,30},{4,24},{6,26},{8,20},{10,22},{12,16},{14,18},{16,12}... | collective-permute-start | bytes 221192 | tf_op jit(solution)/shard_map/ppermute | solution.py:536
  179.1 3.3 %collective-permute-done.26 = bf16[6,16,384]{2,1,0:T(8,128)(2,1)S(1)} collective-permute-done((bf16[6,16,384]{2,1,0:T(8,128)(2,1)S(1)}, bf16[6,16,384]{2,1,0:T(8,128)(2,1)S(1)}, u32[]{:S(2)}, u32[]{:S(2)}) %collective-permute-start.26) | collective-permute-done | bytes 73760 | tf_op jit(solution)/shard_map/ppermute | solution.py:536
  182.4 3.0 %collective-permute-done.30 = bf16[6,16,384]{2,1,0:T(8,128)(2,1)S(1)} collective-permute-done((bf16[6,16,384]{2,1,0:T(8,128)(2,1)S(1)}, bf16[6,16,384]{2,1,0:T(8,128)(2,1)S(1)}, u32[]{:S(2)}, u32[]{:S(2)}) %collective-permute-start.30) | collective-permute-done | bytes 73760 | tf_op jit(solution)/shard_map/ppermute | solution.py:536
  186.0 5.6 %inverse_apart.1 = bf16[3,180,2,768]{3,2,1,0:T(2,128)(2,1)} custom-call(s32[5]{0:T(128)S(1)} %stack.68.at_ref, bf16[3,180,2,768]{3,2,1,0:T(2,128)(2,1)} %bitcast.49, bf16[360,256]{1,0:T(8,128)(2,1)} %constant.70.clone.t_ref, bf16[1,8,16,384]{3,2,1,0:T(8,128)(2,1)} %bitcast.52, bf16[1,8,16,384]{3,2,1,0:T(8,128)(2,1)} %bitcast.53, ...), custom_call_target="tpu_custom_call" | custom-call | flops 800000000 | bytes 4000000 | tf_op jit(solution)/shard_map/inverse_apart/pallas_call | solution.py:221
  191.7 4.6 %inverse.1 = bf16[3,180,2,768]{3,2,1,0:T(2,128)(2,1)} custom-call(bf16[3,180,2,768]{3,2,1,0:T(2,128)(2,1)} %bitcast.45, bf16[360,256]{1,0:T(8,128)(2,1)} %constant.69.clone.t_ref, bf16[2,1,8,2,3,16,384]{6,5,4,3,2,1,0:T(8,128)(2,1)} %bitcast.47), custom_call_target="tpu_custom_call" | custom-call | flops 800000000 | bytes 4000000 | tf_op jit(solution)/shard_map/inverse/pallas_call | solution.py:188
  (137 shorter events, 36.0 us)
Async XLA Ops:
  4.5 35.4 %all-to-all-start = ((bf16[16,6,16,384]{3,2,1,0:T(8,128)(2,1)}), bf16[16,6,16,384]{3,2,1,0:T(8,128)(2,1)S(1)}, u32[]{:S(2)}, u32[]{:S(2)}) async-start(bf16[16,6,16,384]{3,2,1,0:T(8,128)(2,1)} %bitcast.46), calls=%async_computation | async-start | bytes 2359296 | tf_op jit(solution)/shard_map/all_to_all | solution.py:567
  51.3 92.0 %all-to-all-start.1 = ((bf16[16,6,16,384]{3,2,1,0:T(8,128)(2,1)}), bf16[16,6,16,384]{3,2,1,0:T(8,128)(2,1)S(1)}, u32[]{:S(2)}, u32[]{:S(2)}) async-start(bf16[16,6,16,384]{3,2,1,0:T(8,128)(2,1)} %get-tuple-element.104), calls=%async_computation.1 | async-start | bytes 2359296 | tf_op jit(solution)/shard_map/all_to_all | solution.py:567
  62.0 6.9 %collective-permute-start = (bf16[6,16,384]{2,1,0:T(8,128)(2,1)}, bf16[6,16,384]{2,1,0:T(8,128)(2,1)S(1)}, u32[]{:S(2)}, u32[]{:S(2)}) collective-permute-start(bf16[6,16,384]{2,1,0:T(8,128)(2,1)} %bitcast.101), channel_id=1, source_target_pairs={{0,2},{2,0},{4,6},{6,4},{8,10},{10,8},{12,14},{14,12},{16,18},{18,... | collective-permute-start | bytes 221192 | tf_op jit(solution)/shard_map/ppermute | solution.py:536
  64.0 7.3 %collective-permute-start.1 = (bf16[6,16,384]{2,1,0:T(8,128)(2,1)}, bf16[6,16,384]{2,1,0:T(8,128)(2,1)S(1)}, u32[]{:S(2)}, u32[]{:S(2)}) collective-permute-start(bf16[6,16,384]{2,1,0:T(8,128)(2,1)} %bitcast.100), channel_id=1, source_target_pairs={{0,4},{2,6},{4,0},{6,2},{8,12},{10,14},{12,8},{14,10},{16,20},{18,... | collective-permute-start | bytes 221192 | tf_op jit(solution)/shard_map/ppermute | solution.py:536
  65.4 7.5 %collective-permute-start.2 = (bf16[6,16,384]{2,1,0:T(8,128)(2,1)}, bf16[6,16,384]{2,1,0:T(8,128)(2,1)S(1)}, u32[]{:S(2)}, u32[]{:S(2)}) collective-permute-start(bf16[6,16,384]{2,1,0:T(8,128)(2,1)} %bitcast.99), channel_id=1, source_target_pairs={{0,6},{2,4},{4,2},{6,0},{8,14},{10,12},{12,10},{14,8},{16,22},{18,... | collective-permute-start | bytes 221192 | tf_op jit(solution)/shard_map/ppermute | solution.py:536
  65.6 13.8 %collective-permute-start.3 = (bf16[6,16,384]{2,1,0:T(8,128)(2,1)}, bf16[6,16,384]{2,1,0:T(8,128)(2,1)S(1)}, u32[]{:S(2)}, u32[]{:S(2)}) collective-permute-start(bf16[6,16,384]{2,1,0:T(8,128)(2,1)} %bitcast.98), channel_id=1, source_target_pairs={{0,8},{2,10},{4,12},{6,14},{8,0},{10,2},{12,4},{14,6},{16,24},{18,... | collective-permute-start | bytes 221192 | tf_op jit(solution)/shard_map/ppermute | solution.py:536
  67.5 17.5 %collective-permute-start.4 = (bf16[6,16,384]{2,1,0:T(8,128)(2,1)}, bf16[6,16,384]{2,1,0:T(8,128)(2,1)S(1)}, u32[]{:S(2)}, u32[]{:S(2)}) collective-permute-start(bf16[6,16,384]{2,1,0:T(8,128)(2,1)} %bitcast.97), channel_id=1, source_target_pairs={{0,10},{2,8},{4,14},{6,12},{8,2},{10,0},{12,6},{14,4},{16,26},{18,... | collective-permute-start | bytes 221192 | tf_op jit(solution)/shard_map/ppermute | solution.py:536
  68.9 18.6 %collective-permute-start.5 = (bf16[6,16,384]{2,1,0:T(8,128)(2,1)}, bf16[6,16,384]{2,1,0:T(8,128)(2,1)S(1)}, u32[]{:S(2)}, u32[]{:S(2)}) collective-permute-start(bf16[6,16,384]{2,1,0:T(8,128)(2,1)} %bitcast.96), channel_id=1, source_target_pairs={{0,12},{2,14},{4,8},{6,10},{8,4},{10,6},{12,0},{14,2},{16,28},{18,... | collective-permute-start | bytes 221192 | tf_op jit(solution)/shard_map/ppermute | solution.py:536
  71.3 17.8 %collective-permute-start.6 = (bf16[6,16,384]{2,1,0:T(8,128)(2,1)}, bf16[6,16,384]{2,1,0:T(8,128)(2,1)S(1)}, u32[]{:S(2)}, u32[]{:S(2)}) collective-permute-start(bf16[6,16,384]{2,1,0:T(8,128)(2,1)} %bitcast.95), channel_id=1, source_target_pairs={{0,14},{2,12},{4,10},{6,8},{8,6},{10,4},{12,2},{14,0},{16,30},{18,... | collective-permute-start | bytes 221192 | tf_op jit(solution)/shard_map/ppermute | solution.py:536
  72.9 23.3 %collective-permute-start.7 = (bf16[6,16,384]{2,1,0:T(8,128)(2,1)}, bf16[6,16,384]{2,1,0:T(8,128)(2,1)S(1)}, u32[]{:S(2)}, u32[]{:S(2)}) collective-permute-start(bf16[6,16,384]{2,1,0:T(8,128)(2,1)} %bitcast.94), channel_id=1, source_target_pairs={{0,16},{2,18},{4,20},{6,22},{8,24},{10,26},{12,28},{14,30},{16,0},... | collective-permute-start | bytes 221192 | tf_op jit(solution)/shard_map/ppermute | solution.py:536
  79.4 19.8 %collective-permute-start.8 = (bf16[6,16,384]{2,1,0:T(8,128)(2,1)}, bf16[6,16,384]{2,1,0:T(8,128)(2,1)S(1)}, u32[]{:S(2)}, u32[]{:S(2)}) collective-permute-start(bf16[6,16,384]{2,1,0:T(8,128)(2,1)} %bitcast.93), channel_id=1, source_target_pairs={{0,18},{2,16},{4,22},{6,20},{8,26},{10,24},{12,30},{14,28},{16,2},... | collective-permute-start | bytes 221192 | tf_op jit(solution)/shard_map/ppermute | solution.py:536
  85.0 17.1 %collective-permute-start.9 = (bf16[6,16,384]{2,1,0:T(8,128)(2,1)}, bf16[6,16,384]{2,1,0:T(8,128)(2,1)S(1)}, u32[]{:S(2)}, u32[]{:S(2)}) collective-permute-start(bf16[6,16,384]{2,1,0:T(8,128)(2,1)} %bitcast.92), channel_id=1, source_target_pairs={{0,20},{2,22},{4,16},{6,18},{8,28},{10,30},{12,24},{14,26},{16,4},... | collective-permute-start | bytes 221192 | tf_op jit(solution)/shard_map/ppermute | solution.py:536
  87.6 16.6 %collective-permute-start.10 = (bf16[6,16,384]{2,1,0:T(8,128)(2,1)}, bf16[6,16,384]{2,1,0:T(8,128)(2,1)S(1)}, u32[]{:S(2)}, u32[]{:S(2)}) collective-permute-start(bf16[6,16,384]{2,1,0:T(8,128)(2,1)} %bitcast.91), channel_id=1, source_target_pairs={{0,22},{2,20},{4,18},{6,16},{8,30},{10,28},{12,26},{14,24},{16,6},... | collective-permute-start | bytes 221192 | tf_op jit(solution)/shard_map/ppermute | solution.py:536
  89.1 15.0 %collective-permute-start.11 = (bf16[6,16,384]{2,1,0:T(8,128)(2,1)}, bf16[6,16,384]{2,1,0:T(8,128)(2,1)S(1)}, u32[]{:S(2)}, u32[]{:S(2)}) collective-permute-start(bf16[6,16,384]{2,1,0:T(8,128)(2,1)} %bitcast.90), channel_id=1, source_target_pairs={{0,24},{2,26},{4,28},{6,30},{8,16},{10,18},{12,20},{14,22},{16,8},... | collective-permute-start | bytes 221192 | tf_op jit(solution)/shard_map/ppermute | solution.py:536
  96.2 8.1 %collective-permute-start.12 = (bf16[6,16,384]{2,1,0:T(8,128)(2,1)}, bf16[6,16,384]{2,1,0:T(8,128)(2,1)S(1)}, u32[]{:S(2)}, u32[]{:S(2)}) collective-permute-start(bf16[6,16,384]{2,1,0:T(8,128)(2,1)} %bitcast.89), channel_id=1, source_target_pairs={{0,26},{2,24},{4,30},{6,28},{8,18},{10,16},{12,22},{14,20},{16,10}... | collective-permute-start | bytes 221192 | tf_op jit(solution)/shard_map/ppermute | solution.py:536
  99.2 7.5 %collective-permute-start.13 = (bf16[6,16,384]{2,1,0:T(8,128)(2,1)}, bf16[6,16,384]{2,1,0:T(8,128)(2,1)S(1)}, u32[]{:S(2)}, u32[]{:S(2)}) collective-permute-start(bf16[6,16,384]{2,1,0:T(8,128)(2,1)} %bitcast.88), channel_id=1, source_target_pairs={{0,28},{2,30},{4,24},{6,26},{8,20},{10,22},{12,16},{14,18},{16,12}... | collective-permute-start | bytes 221192 | tf_op jit(solution)/shard_map/ppermute | solution.py:536
  102.1 8.3 %collective-permute-start.14 = (bf16[6,16,384]{2,1,0:T(8,128)(2,1)}, bf16[6,16,384]{2,1,0:T(8,128)(2,1)S(1)}, u32[]{:S(2)}, u32[]{:S(2)}) collective-permute-start(bf16[6,16,384]{2,1,0:T(8,128)(2,1)} %bitcast.87), channel_id=1, source_target_pairs={{0,30},{2,28},{4,26},{6,24},{8,22},{10,20},{12,18},{14,16},{16,14}... | collective-permute-start | bytes 221192 | tf_op jit(solution)/shard_map/ppermute | solution.py:536
  129.1 7.3 %collective-permute-start.17 = (bf16[8,16,384]{2,1,0:T(8,128)(2,1)}, bf16[8,16,384]{2,1,0:T(8,128)(2,1)S(1)}, u32[]{:S(2)}, u32[]{:S(2)}) collective-permute-start(bf16[8,16,384]{2,1,0:T(8,128)(2,1)} %get-tuple-element.98), channel_id=1, source_target_pairs={{0,4},{2,6},{4,0},{6,2},{8,12},{10,14},{12,8},{14,10},{16,20},{18,... | collective-permute-start | bytes 294920 | tf_op jit(solution)/shard_map/ppermute | solution.py:536
  129.3 9.1 %collective-permute-start.18 = (bf16[8,16,384]{2,1,0:T(8,128)(2,1)}, bf16[8,16,384]{2,1,0:T(8,128)(2,1)S(1)}, u32[]{:S(2)}, u32[]{:S(2)}) collective-permute-start(bf16[8,16,384]{2,1,0:T(8,128)(2,1)} %get-tuple-element.99), channel_id=1, source_target_pairs={{0,6},{2,4},{4,2},{6,0},{8,14},{10,12},{12,10},{14,8},{16,22},{18,... | collective-permute-start | bytes 294920 | tf_op jit(solution)/shard_map/ppermute | solution.py:536
  132.0 6.4 %collective-permute-start.19 = (bf16[8,16,384]{2,1,0:T(8,128)(2,1)}, bf16[8,16,384]{2,1,0:T(8,128)(2,1)S(1)}, u32[]{:S(2)}, u32[]{:S(2)}) collective-permute-start(bf16[8,16,384]{2,1,0:T(8,128)(2,1)} %get-tuple-element.100), channel_id=1, source_target_pairs={{0,8},{2,10},{4,12},{6,14},{8,0},{10,2},{12,4},{14,6},{16,24},{18,... | collective-permute-start | bytes 294920 | tf_op jit(solution)/shard_map/ppermute | solution.py:536
  134.5 6.8 %collective-permute-start.20 = (bf16[8,16,384]{2,1,0:T(8,128)(2,1)}, bf16[8,16,384]{2,1,0:T(8,128)(2,1)S(1)}, u32[]{:S(2)}, u32[]{:S(2)}) collective-permute-start(bf16[8,16,384]{2,1,0:T(8,128)(2,1)} %get-tuple-element.101), channel_id=1, source_target_pairs={{0,10},{2,8},{4,14},{6,12},{8,2},{10,0},{12,6},{14,4},{16,26},{18,... | collective-permute-start | bytes 294920 | tf_op jit(solution)/shard_map/ppermute | solution.py:536
  134.5 7.7 %collective-permute-start.21 = (bf16[8,16,384]{2,1,0:T(8,128)(2,1)}, bf16[8,16,384]{2,1,0:T(8,128)(2,1)S(1)}, u32[]{:S(2)}, u32[]{:S(2)}) collective-permute-start(bf16[8,16,384]{2,1,0:T(8,128)(2,1)} %get-tuple-element.102), channel_id=1, source_target_pairs={{0,12},{2,14},{4,8},{6,10},{8,4},{10,6},{12,0},{14,2},{16,28},{18,... | collective-permute-start | bytes 294920 | tf_op jit(solution)/shard_map/ppermute | solution.py:536
  136.3 7.0 %collective-permute-start.22 = (bf16[8,16,384]{2,1,0:T(8,128)(2,1)}, bf16[8,16,384]{2,1,0:T(8,128)(2,1)S(1)}, u32[]{:S(2)}, u32[]{:S(2)}) collective-permute-start(bf16[8,16,384]{2,1,0:T(8,128)(2,1)} %get-tuple-element.103), channel_id=1, source_target_pairs={{0,14},{2,12},{4,10},{6,8},{8,6},{10,4},{12,2},{14,0},{16,30},{18,... | collective-permute-start | bytes 294920 | tf_op jit(solution)/shard_map/ppermute | solution.py:536
  145.7 45.9 %all-to-all-start.2 = ((bf16[16,2,16,384]{3,2,1,0:T(8,128)(2,1)}), bf16[16,2,16,384]{3,2,1,0:T(8,128)(2,1)S(1)}, u32[]{:S(2)}, u32[]{:S(2)}) async-start(bf16[16,2,16,384]{3,2,1,0:T(8,128)(2,1)} %totals.1), calls=%async_computation.2 | async-start | bytes 786432 | tf_op jit(solution)/shard_map/all_to_all | solution.py:567
  150.6 21.2 %collective-permute-start.23 = (bf16[6,16,384]{2,1,0:T(8,128)(2,1)S(1)}, bf16[6,16,384]{2,1,0:T(8,128)(2,1)S(1)}, u32[]{:S(2)}, u32[]{:S(2)}) collective-permute-start(bf16[6,16,384]{2,1,0:T(8,128)(2,1)S(1)} %copy-done.43), channel_id=1, source_target_pairs={{0,16},{2,18},{4,20},{6,22},{8,24},{10,26},{12,28},{14,30},{16,0},... | collective-permute-start | bytes 221192 | tf_op jit(solution)/shard_map/ppermute | solution.py:536
  153.4 21.6 %collective-permute-start.24 = (bf16[6,16,384]{2,1,0:T(8,128)(2,1)S(1)}, bf16[6,16,384]{2,1,0:T(8,128)(2,1)S(1)}, u32[]{:S(2)}, u32[]{:S(2)}) collective-permute-start(bf16[6,16,384]{2,1,0:T(8,128)(2,1)S(1)} %copy-done.42), channel_id=1, source_target_pairs={{0,18},{2,16},{4,22},{6,20},{8,26},{10,24},{12,30},{14,28},{16,2},... | collective-permute-start | bytes 221192 | tf_op jit(solution)/shard_map/ppermute | solution.py:536
  154.9 22.4 %collective-permute-start.25 = (bf16[6,16,384]{2,1,0:T(8,128)(2,1)S(1)}, bf16[6,16,384]{2,1,0:T(8,128)(2,1)S(1)}, u32[]{:S(2)}, u32[]{:S(2)}) collective-permute-start(bf16[6,16,384]{2,1,0:T(8,128)(2,1)S(1)} %copy-done.41), channel_id=1, source_target_pairs={{0,20},{2,22},{4,16},{6,18},{8,28},{10,30},{12,24},{14,26},{16,4},... | collective-permute-start | bytes 221192 | tf_op jit(solution)/shard_map/ppermute | solution.py:536
  158.2 24.1 %collective-permute-start.26 = (bf16[6,16,384]{2,1,0:T(8,128)(2,1)S(1)}, bf16[6,16,384]{2,1,0:T(8,128)(2,1)S(1)}, u32[]{:S(2)}, u32[]{:S(2)}) collective-permute-start(bf16[6,16,384]{2,1,0:T(8,128)(2,1)S(1)} %copy-done.40), channel_id=1, source_target_pairs={{0,22},{2,20},{4,18},{6,16},{8,30},{10,28},{12,26},{14,24},{16,6},... | collective-permute-start | bytes 221192 | tf_op jit(solution)/shard_map/ppermute | solution.py:536
  158.3 24.0 %collective-permute-start.27 = (bf16[6,16,384]{2,1,0:T(8,128)(2,1)S(1)}, bf16[6,16,384]{2,1,0:T(8,128)(2,1)S(1)}, u32[]{:S(2)}, u32[]{:S(2)}) collective-permute-start(bf16[6,16,384]{2,1,0:T(8,128)(2,1)S(1)} %copy-done.39), channel_id=1, source_target_pairs={{0,24},{2,26},{4,28},{6,30},{8,16},{10,18},{12,20},{14,22},{16,8},... | collective-permute-start | bytes 221192 | tf_op jit(solution)/shard_map/ppermute | solution.py:536
  171.8 10.5 %collective-permute-start.28 = (bf16[6,16,384]{2,1,0:T(8,128)(2,1)S(1)}, bf16[6,16,384]{2,1,0:T(8,128)(2,1)S(1)}, u32[]{:S(2)}, u32[]{:S(2)}) collective-permute-start(bf16[6,16,384]{2,1,0:T(8,128)(2,1)S(1)} %copy-done.38), channel_id=1, source_target_pairs={{0,26},{2,24},{4,30},{6,28},{8,18},{10,16},{12,22},{14,20},{16,10}... | collective-permute-start | bytes 221192 | tf_op jit(solution)/shard_map/ppermute | solution.py:536
  175.1 7.3 %collective-permute-start.29 = (bf16[6,16,384]{2,1,0:T(8,128)(2,1)S(1)}, bf16[6,16,384]{2,1,0:T(8,128)(2,1)S(1)}, u32[]{:S(2)}, u32[]{:S(2)}) collective-permute-start(bf16[6,16,384]{2,1,0:T(8,128)(2,1)S(1)} %copy-done.37), channel_id=1, source_target_pairs={{0,28},{2,30},{4,24},{6,26},{8,20},{10,22},{12,16},{14,18},{16,12}... | collective-permute-start | bytes 221192 | tf_op jit(solution)/shard_map/ppermute | solution.py:536
  177.3 8.1 %collective-permute-start.30 = (bf16[6,16,384]{2,1,0:T(8,128)(2,1)S(1)}, bf16[6,16,384]{2,1,0:T(8,128)(2,1)S(1)}, u32[]{:S(2)}, u32[]{:S(2)}) collective-permute-start(bf16[6,16,384]{2,1,0:T(8,128)(2,1)S(1)} %copy-done.36), channel_id=1, source_target_pairs={{0,30},{2,28},{4,26},{6,24},{8,22},{10,20},{12,18},{14,16},{16,14}... | collective-permute-start | bytes 221192 | tf_op jit(solution)/shard_map/ppermute | solution.py:536
  (47 other events, 541.1 us)

commit v4 on v3

--- a/solution.py
+++ b/solution.py
@@ -17,6 +17,8 @@
 GROUPS = 8
 GROUP = MODES // GROUPS
 CK = 2 * GROUP
+PER = HALF // BLOCK
+LANES = 128
 F32 = jnp.float32
 BF16 = jnp.bfloat16
 
@@ -248,27 +250,25 @@
     for r in range(shards):
         nx_ref[r] = base_ref[r ^ at_ref[0]]
     transposed(mx_ref, [nx_ref[r] for r in range(shards)])
-    row = lax.broadcasted_iota(jnp.int32, (BLOCK, HALF), 0)
-    lane = lax.broadcasted_iota(jnp.int32, (BLOCK, HALF), 1)
+    row = lax.broadcasted_iota(jnp.int32, (BLOCK, LANES), 0)
+    lane = lax.broadcasted_iota(jnp.int32, (BLOCK, LANES), 1)
+    place = jnp.where(lane == row, 1.0, 0.0).astype(BF16)
+    below = jnp.zeros((LANES - BLOCK, LANES), F32)
     for w_ref, f_ref, t_ref in ((wi_ref, outs[0], outs[1]), (wo_ref, outs[2], outs[3])):
-        diagonal = []
-        for c in range(2):
-            pieces = []
-            for j in range(HALF // BLOCK):
-                place = jnp.where(lane == row + j * BLOCK, 1.0, 0.0).astype(BF16)
-                pieces.append(dot(w_ref[c, j], place))
-            diagonal.append(jnp.concatenate(pieces, axis=0))
-        real, imag = diagonal
-        real_t, imag_t = real.T.astype(BF16), imag.T.astype(BF16)
-        real, imag = real.astype(BF16), imag.astype(BF16)
-        f_ref[:HALF, :HALF] = real
-        f_ref[:HALF, HALF:] = imag
-        f_ref[HALF:, :HALF] = -imag
-        f_ref[HALF:, HALF:] = real
-        t_ref[:HALF, :HALF] = real_t
-        t_ref[:HALF, HALF:] = -imag_t
-        t_ref[HALF:, :HALF] = imag_t
-        t_ref[HALF:, HALF:] = real_t
+        for j in range(PER):
+            real, imag = (
+                jnp.concatenate([dot(w_ref[c, j], place), below], axis=0) for c in range(2)
+            )
+            real_t, imag_t = real.T.astype(BF16), imag.T.astype(BF16)
+            real, imag = real.astype(BF16), imag.astype(BF16)
+            f_ref[j, :LANES, :LANES] = real
+            f_ref[j, :LANES, LANES:] = imag
+            f_ref[j, LANES:, :LANES] = -imag
+            f_ref[j, LANES:, LANES:] = real
+            t_ref[j, :LANES, :LANES] = real_t
+            t_ref[j, :LANES, LANES:] = -imag_t
+            t_ref[j, LANES:, :LANES] = imag_t
+            t_ref[j, LANES:, LANES:] = real_t
 
 
 def prepare(at, base, in_weight, out_weight):
@@ -276,7 +276,7 @@
     weight = pl.BlockSpec((2, HALF // BLOCK, BLOCK, BLOCK), lambda i, at: (0, at[1], 0, 0))
     square = pl.BlockSpec((size, size), lambda i, at: (0, 0))
     stack = pl.BlockSpec((blocks, rows, size), lambda i, at: (0, 0, 0))
-    wide = pl.BlockSpec((2 * HALF, 2 * HALF), lambda i, at: (0, 0))
+    wide = pl.BlockSpec((PER, 2 * LANES, 2 * LANES), lambda i, at: (0, 0, 0))
     return pl.pallas_call(
         prepare_kernel,
         grid_spec=pltpu.PrefetchScalarGridSpec(
@@ -287,7 +287,7 @@
         ),
         out_shape=[pltpu.HBM((size, size), BF16)] * 2
         + [pltpu.HBM((blocks, rows, size), BF16)]
-        + [pltpu.HBM((2 * HALF, 2 * HALF), BF16)] * 4,
+        + [pltpu.HBM((PER, 2 * LANES, 2 * LANES), BF16)] * 4,
         compiler_params=params(40),
         cost_estimate=cost(4),
         name="prepare",
@@ -297,17 +297,36 @@
 SLOPE = math.sqrt(2.0 / math.pi)
 
 
-def side_by_side(x):
+def padded(x):
+    blank = jnp.zeros((x.shape[0], LANES - BLOCK), x.dtype)
+    pieces = []
+    for j in range(PER):
+        pieces += [x[:, j * BLOCK : (j + 1) * BLOCK], blank]
+    return jnp.concatenate(pieces, axis=1)
+
+
+def packed(x):
+    return jnp.concatenate([x[:, j * LANES : j * LANES + BLOCK] for j in range(PER)], axis=1)
+
+
+def lanes_of(j):
+    return slice(j * LANES, (j + 1) * LANES)
+
+
+def parts_of(x, j):
     rows = x.shape[0] // 2
-    return jnp.concatenate([x[:rows], x[rows:]], axis=1)
-
-
-def stacked(x):
-    return jnp.concatenate([x[:, :HALF], x[:, HALF:]], axis=0)
-
-
-def bias_row(ref):
-    return jnp.concatenate([ref[0:1, :], ref[1:2, :]], axis=1)
+    return jnp.concatenate([x[:rows, lanes_of(j)], x[rows:, lanes_of(j)]], axis=1)
+
+
+def joined(blocks):
+    halves = [
+        packed(jnp.concatenate([x[:, lanes_of(c)] for x in blocks], axis=1)) for c in range(2)
+    ]
+    return jnp.concatenate(halves, axis=0)
+
+
+def bias_row(ref, j):
+    return jnp.concatenate([ref[0:1, lanes_of(j)], ref[1:2, lanes_of(j)]], axis=1)
 
 
 def forward_kernel(
@@ -315,17 +334,22 @@
 ):
     del at_ref
     size = m_ref.shape[0]
-    spectrum = dot(m_ref[...], v_ref[...].reshape(size, HALF)).astype(BF16)
+    rows = size // 2
+    spectrum = dot(m_ref[...], padded(v_ref[...].reshape(size, HALF))).astype(BF16)
     s_ref[0] = spectrum
-    pre = dot(side_by_side(spectrum), wi_ref[...]) + bias_row(bi_ref)
-    square = pre * pre
-    tanh = jnp.tanh(SLOPE * (pre + 0.044715 * (square * pre)))
-    gate = 0.5 * (1.0 + tanh)
-    hidden = (pre * gate).astype(BF16)
-    d_ref[0] = gate + 0.5 * pre * (1.0 - tanh * tanh) * (SLOPE * (1.0 + 3 * 0.044715 * square))
-    h_ref[0] = stacked(hidden)
-    out = (dot(hidden, wo_ref[...]) + bias_row(bo_ref)).astype(BF16)
-    back = dot(n_ref[...].reshape(size, size), stacked(out)).astype(BF16)
+    blocks = []
+    for j in range(PER):
+        pre = dot(parts_of(spectrum, j), wi_ref[j]) + bias_row(bi_ref, j)
+        square = pre * pre
+        tanh = jnp.tanh(SLOPE * (pre + 0.044715 * (square * pre)))
+        gate = 0.5 * (1.0 + tanh)
+        hidden = (pre * gate).astype(BF16)
+        rise = SLOPE * (1.0 + 3 * 0.044715 * square)
+        d_ref[0, j] = gate + 0.5 * pre * (1.0 - tanh * tanh) * rise
+        h_ref[0, :rows, lanes_of(j)] = hidden[:, :LANES]
+        h_ref[0, rows:, lanes_of(j)] = hidden[:, LANES:]
+        blocks.append((dot(hidden, wo_ref[j]) + bias_row(bo_ref, j)).astype(BF16))
+    back = dot(n_ref[...].reshape(size, size), joined(blocks)).astype(BF16)
     o_ref[...] = back.reshape(o_ref.shape)
 
 
@@ -335,10 +359,10 @@
     chunk = pl.BlockSpec((shards, rows, CK, HALF), lambda s, at: (0, s, 0, 0))
     square = pl.BlockSpec((size, size), lambda s, at: (0, 0))
     stack = pl.BlockSpec(n.shape, lambda s, at: (0, 0, 0))
-    wide = pl.BlockSpec((2 * HALF, 2 * HALF), lambda s, at: (0, 0))
-    bias = pl.BlockSpec((2, HALF), lambda s, at: (0, at[1]))
-    tall = pl.BlockSpec((1, size, HALF), lambda s, at: (s, 0, 0))
-    pair = pl.BlockSpec((1, size // 2, 2 * HALF), lambda s, at: (s, 0, 0))
+    wide = pl.BlockSpec((PER, 2 * LANES, 2 * LANES), lambda s, at: (0, 0, 0))
+    bias = pl.BlockSpec((2, PER * LANES), lambda s, at: (0, at[1]))
+    tall = pl.BlockSpec((1, size, PER * LANES), lambda s, at: (s, 0, 0))
+    pair = pl.BlockSpec((1, PER, size // 2, 2 * LANES), lambda s, at: (s, 0, 0, 0))
     return pl.pallas_call(
         forward_kernel,
         grid_spec=pltpu.PrefetchScalarGridSpec(
@@ -349,9 +373,9 @@
         ),
         out_shape=[
             pltpu.HBM(v.shape, BF16),
-            pltpu.HBM((local, size, HALF), BF16),
-            pltpu.HBM((local, size, HALF), BF16),
-            pltpu.HBM((local, size // 2, 2 * HALF), F32),
+            pltpu.HBM((local, size, PER * LANES), BF16),
+            pltpu.HBM((local, size, PER * LANES), BF16),
+            pltpu.HBM((local, PER, size // 2, 2 * LANES), F32),
         ],
         compiler_params=params(40),
         cost_estimate=cost(9),
@@ -362,20 +386,14 @@
 PACK = 256
 
 
-def outer_parts(p_ref, at, left, right):
-    rows = right.shape[0] // 2
-    turned = jnp.concatenate([right[rows:], -right[:rows]], axis=0)
-    full = dot_t(left, jnp.concatenate([right, turned], axis=1))
-    block = lax.broadcasted_iota(jnp.int32, (BLOCK, HALF), 1) // BLOCK
+def outer_parts(p_ref, at, j, left, right):
+    lanes = lanes_of(j)
+    turned = jnp.concatenate([right[:, LANES:], -right[:, :LANES]], axis=1)
+    full = dot_t(left, jnp.concatenate([right, turned], axis=0))
+    sums = jnp.sum(right.astype(F32), axis=0, keepdims=True)
     for c in range(2):
-        part = full[:, c * HALF : (c + 1) * HALF]
-        packed = part[:BLOCK]
-        for j in range(1, HALF // BLOCK):
-            packed = jnp.where(block == j, part[j * BLOCK : (j + 1) * BLOCK], packed)
-        p_ref[at, c * BLOCK : (c + 1) * BLOCK] += packed
-    for c in range(2):
-        total = jnp.sum(right[c * rows : (c + 1) * rows].astype(F32), axis=0, keepdims=True)
-        p_ref[at, 2 * BLOCK + c : 2 * BLOCK + c + 1] += total
+        p_ref[at, c * BLOCK : (c + 1) * BLOCK, lanes] += full[:BLOCK, lanes_of(c)]
+        p_ref[at, 2 * BLOCK + c : 2 * BLOCK + c + 1, lanes] += sums[:, lanes_of(c)]
 
 
 def backward_kernel(at_ref, m_ref, wi_ref, wo_ref, s_ref, h_ref, d_ref, *refs):
@@ -387,26 +405,30 @@
 
     rows = slabs[0].shape[0] * CK
     v = jnp.concatenate([x[...].reshape(rows, HALF) for x in slabs], axis=0)
-    incoming = dot(m_ref[...], v).astype(BF16)
-    hidden_grad = dot(side_by_side(incoming), wo_ref[...])
-    pre_grad = (hidden_grad * d_ref[0]).astype(BF16)
-    outer_parts(p_ref, 0, s_ref[0], stacked(pre_grad))
-    outer_parts(p_ref, 1, h_ref[0], incoming)
-    g_ref[0] = stacked(dot(pre_grad, wi_ref[...]).astype(BF16))
+    incoming = dot(m_ref[...], padded(v)).astype(BF16)
+    blocks = []
+    for j in range(PER):
+        coming = parts_of(incoming, j)
+        pre_grad = (dot(coming, wo_ref[j]) * d_ref[0, j]).astype(BF16)
+        blocks.append(dot(pre_grad, wi_ref[j]).astype(BF16))
+        outer_parts(p_ref, 0, j, s_ref[0, :, lanes_of(j)], pre_grad)
+        outer_parts(p_ref, 1, j, h_ref[0, :, lanes_of(j)], coming)
+    g_ref[0] = joined(blocks)
 
     @pl.when(pl.program_id(0) == pl.num_programs(0) - 1)
     def _():
-        kept_ref[...] = p_ref[at_ref[4]]
-        sent_ref[...] = p_ref[1 - at_ref[4]]
+        kept_ref[...] = packed(p_ref[at_ref[4]])
+        sent_ref[...] = packed(p_ref[1 - at_ref[4]])
 
 
 def backward(rows, local, at, slabs, m, wi, wo, spectrum, hidden, slope):
     size = m.shape[0]
     slab = pl.BlockSpec((rows, CK, HALF), lambda s, at: (s, 0, 0))
     square = pl.BlockSpec((size, size), lambda s, at: (0, 0))
-    wide = pl.BlockSpec((2 * HALF, 2 * HALF), lambda s, at: (0, 0))
-    tall = pl.BlockSpec((1, size, HALF), lambda s, at: (s, 0, 0))
-    pair = pl.BlockSpec((1, size // 2, 2 * HALF), lambda s, at: (s, 0, 0))
+    wide = pl.BlockSpec((PER, 2 * LANES, 2 * LANES), lambda s, at: (0, 0, 0))
+    tall = pl.BlockSpec((1, size, PER * LANES), lambda s, at: (s, 0, 0))
+    given = pl.BlockSpec((1, size, HALF), lambda s, at: (s, 0, 0))
+    pair = pl.BlockSpec((1, PER, size // 2, 2 * LANES), lambda s, at: (s, 0, 0, 0))
     packet = pl.BlockSpec((PACK, HALF), lambda s, at: (0, 0))
     return pl.pallas_call(
         backward_kernel,
@@ -414,8 +436,8 @@
             num_scalar_prefetch=1,
             grid=(local,),
             in_specs=[square, wide, wide, tall, tall, pair] + [slab] * len(slabs),
-            out_specs=[tall, packet, packet],
-            scratch_shapes=[pltpu.VMEM((2, PACK, HALF), F32)],
+            out_specs=[given, packet, packet],
+            scratch_shapes=[pltpu.VMEM((2, PACK, PER * LANES), F32)],
         ),
         out_shape=[pltpu.HBM((local, size, HALF), BF16)] + [pltpu.HBM((PACK, HALF), F32)] * 2,
         compiler_params=params(40),
@@ -583,6 +605,10 @@
     incoming = apart(cot)
     matrix, matrix_x, base_x, in_fwd, in_bwd, out_fwd, out_bwd = prepare(
         at, base, in_weight, out_weight
+    )
+    in_bias, out_bias = (
+        jnp.pad(x.reshape(2, BLOCKS, BLOCK), ((0, 0), (0, 0), (0, LANES - BLOCK))).reshape(2, -1)
+        for x in (in_bias, out_bias)
     )
     back, spectrum, hidden, slope = forward(
         rows, local, at, received, matrix, base, in_fwd, out_fwd, in_bias, out_bias

time: 200 us -> 198 us (0.990)
  Pallas kernels: 52 us -> 49.9 us
  transfers between devices with their start and end apart: 35 -> 35, of which waited for: 15 -> 14; matrix products, arithmetic and copies ran while one was open for 0% -> 0% of each run, Pallas kernels for 17% -> 16%
where the time goes in v4:
time: 198 us; the launch traced here: 197 us
  starting transfers between devices  79 us (40%)
  waiting for transfers between devices  62.7 us (32%)
  Pallas kernels  49.9 us (25%)
  local copies, waits for them, and re-layouts  4.44 us (2%)
    ppermute x32, starting transfers between devices, swap(): return lax.ppermute(x, axis, [(i, i ^ bit) for i in range(size)])  59.5 us
    ppermute x32, waiting for transfers between devices, swap(): return lax.ppermute(x, axis, [(i, i ^ bit) for i in range(size)])  40.5 us
    all_to_all x3, waiting for transfers between devices, exchange(): lax.all_to_all(x.reshape((seq, -1) + x.shape[-2:]), 'seq', 0, 0, tiled=True)  22.2 us
    all_to_all x3, starting transfers between devices, exchange(): lax.all_to_all(x.reshape((seq, -1) + x.shape[-2:]), 'seq', 0, 0, tiled=True)  19.5 us
    pallas_call x1, Pallas kernels, forward(): pl.pallas_call(forward_kernel, grid_spec=pltpu.PrefetchScalarGridSpec(num...  10.3 us
    pallas_call x1, Pallas kernels, backward(): pl.pallas_call(backward_kernel, grid_spec=pltpu.PrefetchScalarGridSpec(nu...  9.1 us
    pallas_call x1, Pallas kernels, inverse_apart(): pl.pallas_call(inverse_apart_kernel, grid_spec=pltpu.PrefetchScalarGridSp...  5.59 us
    pallas_call x1, Pallas kernels, inverse(): pl.pallas_call(inverse_kernel, grid=(rows,), in_specs=[whole, pl.BlockSpe...  4.65 us
  transfers between devices with their start and end apart: 35, of which 14 were waited for; matrix products, arithmetic and copies ran while one was open for 0% of the time, Pallas kernels for 16%

profile of v4, /device:TPU:0, one launch (start us, length us, event | category | flops | bytes accessed | tf_op | source)
XLA Modules:
  0.0 197.1 jit_solution(8478722186315019356)
XLA Ops:
  0.6 3.8 %columns.1 = bf16[2,1,8,2,3,16,384]{6,5,4,3,2,1,0:T(8,128)(2,1)} custom-call(bf16[3,180,2,768]{3,2,1,0:T(2,128)(2,1)} %bitcast.52, bf16[256,360]{1,0:T(8,128)(2,1)} %constant.69.clone.t_ref), custom_call_target="tpu_custom_call" | custom-call | flops 600000000 | bytes 3000000 | tf_op jit(solution)/shard_map/columns/pallas_call | solution.py:113
  4.5 8.5 %all-to-all-start = ((bf16[16,6,16,384]{3,2,1,0:T(8,128)(2,1)}), bf16[16,6,16,384]{3,2,1,0:T(8,128)(2,1)S(1)}, u32[]{:S(2)}, u32[]{:S(2)}) async-start(bf16[16,6,16,384]{3,2,1,0:T(8,128)(2,1)} %bitcast.54), calls=%async_computation | async-start | bytes 2359296 | tf_op jit(solution)/shard_map/all_to_all | solution.py:589
  13.3 3.8 %prepare.1 = (bf16[768,768]{1,0:T(8,128)(2,1)}, bf16[768,768]{1,0:T(8,128)(2,1)}, bf16[16,48,768]{2,1,0:T(8,128)(2,1)}, bf16[4,256,256]{2,1,0:T(8,128)(2,1)}, bf...) custom-call(s32[5]{0:T(128)S(1)} %stack.68.at_ref, ...), custom_call_target="tpu_custom_call" | custom-call | flops 800000000 | bytes 4000000 | tf_op jit(solution)/shard_map/prepare/pallas_call | solution.py:280
  17.7 22.2 %all-to-all-done.v_ref = bf16[16,6,16,384]{3,2,1,0:T(8,128)(2,1)S(1)} async-done(((bf16[16,6,16,384]{3,2,1,0:T(8,128)(2,1)}), bf16[16,6,16,384]{3,2,1,0:T(8,128)(2,1)S(1)}, u32[]{:S(2)}, u32[]{:S(2)}) %all-to-all-start) | async-done | bytes 1179680 | tf_op jit(solution)/shard_map/all_to_all | solution.py:589
  40.9 10.3 %forward.1 = (bf16[16,6,16,384]{3,2,1,0:T(8,128)(2,1)}, bf16[2,768,512]{2,1,0:T(8,128)(2,1)}, bf16[2,768,512]{2,1,0:T(8,128)(2,1)}, f32[2,4,384,256]{3,2,1,0:T(8,128)}) custom-call(s32[5]{0:T(128)S(1)} %stack.68.at_ref, bf16[16,6,16,384]{3,2,1,0:T(8,128)(2,1)} %copy-done.11, bf16[768,768]{1,0:T(8,128)(2,1)} %get-tuple-element.71.m_ref, ...), custom_call_target="tpu_custom_call" | custom-call | flops 1800000000 | bytes 9000000 | tf_op jit(solution)/shard_map/forward/pallas_call | solution.py:366
  51.2 6.2 %all-to-all-start.1 = ((bf16[16,6,16,384]{3,2,1,0:T(8,128)(2,1)}), bf16[16,6,16,384]{3,2,1,0:T(8,128)(2,1)S(1)}, u32[]{:S(2)}, u32[]{:S(2)}) async-start(bf16[16,6,16,384]{3,2,1,0:T(8,128)(2,1)} %get-tuple-element.104), calls=%async_computation.1 | async-start | bytes 2359296 | tf_op jit(solution)/shard_map/all_to_all | solution.py:589
  57.4 4.5 %columns_apart.1 = (bf16[1,2,3,16,384]{4,3,2,1,0:T(8,128)(2,1)}, bf16[1,2,3,16,384]{4,3,2,1,0:T(8,128)(2,1)}, bf16[1,2,3,16,384]{4,3,2,1,0:T(8,128)(2,1)}, bf16[...) custom-call(s32[5]{0:T(128)S(1)} %stack.68.at_ref, ...), custom_call_target="tpu_custom_call" | custom-call | flops 600000000 | bytes 3000000 | tf_op jit(solution)/shard_map/columns_apart/pallas_call | solution.py:144
  68.8 2.4 %collective-permute-start.5 = (bf16[6,16,384]{2,1,0:T(8,128)(2,1)}, bf16[6,16,384]{2,1,0:T(8,128)(2,1)S(1)}, u32[]{:S(2)}, u32[]{:S(2)}) collective-permute-start(bf16[6,16,384]{2,1,0:T(8,128)(2,1)} %bitcast.104), channel_id=1, source_target_pairs={{0,12},{2,14},{4,8},{6,10},{8,4},{10,6},{12,0},{14,2},{16,28},{18,... | collective-permute-start | bytes 221192 | tf_op jit(solution)/shard_map/ppermute | solution.py:558
  72.8 3.0 %collective-permute-start.7 = (bf16[6,16,384]{2,1,0:T(8,128)(2,1)}, bf16[6,16,384]{2,1,0:T(8,128)(2,1)S(1)}, u32[]{:S(2)}, u32[]{:S(2)}) collective-permute-start(bf16[6,16,384]{2,1,0:T(8,128)(2,1)} %bitcast.102), channel_id=1, source_target_pairs={{0,16},{2,18},{4,20},{6,22},{8,24},{10,26},{12,28},{14,30},{16,0},... | collective-permute-start | bytes 221192 | tf_op jit(solution)/shard_map/ppermute | solution.py:558
  75.9 3.4 %collective-permute-done.3.refs_4_ = bf16[6,16,384]{2,1,0:T(8,128)(2,1)S(1)} collective-permute-done((bf16[6,16,384]{2,1,0:T(8,128)(2,1)}, bf16[6,16,384]{2,1,0:T(8,128)(2,1)S(1)}, u32[]{:S(2)}, u32[]{:S(2)}) %collective-permute-start.3) | collective-permute-done | bytes 73760 | tf_op jit(solution)/shard_map/ppermute | solution.py:558
  79.3 5.6 %collective-permute-start.8 = (bf16[6,16,384]{2,1,0:T(8,128)(2,1)}, bf16[6,16,384]{2,1,0:T(8,128)(2,1)S(1)}, u32[]{:S(2)}, u32[]{:S(2)}) collective-permute-start(bf16[6,16,384]{2,1,0:T(8,128)(2,1)} %bitcast.101), channel_id=1, source_target_pairs={{0,18},{2,16},{4,22},{6,20},{8,26},{10,24},{12,30},{14,28},{16,2},... | collective-permute-start | bytes 221192 | tf_op jit(solution)/shard_map/ppermute | solution.py:558
  84.9 2.5 %collective-permute-start.9 = (bf16[6,16,384]{2,1,0:T(8,128)(2,1)}, bf16[6,16,384]{2,1,0:T(8,128)(2,1)S(1)}, u32[]{:S(2)}, u32[]{:S(2)}) collective-permute-start(bf16[6,16,384]{2,1,0:T(8,128)(2,1)} %bitcast.100), channel_id=1, source_target_pairs={{0,20},{2,22},{4,16},{6,18},{8,28},{10,30},{12,24},{14,26},{16,4},... | collective-permute-start | bytes 221192 | tf_op jit(solution)/shard_map/ppermute | solution.py:558
  89.6 6.5 %collective-permute-done.7.refs_8_ = bf16[6,16,384]{2,1,0:T(8,128)(2,1)S(1)} collective-permute-done((bf16[6,16,384]{2,1,0:T(8,128)(2,1)}, bf16[6,16,384]{2,1,0:T(8,128)(2,1)S(1)}, u32[]{:S(2)}, u32[]{:S(2)}) %collective-permute-start.7) | collective-permute-done | bytes 73760 | tf_op jit(solution)/shard_map/ppermute | solution.py:558
  96.1 3.0 %collective-permute-start.12 = (bf16[6,16,384]{2,1,0:T(8,128)(2,1)}, bf16[6,16,384]{2,1,0:T(8,128)(2,1)S(1)}, u32[]{:S(2)}, u32[]{:S(2)}) collective-permute-start(bf16[6,16,384]{2,1,0:T(8,128)(2,1)} %bitcast.97), channel_id=1, source_target_pairs={{0,26},{2,24},{4,30},{6,28},{8,18},{10,16},{12,22},{14,20},{16,10}... | collective-permute-start | bytes 221192 | tf_op jit(solution)/shard_map/ppermute | solution.py:558
  99.1 2.9 %collective-permute-start.13 = (bf16[6,16,384]{2,1,0:T(8,128)(2,1)}, bf16[6,16,384]{2,1,0:T(8,128)(2,1)S(1)}, u32[]{:S(2)}, u32[]{:S(2)}) collective-permute-start(bf16[6,16,384]{2,1,0:T(8,128)(2,1)} %bitcast.96), channel_id=1, source_target_pairs={{0,28},{2,30},{4,24},{6,26},{8,20},{10,22},{12,16},{14,18},{16,12}... | collective-permute-start | bytes 221192 | tf_op jit(solution)/shard_map/ppermute | solution.py:558
  104.1 2.6 %collective-permute-done.13.refs_14_ = bf16[6,16,384]{2,1,0:T(8,128)(2,1)S(1)} collective-permute-done((bf16[6,16,384]{2,1,0:T(8,128)(2,1)}, bf16[6,16,384]{2,1,0:T(8,128)(2,1)S(1)}, u32[]{:S(2)}, u32[]{:S(2)}) %collective-permute-start.13) | collective-permute-done | bytes 73760 | tf_op jit(solution)/shard_map/ppermute | solution.py:558
  106.7 3.6 %collective-permute-done.14.refs_15_ = bf16[6,16,384]{2,1,0:T(8,128)(2,1)S(1)} collective-permute-done((bf16[6,16,384]{2,1,0:T(8,128)(2,1)}, bf16[6,16,384]{2,1,0:T(8,128)(2,1)S(1)}, u32[]{:S(2)}, u32[]{:S(2)}) %collective-permute-start.14) | collective-permute-done | bytes 73760 | tf_op jit(solution)/shard_map/ppermute | solution.py:558
  110.9 9.1 %backward.1 = (bf16[2,768,384]{2,1,0:T(8,128)(2,1)}, f32[256,384]{1,0:T(8,128)}, f32[256,384]{1,0:T(8,128)}) custom-call(s32[5]{0:T(128)S(1)} %stack.68.at_ref, bf16[768,768]{1,0:T(8,128)(2,1)} %get-tuple-element.68.m_ref, bf16[4,256,256]{2,1,0:T(8,128)(2,1)} %get-tuple-element.69.wi_ref, bf16[4,256,256]{2,1,0:T(8,128)(2,1)} %get-tuple-element.70.wo_ref, ...), custom_call_target="tpu_custom_call" | custom-call | flops 1800000000 | bytes 9000000 | tf_op jit(solution)/shard_map/backward/pallas_call | solution.py:433
  122.8 4.2 %rows_back.1 = (bf16[8,16,384]{2,1,0:T(8,128)(2,1)}, bf16[8,16,384]{2,1,0:T(8,128)(2,1)}, bf16[8,16,384]{2,1,0:T(8,128)(2,1)}, bf16[8,16,384]{2,1,0:T(8,128)(2,1...) custom-call(s32[5]{0:T(128)S(1)} %stack.68.at_ref, ...), custom_call_target="tpu_custom_call" | custom-call | flops 800000000 | bytes 4000000 | tf_op jit(solution)/shard_map/rows_back/pallas_call | solution.py:467
  127.9 2.7 %collective-permute-start.18 = (bf16[8,16,384]{2,1,0:T(8,128)(2,1)}, bf16[8,16,384]{2,1,0:T(8,128)(2,1)S(1)}, u32[]{:S(2)}, u32[]{:S(2)}) collective-permute-start(bf16[8,16,384]{2,1,0:T(8,128)(2,1)} %get-tuple-element.99), channel_id=1, source_target_pairs={{0,6},{2,4},{4,2},{6,0},{8,14},{10,12},{12,10},{14,8},{16,22},{18,... | collective-permute-start | bytes 294920 | tf_op jit(solution)/shard_map/ppermute | solution.py:558
  130.5 2.5 %collective-permute-start.19 = (bf16[8,16,384]{2,1,0:T(8,128)(2,1)}, bf16[8,16,384]{2,1,0:T(8,128)(2,1)S(1)}, u32[]{:S(2)}, u32[]{:S(2)}) collective-permute-start(bf16[8,16,384]{2,1,0:T(8,128)(2,1)} %get-tuple-element.100), channel_id=1, source_target_pairs={{0,8},{2,10},{4,12},{6,14},{8,0},{10,2},{12,4},{14,6},{16,24},{18,... | collective-permute-start | bytes 294920 | tf_op jit(solution)/shard_map/ppermute | solution.py:558
  136.9 2.9 %collective-permute-done.20.refs_10_.refs_11_ = bf16[8,16,384]{2,1,0:T(8,128)(2,1)S(1)} collective-permute-done((bf16[8,16,384]{2,1,0:T(8,128)(2,1)}, bf16[8,16,384]{2,1,0:T(8,128)(2,1)S(1)}, u32[]{:S(2)}, u32[]{:S(2)}) %collective-permute-start.20) | collective-permute-done | bytes 98336 | tf_op jit(solution)/shard_map/ppermute | solution.py:558
  144.3 4.8 %all-to-all-start.2 = ((bf16[16,2,16,384]{3,2,1,0:T(8,128)(2,1)}), bf16[16,2,16,384]{3,2,1,0:T(8,128)(2,1)S(1)}, u32[]{:S(2)}, u32[]{:S(2)}) async-start(bf16[16,2,16,384]{3,2,1,0:T(8,128)(2,1)} %totals.1), calls=%async_computation.2 | async-start | bytes 786432 | tf_op jit(solution)/shard_map/all_to_all | solution.py:589
  149.1 2.9 %collective-permute-start.23 = (bf16[6,16,384]{2,1,0:T(8,128)(2,1)S(1)}, bf16[6,16,384]{2,1,0:T(8,128)(2,1)S(1)}, u32[]{:S(2)}, u32[]{:S(2)}) collective-permute-start(bf16[6,16,384]{2,1,0:T(8,128)(2,1)S(1)} %copy-done.45), channel_id=1, source_target_pairs={{0,16},{2,18},{4,20},{6,22},{8,24},{10,26},{12,28},{14,30},{16,0},... | collective-permute-start | bytes 221192 | tf_op jit(solution)/shard_map/ppermute | solution.py:558
  153.5 3.3 %collective-permute-start.25 = (bf16[6,16,384]{2,1,0:T(8,128)(2,1)S(1)}, bf16[6,16,384]{2,1,0:T(8,128)(2,1)S(1)}, u32[]{:S(2)}, u32[]{:S(2)}) collective-permute-start(bf16[6,16,384]{2,1,0:T(8,128)(2,1)S(1)} %copy-done.43), channel_id=1, source_target_pairs={{0,20},{2,22},{4,16},{6,18},{8,28},{10,30},{12,24},{14,26},{16,4},... | collective-permute-start | bytes 221192 | tf_op jit(solution)/shard_map/ppermute | solution.py:558
  156.8 3.7 %collective-permute-start.27 = (bf16[6,16,384]{2,1,0:T(8,128)(2,1)S(1)}, bf16[6,16,384]{2,1,0:T(8,128)(2,1)S(1)}, u32[]{:S(2)}, u32[]{:S(2)}) collective-permute-start(bf16[6,16,384]{2,1,0:T(8,128)(2,1)S(1)} %copy-done.41), channel_id=1, source_target_pairs={{0,24},{2,26},{4,28},{6,30},{8,16},{10,18},{12,20},{14,22},{16,8},... | collective-permute-start | bytes 221192 | tf_op jit(solution)/shard_map/ppermute | solution.py:558
  160.5 9.8 %collective-permute-done.23 = bf16[6,16,384]{2,1,0:T(8,128)(2,1)S(1)} collective-permute-done((bf16[6,16,384]{2,1,0:T(8,128)(2,1)S(1)}, bf16[6,16,384]{2,1,0:T(8,128)(2,1)S(1)}, u32[]{:S(2)}, u32[]{:S(2)}) %collective-permute-start.23) | collective-permute-done | bytes 73760 | tf_op jit(solution)/shard_map/ppermute | solution.py:558
  173.6 2.2 %collective-permute-start.29 = (bf16[6,16,384]{2,1,0:T(8,128)(2,1)S(1)}, bf16[6,16,384]{2,1,0:T(8,128)(2,1)S(1)}, u32[]{:S(2)}, u32[]{:S(2)}) collective-permute-start(bf16[6,16,384]{2,1,0:T(8,128)(2,1)S(1)} %copy-done.39), channel_id=1, source_target_pairs={{0,28},{2,30},{4,24},{6,26},{8,20},{10,22},{12,16},{14,18},{16,12}... | collective-permute-start | bytes 221192 | tf_op jit(solution)/shard_map/ppermute | solution.py:558
  177.6 3.3 %collective-permute-done.26 = bf16[6,16,384]{2,1,0:T(8,128)(2,1)S(1)} collective-permute-done((bf16[6,16,384]{2,1,0:T(8,128)(2,1)S(1)}, bf16[6,16,384]{2,1,0:T(8,128)(2,1)S(1)}, u32[]{:S(2)}, u32[]{:S(2)}) %collective-permute-start.26) | collective-permute-done | bytes 73760 | tf_op jit(solution)/shard_map/ppermute | solution.py:558
  180.9 3.0 %collective-permute-done.30 = bf16[6,16,384]{2,1,0:T(8,128)(2,1)S(1)} collective-permute-done((bf16[6,16,384]{2,1,0:T(8,128)(2,1)S(1)}, bf16[6,16,384]{2,1,0:T(8,128)(2,1)S(1)}, u32[]{:S(2)}, u32[]{:S(2)}) %collective-permute-start.30) | collective-permute-done | bytes 73760 | tf_op jit(solution)/shard_map/ppermute | solution.py:558
  184.6 5.6 %inverse_apart.1 = bf16[3,180,2,768]{3,2,1,0:T(2,128)(2,1)} custom-call(s32[5]{0:T(128)S(1)} %stack.68.at_ref, bf16[3,180,2,768]{3,2,1,0:T(2,128)(2,1)} %bitcast.57, bf16[360,256]{1,0:T(8,128)(2,1)} %constant.72.clone.t_ref, bf16[1,8,16,384]{3,2,1,0:T(8,128)(2,1)} %bitcast.60, bf16[1,8,16,384]{3,2,1,0:T(8,128)(2,1)} %bitcast.61, ...), custom_call_target="tpu_custom_call" | custom-call | flops 800000000 | bytes 4000000 | tf_op jit(solution)/shard_map/inverse_apart/pallas_call | solution.py:223
  190.3 4.6 %inverse.1 = bf16[3,180,2,768]{3,2,1,0:T(2,128)(2,1)} custom-call(bf16[3,180,2,768]{3,2,1,0:T(2,128)(2,1)} %bitcast.53, bf16[360,256]{1,0:T(8,128)(2,1)} %constant.71.clone.t_ref, bf16[2,1,8,2,3,16,384]{6,5,4,3,2,1,0:T(8,128)(2,1)} %bitcast.55), custom_call_target="tpu_custom_call" | custom-call | flops 800000000 | bytes 4000000 | tf_op jit(solution)/shard_map/inverse/pallas_call | solution.py:190
  (146 shorter events, 36.6 us)
Async XLA Ops:
  4.5 35.4 %all-to-all-start = ((bf16[16,6,16,384]{3,2,1,0:T(8,128)(2,1)}), bf16[16,6,16,384]{3,2,1,0:T(8,128)(2,1)S(1)}, u32[]{:S(2)}, u32[]{:S(2)}) async-start(bf16[16,6,16,384]{3,2,1,0:T(8,128)(2,1)} %bitcast.54), calls=%async_computation | async-start | bytes 2359296 | tf_op jit(solution)/shard_map/all_to_all | solution.py:589
  51.2 90.7 %all-to-all-start.1 = ((bf16[16,6,16,384]{3,2,1,0:T(8,128)(2,1)}), bf16[16,6,16,384]{3,2,1,0:T(8,128)(2,1)S(1)}, u32[]{:S(2)}, u32[]{:S(2)}) async-start(bf16[16,6,16,384]{3,2,1,0:T(8,128)(2,1)} %get-tuple-element.104), calls=%async_computation.1 | async-start | bytes 2359296 | tf_op jit(solution)/shard_map/all_to_all | solution.py:589
  61.9 6.9 %collective-permute-start = (bf16[6,16,384]{2,1,0:T(8,128)(2,1)}, bf16[6,16,384]{2,1,0:T(8,128)(2,1)S(1)}, u32[]{:S(2)}, u32[]{:S(2)}) collective-permute-start(bf16[6,16,384]{2,1,0:T(8,128)(2,1)} %bitcast.109), channel_id=1, source_target_pairs={{0,2},{2,0},{4,6},{6,4},{8,10},{10,8},{12,14},{14,12},{16,18},{18,... | collective-permute-start | bytes 221192 | tf_op jit(solution)/shard_map/ppermute | solution.py:558
  63.9 7.3 %collective-permute-start.1 = (bf16[6,16,384]{2,1,0:T(8,128)(2,1)}, bf16[6,16,384]{2,1,0:T(8,128)(2,1)S(1)}, u32[]{:S(2)}, u32[]{:S(2)}) collective-permute-start(bf16[6,16,384]{2,1,0:T(8,128)(2,1)} %bitcast.108), channel_id=1, source_target_pairs={{0,4},{2,6},{4,0},{6,2},{8,12},{10,14},{12,8},{14,10},{16,20},{18,... | collective-permute-start | bytes 221192 | tf_op jit(solution)/shard_map/ppermute | solution.py:558
  65.4 7.5 %collective-permute-start.2 = (bf16[6,16,384]{2,1,0:T(8,128)(2,1)}, bf16[6,16,384]{2,1,0:T(8,128)(2,1)S(1)}, u32[]{:S(2)}, u32[]{:S(2)}) collective-permute-start(bf16[6,16,384]{2,1,0:T(8,128)(2,1)} %bitcast.107), channel_id=1, source_target_pairs={{0,6},{2,4},{4,2},{6,0},{8,14},{10,12},{12,10},{14,8},{16,22},{18,... | collective-permute-start | bytes 221192 | tf_op jit(solution)/shard_map/ppermute | solution.py:558
  65.5 13.8 %collective-permute-start.3 = (bf16[6,16,384]{2,1,0:T(8,128)(2,1)}, bf16[6,16,384]{2,1,0:T(8,128)(2,1)S(1)}, u32[]{:S(2)}, u32[]{:S(2)}) collective-permute-start(bf16[6,16,384]{2,1,0:T(8,128)(2,1)} %bitcast.106), channel_id=1, source_target_pairs={{0,8},{2,10},{4,12},{6,14},{8,0},{10,2},{12,4},{14,6},{16,24},{18,... | collective-permute-start | bytes 221192 | tf_op jit(solution)/shard_map/ppermute | solution.py:558
  67.4 17.6 %collective-permute-start.4 = (bf16[6,16,384]{2,1,0:T(8,128)(2,1)}, bf16[6,16,384]{2,1,0:T(8,128)(2,1)S(1)}, u32[]{:S(2)}, u32[]{:S(2)}) collective-permute-start(bf16[6,16,384]{2,1,0:T(8,128)(2,1)} %bitcast.105), channel_id=1, source_target_pairs={{0,10},{2,8},{4,14},{6,12},{8,2},{10,0},{12,6},{14,4},{16,26},{18,... | collective-permute-start | bytes 221192 | tf_op jit(solution)/shard_map/ppermute | solution.py:558
  68.8 18.6 %collective-permute-start.5 = (bf16[6,16,384]{2,1,0:T(8,128)(2,1)}, bf16[6,16,384]{2,1,0:T(8,128)(2,1)S(1)}, u32[]{:S(2)}, u32[]{:S(2)}) collective-permute-start(bf16[6,16,384]{2,1,0:T(8,128)(2,1)} %bitcast.104), channel_id=1, source_target_pairs={{0,12},{2,14},{4,8},{6,10},{8,4},{10,6},{12,0},{14,2},{16,28},{18,... | collective-permute-start | bytes 221192 | tf_op jit(solution)/shard_map/ppermute | solution.py:558
  71.2 17.8 %collective-permute-start.6 = (bf16[6,16,384]{2,1,0:T(8,128)(2,1)}, bf16[6,16,384]{2,1,0:T(8,128)(2,1)S(1)}, u32[]{:S(2)}, u32[]{:S(2)}) collective-permute-start(bf16[6,16,384]{2,1,0:T(8,128)(2,1)} %bitcast.103), channel_id=1, source_target_pairs={{0,14},{2,12},{4,10},{6,8},{8,6},{10,4},{12,2},{14,0},{16,30},{18,... | collective-permute-start | bytes 221192 | tf_op jit(solution)/shard_map/ppermute | solution.py:558
  72.8 23.3 %collective-permute-start.7 = (bf16[6,16,384]{2,1,0:T(8,128)(2,1)}, bf16[6,16,384]{2,1,0:T(8,128)(2,1)S(1)}, u32[]{:S(2)}, u32[]{:S(2)}) collective-permute-start(bf16[6,16,384]{2,1,0:T(8,128)(2,1)} %bitcast.102), channel_id=1, source_target_pairs={{0,16},{2,18},{4,20},{6,22},{8,24},{10,26},{12,28},{14,30},{16,0},... | collective-permute-start | bytes 221192 | tf_op jit(solution)/shard_map/ppermute | solution.py:558
  79.3 19.8 %collective-permute-start.8 = (bf16[6,16,384]{2,1,0:T(8,128)(2,1)}, bf16[6,16,384]{2,1,0:T(8,128)(2,1)S(1)}, u32[]{:S(2)}, u32[]{:S(2)}) collective-permute-start(bf16[6,16,384]{2,1,0:T(8,128)(2,1)} %bitcast.101), channel_id=1, source_target_pairs={{0,18},{2,16},{4,22},{6,20},{8,26},{10,24},{12,30},{14,28},{16,2},... | collective-permute-start | bytes 221192 | tf_op jit(solution)/shard_map/ppermute | solution.py:558
  84.9 17.1 %collective-permute-start.9 = (bf16[6,16,384]{2,1,0:T(8,128)(2,1)}, bf16[6,16,384]{2,1,0:T(8,128)(2,1)S(1)}, u32[]{:S(2)}, u32[]{:S(2)}) collective-permute-start(bf16[6,16,384]{2,1,0:T(8,128)(2,1)} %bitcast.100), channel_id=1, source_target_pairs={{0,20},{2,22},{4,16},{6,18},{8,28},{10,30},{12,24},{14,26},{16,4},... | collective-permute-start | bytes 221192 | tf_op jit(solution)/shard_map/ppermute | solution.py:558
  87.5 16.5 %collective-permute-start.10 = (bf16[6,16,384]{2,1,0:T(8,128)(2,1)}, bf16[6,16,384]{2,1,0:T(8,128)(2,1)S(1)}, u32[]{:S(2)}, u32[]{:S(2)}) collective-permute-start(bf16[6,16,384]{2,1,0:T(8,128)(2,1)} %bitcast.99), channel_id=1, source_target_pairs={{0,22},{2,20},{4,18},{6,16},{8,30},{10,28},{12,26},{14,24},{16,6},... | collective-permute-start | bytes 221192 | tf_op jit(solution)/shard_map/ppermute | solution.py:558
  89.0 15.0 %collective-permute-start.11 = (bf16[6,16,384]{2,1,0:T(8,128)(2,1)}, bf16[6,16,384]{2,1,0:T(8,128)(2,1)S(1)}, u32[]{:S(2)}, u32[]{:S(2)}) collective-permute-start(bf16[6,16,384]{2,1,0:T(8,128)(2,1)} %bitcast.98), channel_id=1, source_target_pairs={{0,24},{2,26},{4,28},{6,30},{8,16},{10,18},{12,20},{14,22},{16,8},... | collective-permute-start | bytes 221192 | tf_op jit(solution)/shard_map/ppermute | solution.py:558
  96.1 7.9 %collective-permute-start.12 = (bf16[6,16,384]{2,1,0:T(8,128)(2,1)}, bf16[6,16,384]{2,1,0:T(8,128)(2,1)S(1)}, u32[]{:S(2)}, u32[]{:S(2)}) collective-permute-start(bf16[6,16,384]{2,1,0:T(8,128)(2,1)} %bitcast.97), channel_id=1, source_target_pairs={{0,26},{2,24},{4,30},{6,28},{8,18},{10,16},{12,22},{14,20},{16,10}... | collective-permute-start | bytes 221192 | tf_op jit(solution)/shard_map/ppermute | solution.py:558
  99.1 7.5 %collective-permute-start.13 = (bf16[6,16,384]{2,1,0:T(8,128)(2,1)}, bf16[6,16,384]{2,1,0:T(8,128)(2,1)S(1)}, u32[]{:S(2)}, u32[]{:S(2)}) collective-permute-start(bf16[6,16,384]{2,1,0:T(8,128)(2,1)} %bitcast.96), channel_id=1, source_target_pairs={{0,28},{2,30},{4,24},{6,26},{8,20},{10,22},{12,16},{14,18},{16,12}... | collective-permute-start | bytes 221192 | tf_op jit(solution)/shard_map/ppermute | solution.py:558
  102.1 8.3 %collective-permute-start.14 = (bf16[6,16,384]{2,1,0:T(8,128)(2,1)}, bf16[6,16,384]{2,1,0:T(8,128)(2,1)S(1)}, u32[]{:S(2)}, u32[]{:S(2)}) collective-permute-start(bf16[6,16,384]{2,1,0:T(8,128)(2,1)} %bitcast.95), channel_id=1, source_target_pairs={{0,30},{2,28},{4,26},{6,24},{8,22},{10,20},{12,18},{14,16},{16,14}... | collective-permute-start | bytes 221192 | tf_op jit(solution)/shard_map/ppermute | solution.py:558
  127.6 7.3 %collective-permute-start.17 = (bf16[8,16,384]{2,1,0:T(8,128)(2,1)}, bf16[8,16,384]{2,1,0:T(8,128)(2,1)S(1)}, u32[]{:S(2)}, u32[]{:S(2)}) collective-permute-start(bf16[8,16,384]{2,1,0:T(8,128)(2,1)} %get-tuple-element.98), channel_id=1, source_target_pairs={{0,4},{2,6},{4,0},{6,2},{8,12},{10,14},{12,8},{14,10},{16,20},{18,... | collective-permute-start | bytes 294920 | tf_op jit(solution)/shard_map/ppermute | solution.py:558
  127.9 9.0 %collective-permute-start.18 = (bf16[8,16,384]{2,1,0:T(8,128)(2,1)}, bf16[8,16,384]{2,1,0:T(8,128)(2,1)S(1)}, u32[]{:S(2)}, u32[]{:S(2)}) collective-permute-start(bf16[8,16,384]{2,1,0:T(8,128)(2,1)} %get-tuple-element.99), channel_id=1, source_target_pairs={{0,6},{2,4},{4,2},{6,0},{8,14},{10,12},{12,10},{14,8},{16,22},{18,... | collective-permute-start | bytes 294920 | tf_op jit(solution)/shard_map/ppermute | solution.py:558
  130.5 6.4 %collective-permute-start.19 = (bf16[8,16,384]{2,1,0:T(8,128)(2,1)}, bf16[8,16,384]{2,1,0:T(8,128)(2,1)S(1)}, u32[]{:S(2)}, u32[]{:S(2)}) collective-permute-start(bf16[8,16,384]{2,1,0:T(8,128)(2,1)} %get-tuple-element.100), channel_id=1, source_target_pairs={{0,8},{2,10},{4,12},{6,14},{8,0},{10,2},{12,4},{14,6},{16,24},{18,... | collective-permute-start | bytes 294920 | tf_op jit(solution)/shard_map/ppermute | solution.py:558
  133.0 6.8 %collective-permute-start.20 = (bf16[8,16,384]{2,1,0:T(8,128)(2,1)}, bf16[8,16,384]{2,1,0:T(8,128)(2,1)S(1)}, u32[]{:S(2)}, u32[]{:S(2)}) collective-permute-start(bf16[8,16,384]{2,1,0:T(8,128)(2,1)} %get-tuple-element.101), channel_id=1, source_target_pairs={{0,10},{2,8},{4,14},{6,12},{8,2},{10,0},{12,6},{14,4},{16,26},{18,... | collective-permute-start | bytes 294920 | tf_op jit(solution)/shard_map/ppermute | solution.py:558
  133.0 7.7 %collective-permute-start.21 = (bf16[8,16,384]{2,1,0:T(8,128)(2,1)}, bf16[8,16,384]{2,1,0:T(8,128)(2,1)S(1)}, u32[]{:S(2)}, u32[]{:S(2)}) collective-permute-start(bf16[8,16,384]{2,1,0:T(8,128)(2,1)} %get-tuple-element.102), channel_id=1, source_target_pairs={{0,12},{2,14},{4,8},{6,10},{8,4},{10,6},{12,0},{14,2},{16,28},{18,... | collective-permute-start | bytes 294920 | tf_op jit(solution)/shard_map/ppermute | solution.py:558
  134.9 7.0 %collective-permute-start.22 = (bf16[8,16,384]{2,1,0:T(8,128)(2,1)}, bf16[8,16,384]{2,1,0:T(8,128)(2,1)S(1)}, u32[]{:S(2)}, u32[]{:S(2)}) collective-permute-start(bf16[8,16,384]{2,1,0:T(8,128)(2,1)} %get-tuple-element.103), channel_id=1, source_target_pairs={{0,14},{2,12},{4,10},{6,8},{8,6},{10,4},{12,2},{14,0},{16,30},{18,... | collective-permute-start | bytes 294920 | tf_op jit(solution)/shard_map/ppermute | solution.py:558
  144.3 45.9 %all-to-all-start.2 = ((bf16[16,2,16,384]{3,2,1,0:T(8,128)(2,1)}), bf16[16,2,16,384]{3,2,1,0:T(8,128)(2,1)S(1)}, u32[]{:S(2)}, u32[]{:S(2)}) async-start(bf16[16,2,16,384]{3,2,1,0:T(8,128)(2,1)} %totals.1), calls=%async_computation.2 | async-start | bytes 786432 | tf_op jit(solution)/shard_map/all_to_all | solution.py:589
  149.1 21.2 %collective-permute-start.23 = (bf16[6,16,384]{2,1,0:T(8,128)(2,1)S(1)}, bf16[6,16,384]{2,1,0:T(8,128)(2,1)S(1)}, u32[]{:S(2)}, u32[]{:S(2)}) collective-permute-start(bf16[6,16,384]{2,1,0:T(8,128)(2,1)S(1)} %copy-done.45), channel_id=1, source_target_pairs={{0,16},{2,18},{4,20},{6,22},{8,24},{10,26},{12,28},{14,30},{16,0},... | collective-permute-start | bytes 221192 | tf_op jit(solution)/shard_map/ppermute | solution.py:558
  152.0 21.6 %collective-permute-start.24 = (bf16[6,16,384]{2,1,0:T(8,128)(2,1)S(1)}, bf16[6,16,384]{2,1,0:T(8,128)(2,1)S(1)}, u32[]{:S(2)}, u32[]{:S(2)}) collective-permute-start(bf16[6,16,384]{2,1,0:T(8,128)(2,1)S(1)} %copy-done.44), channel_id=1, source_target_pairs={{0,18},{2,16},{4,22},{6,20},{8,26},{10,24},{12,30},{14,28},{16,2},... | collective-permute-start | bytes 221192 | tf_op jit(solution)/shard_map/ppermute | solution.py:558
  153.5 22.4 %collective-permute-start.25 = (bf16[6,16,384]{2,1,0:T(8,128)(2,1)S(1)}, bf16[6,16,384]{2,1,0:T(8,128)(2,1)S(1)}, u32[]{:S(2)}, u32[]{:S(2)}) collective-permute-start(bf16[6,16,384]{2,1,0:T(8,128)(2,1)S(1)} %copy-done.43), channel_id=1, source_target_pairs={{0,20},{2,22},{4,16},{6,18},{8,28},{10,30},{12,24},{14,26},{16,4},... | collective-permute-start | bytes 221192 | tf_op jit(solution)/shard_map/ppermute | solution.py:558
  156.7 24.1 %collective-permute-start.26 = (bf16[6,16,384]{2,1,0:T(8,128)(2,1)S(1)}, bf16[6,16,384]{2,1,0:T(8,128)(2,1)S(1)}, u32[]{:S(2)}, u32[]{:S(2)}) collective-permute-start(bf16[6,16,384]{2,1,0:T(8,128)(2,1)S(1)} %copy-done.42), channel_id=1, source_target_pairs={{0,22},{2,20},{4,18},{6,16},{8,30},{10,28},{12,26},{14,24},{16,6},... | collective-permute-start | bytes 221192 | tf_op jit(solution)/shard_map/ppermute | solution.py:558
  156.8 24.0 %collective-permute-start.27 = (bf16[6,16,384]{2,1,0:T(8,128)(2,1)S(1)}, bf16[6,16,384]{2,1,0:T(8,128)(2,1)S(1)}, u32[]{:S(2)}, u32[]{:S(2)}) collective-permute-start(bf16[6,16,384]{2,1,0:T(8,128)(2,1)S(1)} %copy-done.41), channel_id=1, source_target_pairs={{0,24},{2,26},{4,28},{6,30},{8,16},{10,18},{12,20},{14,22},{16,8},... | collective-permute-start | bytes 221192 | tf_op jit(solution)/shard_map/ppermute | solution.py:558
  170.3 10.5 %collective-permute-start.28 = (bf16[6,16,384]{2,1,0:T(8,128)(2,1)S(1)}, bf16[6,16,384]{2,1,0:T(8,128)(2,1)S(1)}, u32[]{:S(2)}, u32[]{:S(2)}) collective-permute-start(bf16[6,16,384]{2,1,0:T(8,128)(2,1)S(1)} %copy-done.40), channel_id=1, source_target_pairs={{0,26},{2,24},{4,30},{6,28},{8,18},{10,16},{12,22},{14,20},{16,10}... | collective-permute-start | bytes 221192 | tf_op jit(solution)/shard_map/ppermute | solution.py:558
  173.6 7.3 %collective-permute-start.29 = (bf16[6,16,384]{2,1,0:T(8,128)(2,1)S(1)}, bf16[6,16,384]{2,1,0:T(8,128)(2,1)S(1)}, u32[]{:S(2)}, u32[]{:S(2)}) collective-permute-start(bf16[6,16,384]{2,1,0:T(8,128)(2,1)S(1)} %copy-done.39), channel_id=1, source_target_pairs={{0,28},{2,30},{4,24},{6,26},{8,20},{10,22},{12,16},{14,18},{16,12}... | collective-permute-start | bytes 221192 | tf_op jit(solution)/shard_map/ppermute | solution.py:558
  175.8 8.1 %collective-permute-start.30 = (bf16[6,16,384]{2,1,0:T(8,128)(2,1)S(1)}, bf16[6,16,384]{2,1,0:T(8,128)(2,1)S(1)}, u32[]{:S(2)}, u32[]{:S(2)}) collective-permute-start(bf16[6,16,384]{2,1,0:T(8,128)(2,1)S(1)} %copy-done.38), channel_id=1, source_target_pairs={{0,30},{2,28},{4,26},{6,24},{8,22},{10,20},{12,18},{14,16},{16,14}... | collective-permute-start | bytes 221192 | tf_op jit(solution)/shard_map/ppermute | solution.py:558
  (49 other events, 559.2 us)

commit v5 on v4

--- a/solution.py
+++ b/solution.py
@@ -199,42 +199,38 @@
     )(*far(x, table, z))
 
 
-def inverse_apart_kernel(at_ref, x_ref, t_ref, *refs):
+def inverse_apart_kernel(local, at_ref, x_ref, t_ref, *refs):
     *slabs, o_ref, z_ref = refs
-    split, local = slabs[0].shape[0], len(slabs) // (HALVES * GROUPS)
+    split = slabs[0].shape[0]
+    row, rows = pl.program_id(0), pl.num_programs(0)
     for s in range(split * local):
         for a in range(HALVES):
             lanes = half_lanes(a ^ at_ref[1])
             for b in range(GROUPS):
-                slab = slabs[(GROUPS * a + b) * local + s % local]
-                tile = slab[(s // local) ^ at_ref[2], 0]
+                slab = slabs[GROUPS * a + b]
+                tile = slab[(s // local) ^ at_ref[2], (s % local) * rows + row]
                 z_ref[s * GROUPS + (b ^ at_ref[3]), :, lanes] = tile
     add_modes(o_ref, x_ref, t_ref, z_ref[...].reshape(t_ref.shape[1], x_ref.shape[3]))
 
 
 def inverse_apart(at, x, table, slabs, dims):
     rows, width, samples, channels = x.shape
-    split, local = dims
     whole = pl.BlockSpec((1, width, samples, channels), lambda h, at: (h, 0, 0, 0))
-    slab = [
-        pl.BlockSpec((split, 1, CK, HALF), lambda h, at, l=l: (0, l * rows + h, 0, 0))
-        for l in range(local)
-    ]
-    return pl.pallas_call(
-        inverse_apart_kernel,
+    return pl.pallas_call(
+        functools.partial(inverse_apart_kernel, dims[1]),
         grid_spec=pltpu.PrefetchScalarGridSpec(
             num_scalar_prefetch=1,
             grid=(rows,),
             in_specs=[whole, pl.BlockSpec(table.shape, lambda h, at: (0, 0))]
-            + slab * len(slabs),
+            + [pl.BlockSpec(y.shape, lambda h, at: (0, 0, 0, 0)) for y in slabs],
             out_specs=whole,
             scratch_shapes=[pltpu.VMEM((samples * GROUPS, CK, channels), BF16)],
         ),
         out_shape=pltpu.HBM(x.shape, BF16),
-        compiler_params=params(16),
+        compiler_params=params(20),
         cost_estimate=cost(4),
         name="inverse_apart",
-    )(at, *far(x, table), *[y for y in far(*slabs) for _ in range(local)])
+    )(at, *far(x, table, *slabs))
 
 
 def transposed(out_ref, blocks):
@@ -449,11 +445,12 @@
 def rows_back_kernel(at_ref, n_ref, g_ref, kept_ref, other_ref, *outs):
     blocks, rows, size = n_ref.shape
     local = g_ref.shape[0]
+    both = jnp.concatenate([g_ref[s] for s in range(local)], axis=1)
+    back = dot(n_ref[...].reshape(blocks * rows, size), both).astype(BF16)
     for s in range(local):
-        back = dot(n_ref[...].reshape(blocks * rows, size), g_ref[s]).astype(BF16)
-        back = back.reshape(blocks, rows // CK, CK, HALF)
+        part = back[:, s * HALF : (s + 1) * HALF].reshape(blocks, rows // CK, CK, HALF)
         for r in range(blocks):
-            outs[r][s * rows // CK : (s + 1) * rows // CK] = back[r]
+            outs[r][s * rows // CK : (s + 1) * rows // CK] = part[r]
     tiles = local * rows // CK
     for r in range(blocks // HALVES):
         to = (r ^ at_ref[0]) % (blocks // HALVES)

time: 198 us -> 198 us (level)
  no operation moved by 1% of the time
where the time goes in v5:
time: 198 us; the launch traced here: 197 us
  starting transfers between devices  79 us (40%)
  waiting for transfers between devices  62.7 us (32%)
  Pallas kernels  49.5 us (25%)
  local copies, waits for them, and re-layouts  4.44 us (2%)
    ppermute x32, starting transfers between devices, swap(): return lax.ppermute(x, axis, [(i, i ^ bit) for i in range(size)])  59.5 us
    ppermute x32, waiting for transfers between devices, swap(): return lax.ppermute(x, axis, [(i, i ^ bit) for i in range(size)])  40.5 us
    all_to_all x3, waiting for transfers between devices, exchange(): lax.all_to_all(x.reshape((seq, -1) + x.shape[-2:]), 'seq', 0, 0, tiled=True)  22.2 us
    all_to_all x3, starting transfers between devices, exchange(): lax.all_to_all(x.reshape((seq, -1) + x.shape[-2:]), 'seq', 0, 0, tiled=True)  19.5 us
    pallas_call x1, Pallas kernels, forward(): pl.pallas_call(forward_kernel, grid_spec=pltpu.PrefetchScalarGridSpec(num...  10.3 us
    pallas_call x1, Pallas kernels, backward(): pl.pallas_call(backward_kernel, grid_spec=pltpu.PrefetchScalarGridSpec(nu...  9.1 us
    pallas_call x1, Pallas kernels, inverse_apart(): pl.pallas_call(functools.partial(inverse_apart_kernel, dims[1]), grid_spe...  5.49 us
    pallas_call x1, Pallas kernels, inverse(): pl.pallas_call(inverse_kernel, grid=(rows,), in_specs=[whole, pl.BlockSpe...  4.65 us
  transfers between devices with their start and end apart: 35, of which 14 were waited for; matrix products, arithmetic and copies ran while one was open for 0% of the time, Pallas kernels for 16%

profile of v5, /device:TPU:0, one launch (start us, length us, event | category | flops | bytes accessed | tf_op | source)
XLA Modules:
  0.0 196.7 jit_solution(3198223195092562562)
XLA Ops:
  0.6 3.8 %columns.1 = bf16[2,1,8,2,3,16,384]{6,5,4,3,2,1,0:T(8,128)(2,1)} custom-call(bf16[3,180,2,768]{3,2,1,0:T(2,128)(2,1)} %bitcast.52, bf16[256,360]{1,0:T(8,128)(2,1)} %constant.69.clone.t_ref), custom_call_target="tpu_custom_call" | custom-call | flops 600000000 | bytes 3000000 | tf_op jit(solution)/shard_map/columns/pallas_call | solution.py:113
  4.5 8.5 %all-to-all-start = ((bf16[16,6,16,384]{3,2,1,0:T(8,128)(2,1)}), bf16[16,6,16,384]{3,2,1,0:T(8,128)(2,1)S(1)}, u32[]{:S(2)}, u32[]{:S(2)}) async-start(bf16[16,6,16,384]{3,2,1,0:T(8,128)(2,1)} %bitcast.54), calls=%async_computation | async-start | bytes 2359296 | tf_op jit(solution)/shard_map/all_to_all | solution.py:586
  13.3 3.8 %prepare.1 = (bf16[768,768]{1,0:T(8,128)(2,1)}, bf16[768,768]{1,0:T(8,128)(2,1)}, bf16[16,48,768]{2,1,0:T(8,128)(2,1)}, bf16[4,256,256]{2,1,0:T(8,128)(2,1)}, bf...) custom-call(s32[5]{0:T(128)S(1)} %stack.68.at_ref, ...), custom_call_target="tpu_custom_call" | custom-call | flops 800000000 | bytes 4000000 | tf_op jit(solution)/shard_map/prepare/pallas_call | solution.py:276
  17.7 22.2 %all-to-all-done.v_ref = bf16[16,6,16,384]{3,2,1,0:T(8,128)(2,1)S(1)} async-done(((bf16[16,6,16,384]{3,2,1,0:T(8,128)(2,1)}), bf16[16,6,16,384]{3,2,1,0:T(8,128)(2,1)S(1)}, u32[]{:S(2)}, u32[]{:S(2)}) %all-to-all-start) | async-done | bytes 1179680 | tf_op jit(solution)/shard_map/all_to_all | solution.py:586
  40.9 10.3 %forward.1 = (bf16[16,6,16,384]{3,2,1,0:T(8,128)(2,1)}, bf16[2,768,512]{2,1,0:T(8,128)(2,1)}, bf16[2,768,512]{2,1,0:T(8,128)(2,1)}, f32[2,4,384,256]{3,2,1,0:T(8,128)}) custom-call(s32[5]{0:T(128)S(1)} %stack.68.at_ref, bf16[16,6,16,384]{3,2,1,0:T(8,128)(2,1)} %copy-done.4, bf16[768,768]{1,0:T(8,128)(2,1)} %get-tuple-element.71.m_ref, ...), custom_call_target="tpu_custom_call" | custom-call | flops 1800000000 | bytes 9000000 | tf_op jit(solution)/shard_map/forward/pallas_call | solution.py:362
  51.2 6.2 %all-to-all-start.1 = ((bf16[16,6,16,384]{3,2,1,0:T(8,128)(2,1)}), bf16[16,6,16,384]{3,2,1,0:T(8,128)(2,1)S(1)}, u32[]{:S(2)}, u32[]{:S(2)}) async-start(bf16[16,6,16,384]{3,2,1,0:T(8,128)(2,1)} %get-tuple-element.104), calls=%async_computation.1 | async-start | bytes 2359296 | tf_op jit(solution)/shard_map/all_to_all | solution.py:586
  57.4 4.5 %columns_apart.1 = (bf16[1,2,3,16,384]{4,3,2,1,0:T(8,128)(2,1)}, bf16[1,2,3,16,384]{4,3,2,1,0:T(8,128)(2,1)}, bf16[1,2,3,16,384]{4,3,2,1,0:T(8,128)(2,1)}, bf16[...) custom-call(s32[5]{0:T(128)S(1)} %stack.68.at_ref, ...), custom_call_target="tpu_custom_call" | custom-call | flops 600000000 | bytes 3000000 | tf_op jit(solution)/shard_map/columns_apart/pallas_call | solution.py:144
  68.8 2.4 %collective-permute-start.5 = (bf16[6,16,384]{2,1,0:T(8,128)(2,1)}, bf16[6,16,384]{2,1,0:T(8,128)(2,1)S(1)}, u32[]{:S(2)}, u32[]{:S(2)}) collective-permute-start(bf16[6,16,384]{2,1,0:T(8,128)(2,1)} %bitcast.88), channel_id=1, source_target_pairs={{0,12},{2,14},{4,8},{6,10},{8,4},{10,6},{12,0},{14,2},{16,28},{18,... | collective-permute-start | bytes 221192 | tf_op jit(solution)/shard_map/ppermute | solution.py:555
  72.8 3.0 %collective-permute-start.7 = (bf16[6,16,384]{2,1,0:T(8,128)(2,1)}, bf16[6,16,384]{2,1,0:T(8,128)(2,1)S(1)}, u32[]{:S(2)}, u32[]{:S(2)}) collective-permute-start(bf16[6,16,384]{2,1,0:T(8,128)(2,1)} %bitcast.86), channel_id=1, source_target_pairs={{0,16},{2,18},{4,20},{6,22},{8,24},{10,26},{12,28},{14,30},{16,0},... | collective-permute-start | bytes 221192 | tf_op jit(solution)/shard_map/ppermute | solution.py:555
  75.9 3.4 %collective-permute-done.3.refs_4_ = bf16[6,16,384]{2,1,0:T(8,128)(2,1)S(1)} collective-permute-done((bf16[6,16,384]{2,1,0:T(8,128)(2,1)}, bf16[6,16,384]{2,1,0:T(8,128)(2,1)S(1)}, u32[]{:S(2)}, u32[]{:S(2)}) %collective-permute-start.3) | collective-permute-done | bytes 73760 | tf_op jit(solution)/shard_map/ppermute | solution.py:555
  79.3 5.6 %collective-permute-start.8 = (bf16[6,16,384]{2,1,0:T(8,128)(2,1)}, bf16[6,16,384]{2,1,0:T(8,128)(2,1)S(1)}, u32[]{:S(2)}, u32[]{:S(2)}) collective-permute-start(bf16[6,16,384]{2,1,0:T(8,128)(2,1)} %bitcast.85), channel_id=1, source_target_pairs={{0,18},{2,16},{4,22},{6,20},{8,26},{10,24},{12,30},{14,28},{16,2},... | collective-permute-start | bytes 221192 | tf_op jit(solution)/shard_map/ppermute | solution.py:555
  84.9 2.5 %collective-permute-start.9 = (bf16[6,16,384]{2,1,0:T(8,128)(2,1)}, bf16[6,16,384]{2,1,0:T(8,128)(2,1)S(1)}, u32[]{:S(2)}, u32[]{:S(2)}) collective-permute-start(bf16[6,16,384]{2,1,0:T(8,128)(2,1)} %bitcast.84), channel_id=1, source_target_pairs={{0,20},{2,22},{4,16},{6,18},{8,28},{10,30},{12,24},{14,26},{16,4},... | collective-permute-start | bytes 221192 | tf_op jit(solution)/shard_map/ppermute | solution.py:555
  89.6 6.5 %collective-permute-done.7.refs_8_ = bf16[6,16,384]{2,1,0:T(8,128)(2,1)S(1)} collective-permute-done((bf16[6,16,384]{2,1,0:T(8,128)(2,1)}, bf16[6,16,384]{2,1,0:T(8,128)(2,1)S(1)}, u32[]{:S(2)}, u32[]{:S(2)}) %collective-permute-start.7) | collective-permute-done | bytes 73760 | tf_op jit(solution)/shard_map/ppermute | solution.py:555
  96.1 3.0 %collective-permute-start.12 = (bf16[6,16,384]{2,1,0:T(8,128)(2,1)}, bf16[6,16,384]{2,1,0:T(8,128)(2,1)S(1)}, u32[]{:S(2)}, u32[]{:S(2)}) collective-permute-start(bf16[6,16,384]{2,1,0:T(8,128)(2,1)} %bitcast.81), channel_id=1, source_target_pairs={{0,26},{2,24},{4,30},{6,28},{8,18},{10,16},{12,22},{14,20},{16,10}... | collective-permute-start | bytes 221192 | tf_op jit(solution)/shard_map/ppermute | solution.py:555
  99.1 2.9 %collective-permute-start.13 = (bf16[6,16,384]{2,1,0:T(8,128)(2,1)}, bf16[6,16,384]{2,1,0:T(8,128)(2,1)S(1)}, u32[]{:S(2)}, u32[]{:S(2)}) collective-permute-start(bf16[6,16,384]{2,1,0:T(8,128)(2,1)} %bitcast.80), channel_id=1, source_target_pairs={{0,28},{2,30},{4,24},{6,26},{8,20},{10,22},{12,16},{14,18},{16,12}... | collective-permute-start | bytes 221192 | tf_op jit(solution)/shard_map/ppermute | solution.py:555
  104.1 2.6 %collective-permute-done.13.refs_14_ = bf16[6,16,384]{2,1,0:T(8,128)(2,1)S(1)} collective-permute-done((bf16[6,16,384]{2,1,0:T(8,128)(2,1)}, bf16[6,16,384]{2,1,0:T(8,128)(2,1)S(1)}, u32[]{:S(2)}, u32[]{:S(2)}) %collective-permute-start.13) | collective-permute-done | bytes 73760 | tf_op jit(solution)/shard_map/ppermute | solution.py:555
  106.7 3.6 %collective-permute-done.14.refs_15_ = bf16[6,16,384]{2,1,0:T(8,128)(2,1)S(1)} collective-permute-done((bf16[6,16,384]{2,1,0:T(8,128)(2,1)}, bf16[6,16,384]{2,1,0:T(8,128)(2,1)S(1)}, u32[]{:S(2)}, u32[]{:S(2)}) %collective-permute-start.14) | collective-permute-done | bytes 73760 | tf_op jit(solution)/shard_map/ppermute | solution.py:555
  110.9 9.1 %backward.1 = (bf16[2,768,384]{2,1,0:T(8,128)(2,1)}, f32[256,384]{1,0:T(8,128)}, f32[256,384]{1,0:T(8,128)}) custom-call(s32[5]{0:T(128)S(1)} %stack.68.at_ref, bf16[768,768]{1,0:T(8,128)(2,1)} %get-tuple-element.68.m_ref, bf16[4,256,256]{2,1,0:T(8,128)(2,1)} %get-tuple-element.69.wi_ref, bf16[4,256,256]{2,1,0:T(8,128)(2,1)} %get-tuple-element.70.wo_ref, ...), custom_call_target="tpu_custom_call" | custom-call | flops 1800000000 | bytes 9000000 | tf_op jit(solution)/shard_map/backward/pallas_call | solution.py:429
  122.8 3.9 %rows_back.1 = (bf16[8,16,384]{2,1,0:T(8,128)(2,1)}, bf16[8,16,384]{2,1,0:T(8,128)(2,1)}, bf16[8,16,384]{2,1,0:T(8,128)(2,1)}, bf16[8,16,384]{2,1,0:T(8,128)(2,1...) custom-call(s32[5]{0:T(128)S(1)} %stack.68.at_ref, ...), custom_call_target="tpu_custom_call" | custom-call | flops 800000000 | bytes 4000000 | tf_op jit(solution)/shard_map/rows_back/pallas_call | solution.py:464
  127.6 2.7 %collective-permute-start.18 = (bf16[8,16,384]{2,1,0:T(8,128)(2,1)}, bf16[8,16,384]{2,1,0:T(8,128)(2,1)S(1)}, u32[]{:S(2)}, u32[]{:S(2)}) collective-permute-start(bf16[8,16,384]{2,1,0:T(8,128)(2,1)} %get-tuple-element.99), channel_id=1, source_target_pairs={{0,6},{2,4},{4,2},{6,0},{8,14},{10,12},{12,10},{14,8},{16,22},{18,... | collective-permute-start | bytes 294920 | tf_op jit(solution)/shard_map/ppermute | solution.py:555
  130.2 2.5 %collective-permute-start.19 = (bf16[8,16,384]{2,1,0:T(8,128)(2,1)}, bf16[8,16,384]{2,1,0:T(8,128)(2,1)S(1)}, u32[]{:S(2)}, u32[]{:S(2)}) collective-permute-start(bf16[8,16,384]{2,1,0:T(8,128)(2,1)} %get-tuple-element.100), channel_id=1, source_target_pairs={{0,8},{2,10},{4,12},{6,14},{8,0},{10,2},{12,4},{14,6},{16,24},{18,... | collective-permute-start | bytes 294920 | tf_op jit(solution)/shard_map/ppermute | solution.py:555
  136.6 2.9 %collective-permute-done.20.refs_10_.refs_11_ = bf16[8,16,384]{2,1,0:T(8,128)(2,1)S(1)} collective-permute-done((bf16[8,16,384]{2,1,0:T(8,128)(2,1)}, bf16[8,16,384]{2,1,0:T(8,128)(2,1)S(1)}, u32[]{:S(2)}, u32[]{:S(2)}) %collective-permute-start.20) | collective-permute-done | bytes 98336 | tf_op jit(solution)/shard_map/ppermute | solution.py:555
  144.0 4.8 %all-to-all-start.2 = ((bf16[16,2,16,384]{3,2,1,0:T(8,128)(2,1)}), bf16[16,2,16,384]{3,2,1,0:T(8,128)(2,1)S(1)}, u32[]{:S(2)}, u32[]{:S(2)}) async-start(bf16[16,2,16,384]{3,2,1,0:T(8,128)(2,1)} %totals.1), calls=%async_computation.2 | async-start | bytes 786432 | tf_op jit(solution)/shard_map/all_to_all | solution.py:586
  148.8 2.9 %collective-permute-start.23 = (bf16[6,16,384]{2,1,0:T(8,128)(2,1)S(1)}, bf16[6,16,384]{2,1,0:T(8,128)(2,1)S(1)}, u32[]{:S(2)}, u32[]{:S(2)}) collective-permute-start(bf16[6,16,384]{2,1,0:T(8,128)(2,1)S(1)} %copy-done.45), channel_id=1, source_target_pairs={{0,16},{2,18},{4,20},{6,22},{8,24},{10,26},{12,28},{14,30},{16,0},... | collective-permute-start | bytes 221192 | tf_op jit(solution)/shard_map/ppermute | solution.py:555
  153.2 3.3 %collective-permute-start.25 = (bf16[6,16,384]{2,1,0:T(8,128)(2,1)S(1)}, bf16[6,16,384]{2,1,0:T(8,128)(2,1)S(1)}, u32[]{:S(2)}, u32[]{:S(2)}) collective-permute-start(bf16[6,16,384]{2,1,0:T(8,128)(2,1)S(1)} %copy-done.43), channel_id=1, source_target_pairs={{0,20},{2,22},{4,16},{6,18},{8,28},{10,30},{12,24},{14,26},{16,4},... | collective-permute-start | bytes 221192 | tf_op jit(solution)/shard_map/ppermute | solution.py:555
  156.5 3.7 %collective-permute-start.27 = (bf16[6,16,384]{2,1,0:T(8,128)(2,1)S(1)}, bf16[6,16,384]{2,1,0:T(8,128)(2,1)S(1)}, u32[]{:S(2)}, u32[]{:S(2)}) collective-permute-start(bf16[6,16,384]{2,1,0:T(8,128)(2,1)S(1)} %copy-done.41), channel_id=1, source_target_pairs={{0,24},{2,26},{4,28},{6,30},{8,16},{10,18},{12,20},{14,22},{16,8},... | collective-permute-start | bytes 221192 | tf_op jit(solution)/shard_map/ppermute | solution.py:555
  160.2 9.8 %collective-permute-done.23 = bf16[6,16,384]{2,1,0:T(8,128)(2,1)S(1)} collective-permute-done((bf16[6,16,384]{2,1,0:T(8,128)(2,1)S(1)}, bf16[6,16,384]{2,1,0:T(8,128)(2,1)S(1)}, u32[]{:S(2)}, u32[]{:S(2)}) %collective-permute-start.23) | collective-permute-done | bytes 73760 | tf_op jit(solution)/shard_map/ppermute | solution.py:555
  173.3 2.2 %collective-permute-start.29 = (bf16[6,16,384]{2,1,0:T(8,128)(2,1)S(1)}, bf16[6,16,384]{2,1,0:T(8,128)(2,1)S(1)}, u32[]{:S(2)}, u32[]{:S(2)}) collective-permute-start(bf16[6,16,384]{2,1,0:T(8,128)(2,1)S(1)} %copy-done.39), channel_id=1, source_target_pairs={{0,28},{2,30},{4,24},{6,26},{8,20},{10,22},{12,16},{14,18},{16,12}... | collective-permute-start | bytes 221192 | tf_op jit(solution)/shard_map/ppermute | solution.py:555
  177.3 3.3 %collective-permute-done.26 = bf16[6,16,384]{2,1,0:T(8,128)(2,1)S(1)} collective-permute-done((bf16[6,16,384]{2,1,0:T(8,128)(2,1)S(1)}, bf16[6,16,384]{2,1,0:T(8,128)(2,1)S(1)}, u32[]{:S(2)}, u32[]{:S(2)}) %collective-permute-start.26) | collective-permute-done | bytes 73760 | tf_op jit(solution)/shard_map/ppermute | solution.py:555
  180.6 3.0 %collective-permute-done.30 = bf16[6,16,384]{2,1,0:T(8,128)(2,1)S(1)} collective-permute-done((bf16[6,16,384]{2,1,0:T(8,128)(2,1)S(1)}, bf16[6,16,384]{2,1,0:T(8,128)(2,1)S(1)}, u32[]{:S(2)}, u32[]{:S(2)}) %collective-permute-start.30) | collective-permute-done | bytes 73760 | tf_op jit(solution)/shard_map/ppermute | solution.py:555
  184.3 5.5 %inverse_apart.1 = bf16[3,180,2,768]{3,2,1,0:T(2,128)(2,1)} custom-call(s32[5]{0:T(128)S(1)} %stack.68.at_ref, bf16[3,180,2,768]{3,2,1,0:T(2,128)(2,1)} %bitcast.57, bf16[360,256]{1,0:T(8,128)(2,1)} %constant.72.clone.t_ref, bf16[1,8,16,384]{3,2,1,0:T(8,128)(2,1)} %bitcast.60, bf16[1,8,16,384]{3,2,1,0:T(8,128)(2,1)} %bitcast.61, ...), custom_call_target="tpu_custom_call" | custom-call | flops 800000000 | bytes 4000000 | tf_op jit(solution)/shard_map/inverse_apart/pallas_call | solution.py:219
  189.9 4.6 %inverse.1 = bf16[3,180,2,768]{3,2,1,0:T(2,128)(2,1)} custom-call(bf16[3,180,2,768]{3,2,1,0:T(2,128)(2,1)} %bitcast.53, bf16[360,256]{1,0:T(8,128)(2,1)} %constant.71.clone.t_ref, bf16[2,1,8,2,3,16,384]{6,5,4,3,2,1,0:T(8,128)(2,1)} %bitcast.55), custom_call_target="tpu_custom_call" | custom-call | flops 800000000 | bytes 4000000 | tf_op jit(solution)/shard_map/inverse/pallas_call | solution.py:190
  (146 shorter events, 36.6 us)
Async XLA Ops:
  4.5 35.4 %all-to-all-start = ((bf16[16,6,16,384]{3,2,1,0:T(8,128)(2,1)}), bf16[16,6,16,384]{3,2,1,0:T(8,128)(2,1)S(1)}, u32[]{:S(2)}, u32[]{:S(2)}) async-start(bf16[16,6,16,384]{3,2,1,0:T(8,128)(2,1)} %bitcast.54), calls=%async_computation | async-start | bytes 2359296 | tf_op jit(solution)/shard_map/all_to_all | solution.py:586
  51.2 90.4 %all-to-all-start.1 = ((bf16[16,6,16,384]{3,2,1,0:T(8,128)(2,1)}), bf16[16,6,16,384]{3,2,1,0:T(8,128)(2,1)S(1)}, u32[]{:S(2)}, u32[]{:S(2)}) async-start(bf16[16,6,16,384]{3,2,1,0:T(8,128)(2,1)} %get-tuple-element.104), calls=%async_computation.1 | async-start | bytes 2359296 | tf_op jit(solution)/shard_map/all_to_all | solution.py:586
  61.9 6.9 %collective-permute-start = (bf16[6,16,384]{2,1,0:T(8,128)(2,1)}, bf16[6,16,384]{2,1,0:T(8,128)(2,1)S(1)}, u32[]{:S(2)}, u32[]{:S(2)}) collective-permute-start(bf16[6,16,384]{2,1,0:T(8,128)(2,1)} %bitcast.93), channel_id=1, source_target_pairs={{0,2},{2,0},{4,6},{6,4},{8,10},{10,8},{12,14},{14,12},{16,18},{18,... | collective-permute-start | bytes 221192 | tf_op jit(solution)/shard_map/ppermute | solution.py:555
  63.9 7.3 %collective-permute-start.1 = (bf16[6,16,384]{2,1,0:T(8,128)(2,1)}, bf16[6,16,384]{2,1,0:T(8,128)(2,1)S(1)}, u32[]{:S(2)}, u32[]{:S(2)}) collective-permute-start(bf16[6,16,384]{2,1,0:T(8,128)(2,1)} %bitcast.92), channel_id=1, source_target_pairs={{0,4},{2,6},{4,0},{6,2},{8,12},{10,14},{12,8},{14,10},{16,20},{18,... | collective-permute-start | bytes 221192 | tf_op jit(solution)/shard_map/ppermute | solution.py:555
  65.4 7.5 %collective-permute-start.2 = (bf16[6,16,384]{2,1,0:T(8,128)(2,1)}, bf16[6,16,384]{2,1,0:T(8,128)(2,1)S(1)}, u32[]{:S(2)}, u32[]{:S(2)}) collective-permute-start(bf16[6,16,384]{2,1,0:T(8,128)(2,1)} %bitcast.91), channel_id=1, source_target_pairs={{0,6},{2,4},{4,2},{6,0},{8,14},{10,12},{12,10},{14,8},{16,22},{18,... | collective-permute-start | bytes 221192 | tf_op jit(solution)/shard_map/ppermute | solution.py:555
  65.5 13.8 %collective-permute-start.3 = (bf16[6,16,384]{2,1,0:T(8,128)(2,1)}, bf16[6,16,384]{2,1,0:T(8,128)(2,1)S(1)}, u32[]{:S(2)}, u32[]{:S(2)}) collective-permute-start(bf16[6,16,384]{2,1,0:T(8,128)(2,1)} %bitcast.90), channel_id=1, source_target_pairs={{0,8},{2,10},{4,12},{6,14},{8,0},{10,2},{12,4},{14,6},{16,24},{18,... | collective-permute-start | bytes 221192 | tf_op jit(solution)/shard_map/ppermute | solution.py:555
  67.4 17.6 %collective-permute-start.4 = (bf16[6,16,384]{2,1,0:T(8,128)(2,1)}, bf16[6,16,384]{2,1,0:T(8,128)(2,1)S(1)}, u32[]{:S(2)}, u32[]{:S(2)}) collective-permute-start(bf16[6,16,384]{2,1,0:T(8,128)(2,1)} %bitcast.89), channel_id=1, source_target_pairs={{0,10},{2,8},{4,14},{6,12},{8,2},{10,0},{12,6},{14,4},{16,26},{18,... | collective-permute-start | bytes 221192 | tf_op jit(solution)/shard_map/ppermute | solution.py:555
  68.8 18.6 %collective-permute-start.5 = (bf16[6,16,384]{2,1,0:T(8,128)(2,1)}, bf16[6,16,384]{2,1,0:T(8,128)(2,1)S(1)}, u32[]{:S(2)}, u32[]{:S(2)}) collective-permute-start(bf16[6,16,384]{2,1,0:T(8,128)(2,1)} %bitcast.88), channel_id=1, source_target_pairs={{0,12},{2,14},{4,8},{6,10},{8,4},{10,6},{12,0},{14,2},{16,28},{18,... | collective-permute-start | bytes 221192 | tf_op jit(solution)/shard_map/ppermute | solution.py:555
  71.2 17.8 %collective-permute-start.6 = (bf16[6,16,384]{2,1,0:T(8,128)(2,1)}, bf16[6,16,384]{2,1,0:T(8,128)(2,1)S(1)}, u32[]{:S(2)}, u32[]{:S(2)}) collective-permute-start(bf16[6,16,384]{2,1,0:T(8,128)(2,1)} %bitcast.87), channel_id=1, source_target_pairs={{0,14},{2,12},{4,10},{6,8},{8,6},{10,4},{12,2},{14,0},{16,30},{18,... | collective-permute-start | bytes 221192 | tf_op jit(solution)/shard_map/ppermute | solution.py:555
  72.8 23.3 %collective-permute-start.7 = (bf16[6,16,384]{2,1,0:T(8,128)(2,1)}, bf16[6,16,384]{2,1,0:T(8,128)(2,1)S(1)}, u32[]{:S(2)}, u32[]{:S(2)}) collective-permute-start(bf16[6,16,384]{2,1,0:T(8,128)(2,1)} %bitcast.86), channel_id=1, source_target_pairs={{0,16},{2,18},{4,20},{6,22},{8,24},{10,26},{12,28},{14,30},{16,0},... | collective-permute-start | bytes 221192 | tf_op jit(solution)/shard_map/ppermute | solution.py:555
  79.3 19.8 %collective-permute-start.8 = (bf16[6,16,384]{2,1,0:T(8,128)(2,1)}, bf16[6,16,384]{2,1,0:T(8,128)(2,1)S(1)}, u32[]{:S(2)}, u32[]{:S(2)}) collective-permute-start(bf16[6,16,384]{2,1,0:T(8,128)(2,1)} %bitcast.85), channel_id=1, source_target_pairs={{0,18},{2,16},{4,22},{6,20},{8,26},{10,24},{12,30},{14,28},{16,2},... | collective-permute-start | bytes 221192 | tf_op jit(solution)/shard_map/ppermute | solution.py:555
  84.9 17.1 %collective-permute-start.9 = (bf16[6,16,384]{2,1,0:T(8,128)(2,1)}, bf16[6,16,384]{2,1,0:T(8,128)(2,1)S(1)}, u32[]{:S(2)}, u32[]{:S(2)}) collective-permute-start(bf16[6,16,384]{2,1,0:T(8,128)(2,1)} %bitcast.84), channel_id=1, source_target_pairs={{0,20},{2,22},{4,16},{6,18},{8,28},{10,30},{12,24},{14,26},{16,4},... | collective-permute-start | bytes 221192 | tf_op jit(solution)/shard_map/ppermute | solution.py:555
  87.5 16.5 %collective-permute-start.10 = (bf16[6,16,384]{2,1,0:T(8,128)(2,1)}, bf16[6,16,384]{2,1,0:T(8,128)(2,1)S(1)}, u32[]{:S(2)}, u32[]{:S(2)}) collective-permute-start(bf16[6,16,384]{2,1,0:T(8,128)(2,1)} %bitcast.83), channel_id=1, source_target_pairs={{0,22},{2,20},{4,18},{6,16},{8,30},{10,28},{12,26},{14,24},{16,6},... | collective-permute-start | bytes 221192 | tf_op jit(solution)/shard_map/ppermute | solution.py:555
  89.0 15.0 %collective-permute-start.11 = (bf16[6,16,384]{2,1,0:T(8,128)(2,1)}, bf16[6,16,384]{2,1,0:T(8,128)(2,1)S(1)}, u32[]{:S(2)}, u32[]{:S(2)}) collective-permute-start(bf16[6,16,384]{2,1,0:T(8,128)(2,1)} %bitcast.82), channel_id=1, source_target_pairs={{0,24},{2,26},{4,28},{6,30},{8,16},{10,18},{12,20},{14,22},{16,8},... | collective-permute-start | bytes 221192 | tf_op jit(solution)/shard_map/ppermute | solution.py:555
  96.1 7.9 %collective-permute-start.12 = (bf16[6,16,384]{2,1,0:T(8,128)(2,1)}, bf16[6,16,384]{2,1,0:T(8,128)(2,1)S(1)}, u32[]{:S(2)}, u32[]{:S(2)}) collective-permute-start(bf16[6,16,384]{2,1,0:T(8,128)(2,1)} %bitcast.81), channel_id=1, source_target_pairs={{0,26},{2,24},{4,30},{6,28},{8,18},{10,16},{12,22},{14,20},{16,10}... | collective-permute-start | bytes 221192 | tf_op jit(solution)/shard_map/ppermute | solution.py:555
  99.1 7.5 %collective-permute-start.13 = (bf16[6,16,384]{2,1,0:T(8,128)(2,1)}, bf16[6,16,384]{2,1,0:T(8,128)(2,1)S(1)}, u32[]{:S(2)}, u32[]{:S(2)}) collective-permute-start(bf16[6,16,384]{2,1,0:T(8,128)(2,1)} %bitcast.80), channel_id=1, source_target_pairs={{0,28},{2,30},{4,24},{6,26},{8,20},{10,22},{12,16},{14,18},{16,12}... | collective-permute-start | bytes 221192 | tf_op jit(solution)/shard_map/ppermute | solution.py:555
  102.1 8.3 %collective-permute-start.14 = (bf16[6,16,384]{2,1,0:T(8,128)(2,1)}, bf16[6,16,384]{2,1,0:T(8,128)(2,1)S(1)}, u32[]{:S(2)}, u32[]{:S(2)}) collective-permute-start(bf16[6,16,384]{2,1,0:T(8,128)(2,1)} %bitcast.79), channel_id=1, source_target_pairs={{0,30},{2,28},{4,26},{6,24},{8,22},{10,20},{12,18},{14,16},{16,14}... | collective-permute-start | bytes 221192 | tf_op jit(solution)/shard_map/ppermute | solution.py:555
  127.3 7.3 %collective-permute-start.17 = (bf16[8,16,384]{2,1,0:T(8,128)(2,1)}, bf16[8,16,384]{2,1,0:T(8,128)(2,1)S(1)}, u32[]{:S(2)}, u32[]{:S(2)}) collective-permute-start(bf16[8,16,384]{2,1,0:T(8,128)(2,1)} %get-tuple-element.98), channel_id=1, source_target_pairs={{0,4},{2,6},{4,0},{6,2},{8,12},{10,14},{12,8},{14,10},{16,20},{18,... | collective-permute-start | bytes 294920 | tf_op jit(solution)/shard_map/ppermute | solution.py:555
  127.6 9.0 %collective-permute-start.18 = (bf16[8,16,384]{2,1,0:T(8,128)(2,1)}, bf16[8,16,384]{2,1,0:T(8,128)(2,1)S(1)}, u32[]{:S(2)}, u32[]{:S(2)}) collective-permute-start(bf16[8,16,384]{2,1,0:T(8,128)(2,1)} %get-tuple-element.99), channel_id=1, source_target_pairs={{0,6},{2,4},{4,2},{6,0},{8,14},{10,12},{12,10},{14,8},{16,22},{18,... | collective-permute-start | bytes 294920 | tf_op jit(solution)/shard_map/ppermute | solution.py:555
  130.2 6.4 %collective-permute-start.19 = (bf16[8,16,384]{2,1,0:T(8,128)(2,1)}, bf16[8,16,384]{2,1,0:T(8,128)(2,1)S(1)}, u32[]{:S(2)}, u32[]{:S(2)}) collective-permute-start(bf16[8,16,384]{2,1,0:T(8,128)(2,1)} %get-tuple-element.100), channel_id=1, source_target_pairs={{0,8},{2,10},{4,12},{6,14},{8,0},{10,2},{12,4},{14,6},{16,24},{18,... | collective-permute-start | bytes 294920 | tf_op jit(solution)/shard_map/ppermute | solution.py:555
  132.7 6.8 %collective-permute-start.20 = (bf16[8,16,384]{2,1,0:T(8,128)(2,1)}, bf16[8,16,384]{2,1,0:T(8,128)(2,1)S(1)}, u32[]{:S(2)}, u32[]{:S(2)}) collective-permute-start(bf16[8,16,384]{2,1,0:T(8,128)(2,1)} %get-tuple-element.101), channel_id=1, source_target_pairs={{0,10},{2,8},{4,14},{6,12},{8,2},{10,0},{12,6},{14,4},{16,26},{18,... | collective-permute-start | bytes 294920 | tf_op jit(solution)/shard_map/ppermute | solution.py:555
  132.7 7.7 %collective-permute-start.21 = (bf16[8,16,384]{2,1,0:T(8,128)(2,1)}, bf16[8,16,384]{2,1,0:T(8,128)(2,1)S(1)}, u32[]{:S(2)}, u32[]{:S(2)}) collective-permute-start(bf16[8,16,384]{2,1,0:T(8,128)(2,1)} %get-tuple-element.102), channel_id=1, source_target_pairs={{0,12},{2,14},{4,8},{6,10},{8,4},{10,6},{12,0},{14,2},{16,28},{18,... | collective-permute-start | bytes 294920 | tf_op jit(solution)/shard_map/ppermute | solution.py:555
  134.6 7.0 %collective-permute-start.22 = (bf16[8,16,384]{2,1,0:T(8,128)(2,1)}, bf16[8,16,384]{2,1,0:T(8,128)(2,1)S(1)}, u32[]{:S(2)}, u32[]{:S(2)}) collective-permute-start(bf16[8,16,384]{2,1,0:T(8,128)(2,1)} %get-tuple-element.103), channel_id=1, source_target_pairs={{0,14},{2,12},{4,10},{6,8},{8,6},{10,4},{12,2},{14,0},{16,30},{18,... | collective-permute-start | bytes 294920 | tf_op jit(solution)/shard_map/ppermute | solution.py:555
  144.0 45.8 %all-to-all-start.2 = ((bf16[16,2,16,384]{3,2,1,0:T(8,128)(2,1)}), bf16[16,2,16,384]{3,2,1,0:T(8,128)(2,1)S(1)}, u32[]{:S(2)}, u32[]{:S(2)}) async-start(bf16[16,2,16,384]{3,2,1,0:T(8,128)(2,1)} %totals.1), calls=%async_computation.2 | async-start | bytes 786432 | tf_op jit(solution)/shard_map/all_to_all | solution.py:586
  148.8 21.2 %collective-permute-start.23 = (bf16[6,16,384]{2,1,0:T(8,128)(2,1)S(1)}, bf16[6,16,384]{2,1,0:T(8,128)(2,1)S(1)}, u32[]{:S(2)}, u32[]{:S(2)}) collective-permute-start(bf16[6,16,384]{2,1,0:T(8,128)(2,1)S(1)} %copy-done.45), channel_id=1, source_target_pairs={{0,16},{2,18},{4,20},{6,22},{8,24},{10,26},{12,28},{14,30},{16,0},... | collective-permute-start | bytes 221192 | tf_op jit(solution)/shard_map/ppermute | solution.py:555
  151.7 21.6 %collective-permute-start.24 = (bf16[6,16,384]{2,1,0:T(8,128)(2,1)S(1)}, bf16[6,16,384]{2,1,0:T(8,128)(2,1)S(1)}, u32[]{:S(2)}, u32[]{:S(2)}) collective-permute-start(bf16[6,16,384]{2,1,0:T(8,128)(2,1)S(1)} %copy-done.44), channel_id=1, source_target_pairs={{0,18},{2,16},{4,22},{6,20},{8,26},{10,24},{12,30},{14,28},{16,2},... | collective-permute-start | bytes 221192 | tf_op jit(solution)/shard_map/ppermute | solution.py:555
  153.2 22.4 %collective-permute-start.25 = (bf16[6,16,384]{2,1,0:T(8,128)(2,1)S(1)}, bf16[6,16,384]{2,1,0:T(8,128)(2,1)S(1)}, u32[]{:S(2)}, u32[]{:S(2)}) collective-permute-start(bf16[6,16,384]{2,1,0:T(8,128)(2,1)S(1)} %copy-done.43), channel_id=1, source_target_pairs={{0,20},{2,22},{4,16},{6,18},{8,28},{10,30},{12,24},{14,26},{16,4},... | collective-permute-start | bytes 221192 | tf_op jit(solution)/shard_map/ppermute | solution.py:555
  156.4 24.1 %collective-permute-start.26 = (bf16[6,16,384]{2,1,0:T(8,128)(2,1)S(1)}, bf16[6,16,384]{2,1,0:T(8,128)(2,1)S(1)}, u32[]{:S(2)}, u32[]{:S(2)}) collective-permute-start(bf16[6,16,384]{2,1,0:T(8,128)(2,1)S(1)} %copy-done.42), channel_id=1, source_target_pairs={{0,22},{2,20},{4,18},{6,16},{8,30},{10,28},{12,26},{14,24},{16,6},... | collective-permute-start | bytes 221192 | tf_op jit(solution)/shard_map/ppermute | solution.py:555
  156.5 24.0 %collective-permute-start.27 = (bf16[6,16,384]{2,1,0:T(8,128)(2,1)S(1)}, bf16[6,16,384]{2,1,0:T(8,128)(2,1)S(1)}, u32[]{:S(2)}, u32[]{:S(2)}) collective-permute-start(bf16[6,16,384]{2,1,0:T(8,128)(2,1)S(1)} %copy-done.41), channel_id=1, source_target_pairs={{0,24},{2,26},{4,28},{6,30},{8,16},{10,18},{12,20},{14,22},{16,8},... | collective-permute-start | bytes 221192 | tf_op jit(solution)/shard_map/ppermute | solution.py:555
  170.0 10.5 %collective-permute-start.28 = (bf16[6,16,384]{2,1,0:T(8,128)(2,1)S(1)}, bf16[6,16,384]{2,1,0:T(8,128)(2,1)S(1)}, u32[]{:S(2)}, u32[]{:S(2)}) collective-permute-start(bf16[6,16,384]{2,1,0:T(8,128)(2,1)S(1)} %copy-done.40), channel_id=1, source_target_pairs={{0,26},{2,24},{4,30},{6,28},{8,18},{10,16},{12,22},{14,20},{16,10}... | collective-permute-start | bytes 221192 | tf_op jit(solution)/shard_map/ppermute | solution.py:555
  173.3 7.3 %collective-permute-start.29 = (bf16[6,16,384]{2,1,0:T(8,128)(2,1)S(1)}, bf16[6,16,384]{2,1,0:T(8,128)(2,1)S(1)}, u32[]{:S(2)}, u32[]{:S(2)}) collective-permute-start(bf16[6,16,384]{2,1,0:T(8,128)(2,1)S(1)} %copy-done.39), channel_id=1, source_target_pairs={{0,28},{2,30},{4,24},{6,26},{8,20},{10,22},{12,16},{14,18},{16,12}... | collective-permute-start | bytes 221192 | tf_op jit(solution)/shard_map/ppermute | solution.py:555
  175.5 8.1 %collective-permute-start.30 = (bf16[6,16,384]{2,1,0:T(8,128)(2,1)S(1)}, bf16[6,16,384]{2,1,0:T(8,128)(2,1)S(1)}, u32[]{:S(2)}, u32[]{:S(2)}) collective-permute-start(bf16[6,16,384]{2,1,0:T(8,128)(2,1)S(1)} %copy-done.38), channel_id=1, source_target_pairs={{0,30},{2,28},{4,26},{6,24},{8,22},{10,20},{12,18},{14,16},{16,14}... | collective-permute-start | bytes 221192 | tf_op jit(solution)/shard_map/ppermute | solution.py:555
  (49 other events, 559.2 us)
